TPU v7x, 32 devices: a whole 2x2x4 slice. The times are simulated.
32 devices in a mesh: dp: 8 (over z, y), tensor: 4 (over x, core).
Axes of the slice: x: 2, y: 2, z: 4, core: 2. Of those that a mesh axis runs over, the one named last changes fastest.
Arguments:
- inputs: bfloat16 [26656, 768], P('dp'), may hold values from -6 to 6
- cotangent: bfloat16 [26656, 768], P('dp'), may hold values from -6 to 6
- master_inward: float32 [3, 768, 768], P(None, 'dp', 'tensor'), may hold values from -0.28867513 to 0.28867513
- first_inward: float32 [3, 768, 768], P(None, 'dp', 'tensor'), may hold values from -512 to 512
- second_inward: float32 [3, 768, 768], P(None, 'dp', 'tensor'), may hold values from 3332 to 53312
- master_outward: float32 [768, 768], P('tensor', 'dp'), may hold values from -0.8164966 to 0.8164966
- first_outward: float32 [768, 768], P('tensor', 'dp'), may hold values from -320 to 320
- second_outward: float32 [768, 768], P('tensor', 'dp'), may hold values from 1332.8 to 21324.8
- master_widening: float32 [768, 3072], P('dp', 'tensor'), may hold values from -0.28867513 to 0.28867513
- first_widening: float32 [768, 3072], P('dp', 'tensor'), may hold values from -320 to 320
- second_widening: float32 [768, 3072], P('dp', 'tensor'), may hold values from 1332.8 to 21324.8
- master_narrowing: float32 [3072, 768], P('tensor', 'dp'), may hold values from -0.14433757 to 0.14433757
- first_narrowing: float32 [3072, 768], P('tensor', 'dp'), may hold values from -640 to 640
- second_narrowing: float32 [3072, 768], P('tensor', 'dp'), may hold values from 5331.2 to 85299.2
- master_scaling: float32 [768], P('dp'), may hold values from 0.5 to 1.5
- first_scaling: float32 [768], P('dp'), may hold values from -1024 to 1024
- second_scaling: float32 [768], P('dp'), may hold values from 13328 to 213248
Outputs:
- output: bfloat16 [26656, 768], P(('dp', 'tensor'))
- input_grad: bfloat16 [26656, 768], P('dp')
- moment_inward: float32 [3, 768, 768], P(None, 'dp', 'tensor')
- square_inward: float32 [3, 768, 768], P(None, 'dp', 'tensor')
- weight_inward: float32 [3, 768, 768], P(None, 'dp', 'tensor')
- bfloat_inward: bfloat16 [3, 768, 768], P(None, 'dp', 'tensor')
- moment_outward: float32 [768, 768], P('tensor', 'dp')
- square_outward: float32 [768, 768], P('tensor', 'dp')
- weight_outward: float32 [768, 768], P('tensor', 'dp')
- bfloat_outward: bfloat16 [768, 768], P('tensor', 'dp')
- moment_widening: float32 [768, 3072], P('dp', 'tensor')
- square_widening: float32 [768, 3072], P('dp', 'tensor')
- weight_widening: float32 [768, 3072], P('dp', 'tensor')
- bfloat_widening: bfloat16 [768, 3072], P('dp', 'tensor')
- moment_narrowing: float32 [3072, 768], P('tensor', 'dp')
- square_narrowing: float32 [3072, 768], P('tensor', 'dp')
- weight_narrowing: float32 [3072, 768], P('tensor', 'dp')
- bfloat_narrowing: bfloat16 [3072, 768], P('tensor', 'dp')
- moment_scaling: float32 [768], P('dp')
- square_scaling: float32 [768], P('dp')
- weight_scaling: float32 [768], P('dp')
- bfloat_scaling: bfloat16 [768], P('dp')
- trust_norms: float32 [5, 2], replicated
All inputs are finite; a program needn't handle non-finite values.
Results may differ from a plain program's by a relative error of at most 0.012.
The roundings to bfloat16 on the way count: a program that leaves them out, or rounds other values in their place, can miss the bound.
Values may be sent and summed in bfloat16 or wider, within the bound.
A program may use at most 192 MiB of HBM per device.

v0:
```python
import jax
import jax.numpy as jnp
from jax import lax
from jax.sharding import PartitionSpec as P

HEAD_DIM = 64
SEQ = 196
STEP = 5


norm_eps = 1e-06
beta_one = 0.5
beta_two = 0.5
lamb_eps = 1e-06
weight_decay = 0.01
learn_rate = 0.5


def lamb_parts(master, first, second, grad):
    moment = beta_one * first + (1.0 - beta_one) * grad
    square = beta_two * second + (1.0 - beta_two) * grad * grad
    update = (
        moment / (1.0 - beta_one**STEP) / (jnp.sqrt(square / (1.0 - beta_two**STEP)) + lamb_eps)
        + weight_decay * master
    )
    return (moment, square, update)


def gelu_tanh(values):
    return jax.nn.gelu(values, approximate=True)


def local(
    inputs,
    cotangent,
    master_inward,
    first_inward,
    second_inward,
    master_outward,
    first_outward,
    second_outward,
    master_widening,
    first_widening,
    second_widening,
    master_narrowing,
    first_narrowing,
    second_narrowing,
    master_scaling,
    first_scaling,
    second_scaling,
):
    inward, outward, widening, narrowing, scaling = (
        lax.all_gather(master_inward.astype(jnp.bfloat16), "dp", axis=1, tiled=True),
        lax.all_gather(master_outward.astype(jnp.bfloat16), "dp", axis=1, tiled=True),
        lax.all_gather(master_widening.astype(jnp.bfloat16), "dp", axis=0, tiled=True),
        lax.all_gather(master_narrowing.astype(jnp.bfloat16), "dp", axis=1, tiled=True),
        lax.all_gather(master_scaling.astype(jnp.bfloat16), "dp", axis=0, tiled=True),
    )
    floats_in = inputs.astype(jnp.float32)
    rows_here = floats_in.shape[0]
    images = rows_here // SEQ
    heads_here = inward.shape[2] // HEAD_DIM
    factor = HEAD_DIM ** (-0.5)
    centred = floats_in - jnp.mean(floats_in, axis=1, keepdims=True)
    inv_std = lax.rsqrt(jnp.mean(centred * centred, axis=1, keepdims=True) + norm_eps)
    unit_rows = centred * inv_std
    gain_rows = scaling.astype(jnp.float32)
    normed = (unit_rows * gain_rows).astype(jnp.bfloat16)
    projected = jnp.einsum(
        "rd,tde->tre", normed, inward, preferred_element_type=jnp.float32
    ).astype(jnp.bfloat16)
    blocks = projected.reshape(3, images, SEQ, heads_here, HEAD_DIM)
    query_rows, key_rows, value_rows = (blocks[0], blocks[1], blocks[2])
    scores = (
        jnp.einsum("bqhd,bkhd->bhqk", query_rows, key_rows, preferred_element_type=jnp.float32)
        * factor
    )
    peak = jnp.max(scores, axis=-1, keepdims=True)
    log_total = peak + jnp.log(jnp.sum(jnp.exp(scores - peak), axis=-1, keepdims=True))
    probs_low = jnp.exp(scores - log_total).astype(jnp.bfloat16)
    attended = jnp.einsum(
        "bhqk,bkhd->bqhd", probs_low, value_rows, preferred_element_type=jnp.float32
    )
    attended = attended.astype(jnp.bfloat16).reshape(rows_here, heads_here * HEAD_DIM)
    upper = jnp.dot(normed, widening, preferred_element_type=jnp.float32)
    hidden = gelu_tanh(upper).astype(jnp.bfloat16)
    partial_sum = jnp.dot(attended, outward, preferred_element_type=jnp.float32) + jnp.dot(
        hidden, narrowing, preferred_element_type=jnp.float32
    )
    share = rows_here // lax.axis_size("tensor")
    start = lax.axis_index("tensor") * share
    total = lax.psum(partial_sum.astype(jnp.bfloat16), "tensor").astype(jnp.float32)
    mixed = lax.dynamic_slice_in_dim(floats_in, start, share, 0) + lax.dynamic_slice_in_dim(
        total, start, share, 0
    )
    output = mixed.astype(jnp.bfloat16)
    d_attended = jnp.einsum(
        "rd,ed->re", cotangent, outward, preferred_element_type=jnp.float32
    ).astype(jnp.bfloat16)
    grad_outward = jnp.einsum("re,rd->ed", attended, cotangent, preferred_element_type=jnp.float32)
    d_hidden = jnp.einsum("rd,fd->rf", cotangent, narrowing, preferred_element_type=jnp.float32)
    grad_narrowing = jnp.einsum("rf,rd->fd", hidden, cotangent, preferred_element_type=jnp.float32)
    gelu_value, gelu_pull = jax.vjp(gelu_tanh, upper)
    d_upper = gelu_pull(d_hidden)[0].astype(jnp.bfloat16)
    grad_widening = jnp.einsum("rd,rf->df", normed, d_upper, preferred_element_type=jnp.float32)
    back_sum = jnp.einsum("rf,df->rd", d_upper, widening, preferred_element_type=jnp.float32)
    d_att_blocks = d_attended.reshape(images, SEQ, heads_here, HEAD_DIM)
    rescored = (
        jnp.einsum("bqhd,bkhd->bhqk", query_rows, key_rows, preferred_element_type=jnp.float32)
        * factor
    )
    probs_full = jnp.exp(rescored - log_total)
    probs_again = probs_full.astype(jnp.bfloat16)
    d_probs = jnp.einsum(
        "bqhd,bkhd->bhqk", d_att_blocks, value_rows, preferred_element_type=jnp.float32
    )
    d_value = jnp.einsum(
        "bhqk,bqhd->bkhd", probs_again, d_att_blocks, preferred_element_type=jnp.float32
    ).astype(jnp.bfloat16)
    inner = jnp.sum(probs_full * d_probs, axis=-1, keepdims=True)
    d_scores = (probs_full * (d_probs - inner)).astype(jnp.bfloat16)
    d_query = (
        jnp.einsum("bhqk,bkhd->bqhd", d_scores, key_rows, preferred_element_type=jnp.float32)
        * factor
    ).astype(jnp.bfloat16)
    d_key = (
        jnp.einsum("bhqk,bqhd->bkhd", d_scores, query_rows, preferred_element_type=jnp.float32)
        * factor
    ).astype(jnp.bfloat16)
    d_projected = jnp.stack([d_query, d_key, d_value]).reshape(3, rows_here, heads_here * HEAD_DIM)
    grad_inward = jnp.einsum("rd,tre->tde", normed, d_projected, preferred_element_type=jnp.float32)
    back_sum = back_sum + jnp.einsum(
        "tre,tde->rd", d_projected, inward, preferred_element_type=jnp.float32
    )
    d_normed = lax.psum(back_sum.astype(jnp.bfloat16), "tensor").astype(jnp.float32)
    grad_scaling = jnp.sum(d_normed * unit_rows, axis=0)
    d_unit = d_normed * gain_rows
    d_floats = inv_std * (
        d_unit
        - jnp.mean(d_unit, axis=1, keepdims=True)
        - unit_rows * jnp.mean(d_unit * unit_rows, axis=1, keepdims=True)
    )
    input_grad = (cotangent.astype(jnp.float32) + d_floats).astype(jnp.bfloat16)
    grad_inward, grad_outward, grad_widening, grad_narrowing, grad_scaling = (
        lax.psum_scatter(grad_inward, "dp", scatter_dimension=1, tiled=True),
        lax.psum_scatter(grad_outward, "dp", scatter_dimension=1, tiled=True),
        lax.psum_scatter(grad_widening, "dp", scatter_dimension=0, tiled=True),
        lax.psum_scatter(grad_narrowing, "dp", scatter_dimension=1, tiled=True),
        lax.psum_scatter(grad_scaling, "dp", scatter_dimension=0, tiled=True),
    )
    part_in = lamb_parts(master_inward, first_inward, second_inward, grad_inward)
    part_out = lamb_parts(master_outward, first_outward, second_outward, grad_outward)
    part_wide = lamb_parts(master_widening, first_widening, second_widening, grad_widening)
    part_narrow = lamb_parts(master_narrowing, first_narrowing, second_narrowing, grad_narrowing)
    part_scale = lamb_parts(master_scaling, first_scaling, second_scaling, grad_scaling)
    replicas = 1.0 / lax.axis_size("tensor")
    local_sums = jnp.stack(
        [
            jnp.stack([jnp.sum(master_inward * master_inward), jnp.sum(part_in[2] * part_in[2])]),
            jnp.stack(
                [jnp.sum(master_outward * master_outward), jnp.sum(part_out[2] * part_out[2])]
            ),
            jnp.stack(
                [jnp.sum(master_widening * master_widening), jnp.sum(part_wide[2] * part_wide[2])]
            ),
            jnp.stack(
                [
                    jnp.sum(master_narrowing * master_narrowing),
                    jnp.sum(part_narrow[2] * part_narrow[2]),
                ]
            ),
            jnp.stack(
                [jnp.sum(master_scaling * master_scaling), jnp.sum(part_scale[2] * part_scale[2])]
            )
            * replicas,
        ]
    )
    trust_norms = jnp.sqrt(lax.psum(local_sums, ("dp", "tensor")))
    fresh_in = master_inward - learn_rate * (trust_norms[0, 0] / trust_norms[0, 1]) * part_in[2]
    fresh_out = master_outward - learn_rate * (trust_norms[1, 0] / trust_norms[1, 1]) * part_out[2]
    fresh_wide = (
        master_widening - learn_rate * (trust_norms[2, 0] / trust_norms[2, 1]) * part_wide[2]
    )
    fresh_narrow = (
        master_narrowing - learn_rate * (trust_norms[3, 0] / trust_norms[3, 1]) * part_narrow[2]
    )
    fresh_scale = (
        master_scaling - learn_rate * (trust_norms[4, 0] / trust_norms[4, 1]) * part_scale[2]
    )
    return (
        output,
        input_grad,
        part_in[0],
        part_in[1],
        fresh_in,
        fresh_in.astype(jnp.bfloat16),
        part_out[0],
        part_out[1],
        fresh_out,
        fresh_out.astype(jnp.bfloat16),
        part_wide[0],
        part_wide[1],
        fresh_wide,
        fresh_wide.astype(jnp.bfloat16),
        part_narrow[0],
        part_narrow[1],
        fresh_narrow,
        fresh_narrow.astype(jnp.bfloat16),
        part_scale[0],
        part_scale[1],
        fresh_scale,
        fresh_scale.astype(jnp.bfloat16),
        trust_norms,
    )


def solution(mesh):
    in_specs = (
        P("dp", None),
        P("dp", None),
        P(None, "dp", "tensor"),
        P(None, "dp", "tensor"),
        P(None, "dp", "tensor"),
        P("tensor", "dp"),
        P("tensor", "dp"),
        P("tensor", "dp"),
        P("dp", "tensor"),
        P("dp", "tensor"),
        P("dp", "tensor"),
        P("tensor", "dp"),
        P("tensor", "dp"),
        P("tensor", "dp"),
        P("dp"),
        P("dp"),
        P("dp"),
    )
    out_specs = (
        P(("dp", "tensor"), None),
        P("dp", None),
        P(None, "dp", "tensor"),
        P(None, "dp", "tensor"),
        P(None, "dp", "tensor"),
        P(None, "dp", "tensor"),
        P("tensor", "dp"),
        P("tensor", "dp"),
        P("tensor", "dp"),
        P("tensor", "dp"),
        P("dp", "tensor"),
        P("dp", "tensor"),
        P("dp", "tensor"),
        P("dp", "tensor"),
        P("tensor", "dp"),
        P("tensor", "dp"),
        P("tensor", "dp"),
        P("tensor", "dp"),
        P("dp"),
        P("dp"),
        P("dp"),
        P("dp"),
        P(),
    )
    return jax.shard_map(local, mesh=mesh, in_specs=in_specs, out_specs=out_specs, check_vma=False)
```

profile of v0, /device:TPU:0, one launch (start us, length us, event | category | flops | bytes accessed | tf_op | source)
XLA Modules:
  0.0 706.7 jit_solution(8922916075300123028)
XLA Ops:
  9.0 3.2 convert_reduce_fusion
  14.3 23.4 %all-reduce = bf16[768]{0:T(1024)(128)(2,1)S(1)} all-reduce(bf16[768]{0:T(1024)(128)(2,1)S(1)} %dynamic-update-slice), channel_id=1, replica_groups=mesh['dp'=8,'tensor'=4] {'dp'}, use_global_device_ids=true, to_apply=%add | all-reduce | flops 768 | bytes 3072
  37.7 4.2 multiply_reduce_fusion.1
  42.6 6.7 multiply_convert_fusion.2
  49.3 5.3 all-gather.3.cloned.1.call-done
  54.6 6.5 fusion.62
  61.2 3.9 copy-done.47
  65.1 9.5 %fusion.46 = f32[768,768]{0,1:T(8,128)} fusion(bf16[3332,768]{1,0:T(8,128)(2,1)} %param.18, f32[3332,768]{1,0:T(8,128)S(1)} %fusion.62), kind=kOutput, calls=%fused_computation.109 | convolution fusion | flops 3953617920 | bytes 17713152 | tf_op jit(solution)/shard_map/rf,rd->fd/dot_general | solution.py:102
  75.5 41.9 %all_gather.16 = bf16[3,768,192]{2,0,1:T(4,128)(2,1)S(1)} all-gather(bf16[3,96,192]{2,0,1:T(4,128)(2,1)S(1)} %copy.122), channel_id=1, replica_groups=mesh['dp'=8,'tensor'=4] {'dp'}, dimensions={1}, use_global_device_ids=true | all-gather | bytes 995328 | tf_op jit(solution)/shard_map/all_gather | solution.py:53
  118.3 5.8 fusion.61
  125.9 3.8 squeeze.7
  129.7 3.8 squeeze.8
  133.5 4.2 squeeze.6
  137.7 9.7 %multiply_reduce_fusion.2 = (f32[17,3,196]{2,1,0:T(4,128)S(1)}, f32[17,3,196,196]{2,3,1,0:T(8,128)}) fusion(bf16[17,196,3,64]{1,0,3,2:T(8,128)(2,1)} %squeeze.8, bf16[17,196,3,64]{1,0,3,2:T(8,128)(2,1)} %squeeze.7), kind=kOutput, calls=%fused_computation.31 | convolution fusion | flops 254688080 | bytes 10435824 | tf_op jit(solution)/shard_map/bqhd,bkhd->bhqk/dot_general | solution.py:75
  147.4 7.8 %reduce-scatter.11.cloned.1.call-done = f32[768,96]{0,1:T(8,128)} async-done(((f32[768,768]{0,1:T(8,128)}), f32[768,96]{0,1:T(8,128)}) %reduce-scatter.11.cloned.1.call-update) | async-done | bytes 294928 | tf_op jit(solution)/shard_map/reduce_scatter | solution.py:148
  155.3 2.6 multiply_reduce_fusion.4
  158.4 6.3 exponential_reduce_fusion
  168.6 2.6 reshape.143
  171.2 6.0 convolution_bitcast_fusion
  177.3 31.7 %all_gather.17 = bf16[192,768]{0,1:T(8,128)(2,1)S(1)} all-gather(bf16[192,96]{0,1:T(8,128)(2,1)S(1)} %copy.129), channel_id=1, replica_groups=mesh['dp'=8,'tensor'=4] {'dp'}, dimensions={1}, use_global_device_ids=true | all-gather | bytes 331776 | tf_op jit(solution)/shard_map/all_gather | solution.py:54
  209.8 4.2 convolution_convert_fusion
  214.0 4.0 reshape.144
  218.0 12.7 %multiply_reduce_fusion = (f32[17,3,196]{2,1,0:T(4,128)S(1)}, f32[17,3,196,196]{2,3,1,0:T(8,128)}) fusion(f32[17,3,196,196]{2,3,1,0:T(8,128)} %get-tuple-element.170, f32[17,3,196]{2,1,0:T(4,128)S(1)} %log_add_fusion, bf16[17,196,3,64]{1,0,3,2:T(8,128)(2,1)} %copy-done.1, bf16[17,196,3,64]{1,0,3,2:T(8,128)(2,1)} %reshape.144), kind=kOutput, calls=%fused_computation.8 | convolution fusion | flops 258606512 | bytes 18312672 | tf_op jit(solution)/shard_map/bqhd,bkhd->bhqk/dot_general | solution.py:114
  230.8 5.9 multiply_convert_fusion
  240.7 3.3 fusion.24
  245.0 2.6 stack.74
  250.1 3.0 stack.73
  258.1 2.6 stack.75
  260.7 2.5 constant_dynamic-update-slice_fusion.1
  263.2 2.5 constant_dynamic-update-slice_fusion
  265.7 8.2 %fusion.20 = f32[3,768,192]{1,2,0:T(8,128)} fusion(bf16[3,3332,192]{1,2,0:T(8,128)(2,1)} %constant_dynamic-update-slice_fusion, bf16[3332,768]{1,0:T(8,128)(2,1)} %multiply_convert_fusion.2), kind=kOutput, calls=%fused_computation.43 | convolution fusion | flops 2947940352 | bytes 10725888 | tf_op jit(solution)/shard_map/rd,tre->tde/dot_general | solution.py:131
  273.9 2.9 copy.158
  276.9 2.8 reshape.154
  279.8 12.9 %fusion.15 = bf16[3332,768]{1,0:T(8,128)(2,1)S(1)} fusion(f32[3332,768]{1,0:T(8,128)} %copy-done.47, bf16[3332,768]{1,0:T(8,128)(2,1)} %param.18, bf16[768,768]{0,1:T(8,128)(2,1)} %all-gather.5.cloned.1.call-done), kind=kOutput, calls=%fused_computation.23 | convolution fusion | flops 3981766656 | bytes 21651456 | tf_op jit(solution)/shard_map/rd,fd->rf/dot_general | solution.py:101
  295.0 8.6 %fusion.64 = f32[768,768]{1,0:T(8,128)} fusion(bf16[3332,768]{1,0:T(8,128)(2,1)} %multiply_convert_fusion.2, bf16[3332,768]{1,0:T(8,128)(2,1)S(1)} %fusion.15), kind=kOutput, calls=%fused_computation.122 | convolution fusion | flops 3930587136 | bytes 12595200 | tf_op jit(solution)/shard_map/rd,rf->df/dot_general | solution.py:105
  303.7 9.2 %fusion.47 = f32[3332,768]{1,0:T(8,128)S(1)} fusion(bf16[768,768]{0,1:T(8,128)(2,1)S(1)} %copy-done.44, f32[3332,768]{1,0:T(8,128)} %copy-done.47), kind=kOutput, calls=%fused_computation.110 | convolution fusion | flops 3953617920 | bytes 21651456 | tf_op jit(solution)/shard_map/dot_general | solution.py:87
  313.0 4.0 add_convert_fusion
  317.0 4.4 fusion.63
  321.4 6.6 fusion.16
  329.2 7.2 %convert_element_type.106 = f32[3332,768]{1,0:T(8,128)} convert(bf16[3332,768]{1,0:T(8,128)(2,1)} %param.17) | non-fusion elementwise | flops 2558976 | bytes 15353856 | tf_op jit(solution)/shard_map/convert_element_type | solution.py:59
  340.7 5.5 reduce-scatter.13.cloned.1.call-done
  352.1 66.1 %reduce-scatter.9.cloned.1.call-done = f32[96,768]{1,0:T(8,128)} async-done(((f32[768,768]{1,0:T(8,128)}), f32[96,768]{1,0:T(8,128)}) %reduce-scatter.9.cloned.1.call-update) | async-done | bytes 294928 | tf_op jit(solution)/shard_map/reduce_scatter | solution.py:147
  421.5 182.5 %all-reduce.5.cloned.1.call-done = (bf16[3332,768]{1,0:T(8,128)(2,1)}, bf16[3332,768]{1,0:T(8,128)(2,1)}) async-done(((bf16[3332,768]{1,0:T(8,128)(2,1)}, bf16[3332,768]{1,0:T(8,128)(2,1)}), (bf16[3332,768]{1,0:T(8,128)(2,1)}, bf16[3332,768]{1,0:T(8,128)(2,1)})) %all-reduce.5.cloned.1.call-update) | async-done | bytes 10235920 | tf_op jit(solution)/shard_map/psum | solution.py:92
  604.1 7.5 %fusion.8 = (f32[768]{0:T(1024)S(1)}, f32[3332]{0:T(1024)S(1)}, f32[3332]{0:T(1024)S(1)}) fusion(bf16[3332,768]{1,0:T(8,128)(2,1)} %get-tuple-element.125, bf16[3332,768]{1,0:T(8,128)(2,1)} %param.17, f32[3332]{0:T(1024)S(1)} %copy-done.32, f32[3332]{0:T(1024)S(1)} %copy-done.22, f32[768]{0:T(1024)S(1)} %copy-done.36), kind=kLoop, calls=%fused_computation.16 | loop fusion | flops 25582328 | bytes 10295360 | tf_op jit(solution)/shard_map/reduce_sum | solution.py:136
  611.6 21.4 %all-reduce.1 = f32[768]{0:T(1024)S(1)} all-reduce(f32[768]{0:T(1024)S(1)} %get-tuple-element.115), channel_id=6, replica_groups=mesh['dp'=8,'tensor'=4] {'dp'}, use_global_device_ids=true, to_apply=%region_23.0.clone | all-reduce | flops 768 | bytes 6144
  636.5 36.8 %psum.23 = f32[5,2]{0,1:T(2,128)S(1)} all-reduce(f32[5,2]{0,1:T(2,128)S(1)} %stack.96), channel_id=1, replica_groups=mesh['dp'=8,'tensor'=4] {'dp','tensor'}, use_global_device_ids=true, to_apply=%region_25.0 | all-reduce | flops 10 | bytes 80 | tf_op jit(solution)/shard_map/psum | solution.py:178
  683.0 10.4 %fusion.6 = bf16[3332,768]{1,0:T(8,128)(2,1)} fusion(bf16[3332,768]{1,0:T(8,128)(2,1)} %get-tuple-element.125, bf16[3332,768]{1,0:T(8,128)(2,1)} %param.18, bf16[3332,768]{1,0:T(8,128)(2,1)} %param.17, f32[3332]{0:T(1024)S(1)} %get-tuple-element.173, f32[3332]{0:T(1024)S(1)} %get-tuple-element.174, f32[768]{0:T(1024)S(1)} %copy-done.36, ...), kind=kLoop, calls=%fused_computation.14 | loop fusion | flops 30707712 | bytes 20528192 | tf_op jit(solution)/shard_map/convert_element_type | solution.py:143
  696.0 3.7 add_convert_fusion.1
  (173 shorter events, 50.2 us)
Async XLA Ops:
  7.2 5.6 copy-start.40
  7.2 5.0 copy-start.38
  7.2 47.4 %all-gather.3.cloned.1.call-start = ((), (), s32[]{:S(2)}) async-start(), calls=%async_computation.4 | async-start | bytes 1327104 | tf_op jit(solution)/shard_map/all_gather | solution.py:55
  8.9 146.3 %reduce-scatter.11.cloned.1.call-start = ((), (), s32[]{:S(2)}) async-start(), calls=%async_computation.7 | async-start | bytes 2654208 | tf_op jit(solution)/shard_map/reduce_scatter | solution.py:148
  37.7 4.3 copy-start.35
  65.1 9.6 %copy-start.9 = (f32[3,96,192]{2,1,0:T(8,128)S(1)}, f32[3,96,192]{2,1,0:T(8,128)}, u32[]{:S(2)}) copy-start(f32[3,96,192]{2,1,0:T(8,128)} %param.19) | copy-start | bytes 663556
  74.6 205.2 %all-gather.5.cloned.1.call-start = ((), (), s32[]{:S(2)}) async-start(), calls=%async_computation.5 | async-start | bytes 1327104 | tf_op jit(solution)/shard_map/all_gather | solution.py:56
  118.3 5.9 copy-start.17
  137.7 27.0 %copy-start.1 = (bf16[17,196,3,64]{1,0,3,2:T(8,128)(2,1)}, bf16[17,196,3,64]{1,0,3,2:T(8,128)(2,1)S(1)}, u32[]{:S(2)}) copy-start(bf16[17,196,3,64]{1,0,3,2:T(8,128)(2,1)S(1)} %squeeze.6) | copy-start | bytes 3838468
  137.7 17.6 %copy-start.11 = (f32[768,96]{0,1:T(8,128)S(1)}, f32[768,96]{0,1:T(8,128)}, u32[]{:S(2)}) copy-start(f32[768,96]{0,1:T(8,128)} %param.28) | copy-start | bytes 884740
  137.7 17.5 %copy-start.25 = (f32[768,96]{0,1:T(8,128)S(1)}, f32[768,96]{0,1:T(8,128)}, u32[]{:S(2)}) copy-start(f32[768,96]{0,1:T(8,128)} %param.29) | copy-start | bytes 884740
  137.7 17.5 %copy-start.26 = (f32[768,96]{0,1:T(8,128)S(1)}, f32[768,96]{0,1:T(8,128)}, u32[]{:S(2)}) copy-start(f32[768,96]{0,1:T(8,128)} %param.30) | copy-start | bytes 884740
  157.9 179.6 %reduce-scatter.15.cloned.1.call-start = ((), (), s32[]{:S(2)}) async-start(), calls=%async_computation.9 | async-start | bytes 884736
  158.3 7.0 copy-start
  171.2 6.0 copy-start.19
  177.2 169.0 %reduce-scatter.13.cloned.1.call-start = ((), (), s32[]{:S(2)}) async-start(), calls=%async_computation.8 | async-start | bytes 2211840
  214.0 16.8 %slice-start = ((s8[10444800]{0:T(1024)(128)(4,1)}), s8[2056192]{0:T(1024)(128)(4,1)S(1)}, s32[]{:S(2)}) async-start(s8[10444800]{0:T(1024)(128)(4,1)} %bitcast.95), calls=%async_computation.11 | async-start | bytes 4112384
  218.0 12.8 %slice-start.1 = ((s8[10444800]{0:T(1024)(128)(4,1)}), s8[4194304]{0:T(1024)(128)(4,1)S(1)}, s32[]{:S(2)}) async-start(s8[10444800]{0:T(1024)(128)(4,1)} %bitcast.95), calls=%async_computation.12 | async-start | bytes 8388608
  218.0 12.8 %slice-start.2 = ((s8[10444800]{0:T(1024)(128)(4,1)}), s8[4194304]{0:T(1024)(128)(4,1)S(1)}, s32[]{:S(2)}) async-start(s8[10444800]{0:T(1024)(128)(4,1)} %bitcast.95), calls=%async_computation.13 | async-start | bytes 8388608
  230.8 5.9 copy-start.3
  279.7 138.5 %reduce-scatter.9.cloned.1.call-start = ((), (), s32[]{:S(2)}) async-start(), calls=%async_computation.6 | async-start | bytes 2654208 | tf_op jit(solution)/shard_map/reduce_scatter | solution.py:147
  295.0 8.7 %copy-start.44 = (bf16[768,768]{0,1:T(8,128)(2,1)S(1)}, bf16[768,768]{0,1:T(8,128)(2,1)}, u32[]{:S(2)}) copy-start(bf16[768,768]{0,1:T(8,128)(2,1)} %all-gather.5.cloned.1.call-done) | copy-start | bytes 3538948
  303.6 9.3 %copy-start.5 = (bf16[3332,192]{0,1:T(8,128)(2,1)S(1)}, bf16[3332,192]{0,1:T(8,128)(2,1)}, u32[]{:S(2)}) copy-start(bf16[3332,192]{0,1:T(8,128)(2,1)} %reshape.143) | copy-start | bytes 3838468
  303.6 9.3 %copy-start.7 = (bf16[192,768]{0,1:T(8,128)(2,1)S(1)}, bf16[192,768]{0,1:T(8,128)(2,1)}, u32[]{:S(2)}) copy-start(bf16[192,768]{0,1:T(8,128)(2,1)} %copy-done.6) | copy-start | bytes 884740
  303.6 300.4 %all-reduce.5.cloned.1.call-start = ((), (), s32[]{:S(2)}) async-start(), calls=%async_computation.10 | async-start | bytes 20496384 | tf_op jit(solution)/shard_map/psum | solution.py:92
  317.0 4.4 copy-start.18
  317.0 4.4 copy-start.20
  329.1 7.3 %copy-start.27 = (f32[3,96,192]{2,1,0:T(8,128)S(1)}, f32[3,96,192]{2,1,0:T(8,128)}, u32[]{:S(2)}) copy-start(f32[3,96,192]{2,1,0:T(8,128)} %param.20) | copy-start | bytes 663556
  329.2 7.5 %copy-start.28 = (f32[3,96,192]{2,1,0:T(8,128)S(1)}, f32[3,96,192]{2,1,0:T(8,128)}, u32[]{:S(2)}) copy-start(f32[3,96,192]{2,1,0:T(8,128)} %param.21) | copy-start | bytes 663556
  329.2 9.3 %copy-start.33 = (f32[192,96]{1,0:T(8,128)S(1)}, f32[192,96]{1,0:T(8,128)}, u32[]{:S(2)}) copy-start(f32[192,96]{1,0:T(8,128)} %param.23) | copy-start | bytes 221188
  329.2 9.3 %copy-start.34 = (f32[192,96]{1,0:T(8,128)S(1)}, f32[192,96]{1,0:T(8,128)}, u32[]{:S(2)}) copy-start(f32[192,96]{1,0:T(8,128)} %param.24) | copy-start | bytes 221188
  336.4 81.8 %copy-start.8 = (f32[96,768]{1,0:T(8,128)S(1)}, f32[96,768]{1,0:T(8,128)}, u32[]{:S(2)}) copy-start(f32[96,768]{1,0:T(8,128)} %param.25) | copy-start | bytes 884740
  336.4 81.8 %copy-start.29 = (f32[96,768]{1,0:T(8,128)S(1)}, f32[96,768]{1,0:T(8,128)}, u32[]{:S(2)}) copy-start(f32[96,768]{1,0:T(8,128)} %param.26) | copy-start | bytes 884740
  336.4 81.8 %copy-start.30 = (f32[96,768]{1,0:T(8,128)S(1)}, f32[96,768]{1,0:T(8,128)}, u32[]{:S(2)}) copy-start(f32[96,768]{1,0:T(8,128)} %param.27) | copy-start | bytes 884740
  336.5 267.6 %copy-start.22 = (f32[3332]{0:T(1024)S(1)}, f32[3332]{0:T(1024)}, u32[]{:S(2)}) copy-start(f32[3332]{0:T(1024)} %copy-done.21) | copy-start | bytes 39988
  336.5 267.6 %copy-start.32 = (f32[3332]{0:T(1024)S(1)}, f32[3332]{0:T(1024)}, u32[]{:S(2)}) copy-start(f32[3332]{0:T(1024)} %copy-done.31) | copy-start | bytes 39988
  336.5 267.6 %copy-start.36 = (f32[768]{0:T(1024)S(1)}, f32[768]{0:T(1024)}, u32[]{:S(2)}) copy-start(f32[768]{0:T(1024)} %copy-done.35) | copy-start | bytes 9220
  339.2 356.1 %copy-start.23 = (f32[192,96]{1,0:T(8,128)}, f32[192,96]{1,0:T(8,128)S(1)}, u32[]{:S(2)}) copy-start(f32[192,96]{1,0:T(8,128)S(1)} %get-tuple-element.144) | copy-start | bytes 221188
  339.2 356.1 %copy-start.24 = (f32[192,96]{1,0:T(8,128)}, f32[192,96]{1,0:T(8,128)S(1)}, u32[]{:S(2)}) copy-start(f32[192,96]{1,0:T(8,128)S(1)} %get-tuple-element.145) | copy-start | bytes 221188
  420.1 274.3 %copy-start.15 = (f32[96,768]{1,0:T(8,128)}, f32[96,768]{1,0:T(8,128)S(1)}, u32[]{:S(2)}) copy-start(f32[96,768]{1,0:T(8,128)S(1)} %get-tuple-element.142) | copy-start | bytes 884740
  420.1 274.3 %copy-start.16 = (f32[96,768]{1,0:T(8,128)}, f32[96,768]{1,0:T(8,128)S(1)}, u32[]{:S(2)}) copy-start(f32[96,768]{1,0:T(8,128)S(1)} %get-tuple-element.143) | copy-start | bytes 884740
  604.1 28.9 %copy-start.39 = (f32[96]{0:T(128)S(1)}, f32[96]{0:T(128)}, u32[]{:S(2)}) copy-start(f32[96]{0:T(128)} %param.31) | copy-start | bytes 1156
  604.1 28.9 %copy-start.41 = (f32[96]{0:T(128)S(1)}, f32[96]{0:T(128)}, u32[]{:S(2)}) copy-start(f32[96]{0:T(128)} %param.32) | copy-start | bytes 1156
  604.1 28.9 %copy-start.42 = (f32[96]{0:T(128)S(1)}, f32[96]{0:T(128)}, u32[]{:S(2)}) copy-start(f32[96]{0:T(128)} %param.33) | copy-start | bytes 1156
  673.3 20.1 %copy-start.37 = (f32[5,2]{0,1:T(2,128)}, f32[5,2]{0,1:T(2,128)S(1)}, u32[]{:S(2)}) copy-start(f32[5,2]{0,1:T(2,128)S(1)} %sqrt.23) | copy-start | bytes 124
  683.0 10.4 %copy-start.12 = (f32[768,96]{0,1:T(8,128)S(1)}, f32[768,96]{0,1:T(8,128)}, u32[]{:S(2)}) copy-start(f32[768,96]{0,1:T(8,128)} %param.28) | copy-start | bytes 884740
  683.0 10.4 %copy-start.13 = (f32[768,96]{0,1:T(8,128)S(1)}, f32[768,96]{0,1:T(8,128)}, u32[]{:S(2)}) copy-start(f32[768,96]{0,1:T(8,128)} %get-tuple-element.140) | copy-start | bytes 884740
  683.0 10.4 %copy-start.14 = (f32[768,96]{0,1:T(8,128)S(1)}, f32[768,96]{0,1:T(8,128)}, u32[]{:S(2)}) copy-start(f32[768,96]{0,1:T(8,128)} %get-tuple-element.141) | copy-start | bytes 884740
  (10 other events, 24.8 us)
Sparse Core Ops, SparseCore 0:
  10.8 43.7 all-gather.2
  74.8 80.4 reduce-scatter.10
  158.0 42.7 all-gather.4
  204.0 61.8 reduce-scatter.14
  279.8 66.3 reduce-scatter.12
  349.5 68.6 reduce-scatter.8
  421.4 182.5 all-reduce.4
where the time goes:
time: 716 us; the launch traced here: 707 us
  waiting for transfers between devices  267 us (37%)
  blocking collectives  155 us (22%)
  matrix products  118 us (16%)
  other arithmetic  75.7 us (11%)
  local copies, waits for them, and re-layouts  66.7 us (9%)
  between operations  23.1 us (3%)
    psum x1, waiting for transfers between devices, local(): lax.psum(partial_sum.astype(jnp.bfloat16), 'tensor').astype(jnp.float32)  183 us
    reduce_scatter x1, waiting for transfers between devices, local(): lax.psum_scatter(grad_widening, 'dp', scatter_dimension=0, tiled=True)  66.1 us
    unnamed x2, blocking collectives  44.8 us
    all_gather x1, blocking collectives, local(): lax.all_gather(master_inward.astype(jnp.bfloat16), 'dp', axis=1, tiled=True)  41.9 us
    psum x1, blocking collectives, local(): trust_norms = jnp.sqrt(lax.psum(local_sums, ('dp', 'tensor')))  36.8 us
    all_gather x1, blocking collectives, local(): lax.all_gather(master_outward.astype(jnp.bfloat16), 'dp', axis=1, tiled=T...  31.7 us
    unnamed x120, local copies, waits for them, and re-layouts  27.1 us
  transfers between devices with their start and end apart: 7, of which 5 were waited for; matrix products, arithmetic and copies ran while one was open for 28% of the time, Pallas kernels for 0%

commit v1 on v0

--- a/solution.py
+++ b/solution.py
@@ -1,7 +1,14 @@
+import functools
+
 import jax
 import jax.numpy as jnp
 from jax import lax
+from jax.experimental import pallas as pl
+from jax.experimental.pallas import tpu as pltpu
 from jax.sharding import PartitionSpec as P
+
+MESH = pl.DeviceIdType.MESH
+PAIR = 2
 
 HEAD_DIM = 64
 SEQ = 196
@@ -24,6 +31,357 @@
         + weight_decay * master
     )
     return (moment, square, update)
+
+
+def greet(place, line, up, down, other):
+    barrier = pltpu.get_barrier_semaphore()
+    pl.semaphore_signal(barrier, inc=1, device_id=other, device_id_type=MESH)
+
+    @pl.when(place < line - 1)
+    def _():
+        pl.semaphore_signal(barrier, inc=1, device_id=up, device_id_type=MESH)
+
+    @pl.when(place > 0)
+    def _():
+        pl.semaphore_signal(barrier, inc=1, device_id=down, device_id_type=MESH)
+
+    pl.semaphore_wait(barrier, 1 + jnp.minimum(place, 1) + jnp.minimum(line - 1 - place, 1))
+
+
+def gather_kernel(line, own_ref, all_ref, own_sem, up_sem, down_sem, pair_sem, recv_sem):
+    me = lax.axis_index("dp")
+    place, side = me // PAIR, me % PAIR
+    up, down, other = {"dp": me + PAIR}, {"dp": me - PAIR}, {"dp": me + 1 - 2 * side}
+    has_up, has_down = place < line - 1, place > 0
+    greet(place, line, up, down, other)
+
+    def move(step, source, block, sems, peer):
+        return pltpu.make_async_remote_copy(
+            src_ref=source,
+            dst_ref=all_ref.at[block],
+            send_sem=sems.at[step],
+            recv_sem=recv_sem.at[block],
+            device_id=peer,
+            device_id_type=MESH,
+        )
+
+    def held(block):
+        return all_ref.at[block]
+
+    def arrived(block, peer):
+        move(0, held(block), block, pair_sem, peer).wait_recv()
+
+    own = pltpu.make_async_copy(own_ref, all_ref.at[me], own_sem)
+
+    @pl.when(has_up)
+    def _():
+        move(place, own_ref, me, up_sem, up).start()
+
+    @pl.when(has_down)
+    def _():
+        move(place, own_ref, me, down_sem, down).start()
+
+    move(place, own_ref, me, pair_sem, other).start()
+    own.start()
+
+    @pl.loop(1, line)
+    def _(step):
+        low, high = place - step, place + step
+
+        @pl.when(low >= 0)
+        def _():
+            block = low * PAIR + side
+            arrived(block, other)
+
+            @pl.when(has_up)
+            def _():
+                move(low, held(block), block, up_sem, up).start()
+
+            move(low, held(block), block, pair_sem, other).start()
+
+        @pl.when(high < line)
+        def _():
+            block = high * PAIR + side
+            arrived(block, other)
+
+            @pl.when(has_down)
+            def _():
+                move(high, held(block), block, down_sem, down).start()
+
+            move(high, held(block), block, pair_sem, other).start()
+
+    own.wait()
+
+    @pl.loop(0, line)
+    def _(spot):
+        block = spot * PAIR + side
+        arrived(spot * PAIR + 1 - side, other)
+        move(spot, held(block), block, pair_sem, other).wait_send()
+
+        @pl.when(jnp.logical_and(has_up, spot <= place))
+        def _():
+            move(spot, held(block), block, up_sem, up).wait_send()
+
+        @pl.when(jnp.logical_and(has_down, spot >= place))
+        def _():
+            move(spot, held(block), block, down_sem, down).wait_send()
+
+
+def gather_blocks(own):
+    rows, width = own.shape
+    devices = lax.axis_size("dp")
+    line = devices // PAIR
+    return pl.pallas_call(
+        functools.partial(gather_kernel, line),
+        out_shape=jax.ShapeDtypeStruct((devices, rows, width), own.dtype),
+        in_specs=[pl.BlockSpec(memory_space=pltpu.VMEM)],
+        out_specs=pl.BlockSpec(memory_space=pl.ANY),
+        scratch_shapes=[
+            pltpu.SemaphoreType.DMA,
+            pltpu.SemaphoreType.DMA((line,)),
+            pltpu.SemaphoreType.DMA((line,)),
+            pltpu.SemaphoreType.DMA((line,)),
+            pltpu.SemaphoreType.DMA((devices,)),
+        ],
+        compiler_params=pltpu.CompilerParams(collective_id=0, has_side_effects=True),
+        cost_estimate=pl.CostEstimate(flops=0, bytes_accessed=100_000_000, transcendentals=0),
+        name="gather_blocks",
+    )(own)
+
+
+def reduce_kernel(
+    line, own_ref, sum_ref, pair_in, up_in, down_in, up_out, down_out,
+    pair_send, pair_recv, up_send, up_recv, down_send, down_recv,
+):
+    me = lax.axis_index("dp")
+    place, side = me // PAIR, me % PAIR
+    up, down, other = {"dp": me + PAIR}, {"dp": me - PAIR}, {"dp": me + 1 - 2 * side}
+    has_up, has_down = place < line - 1, place > 0
+    greet(place, line, up, down, other)
+
+    def pair_move(spot):
+        return pltpu.make_async_remote_copy(
+            src_ref=own_ref.at[spot * PAIR + 1 - side],
+            dst_ref=pair_in.at[spot],
+            send_sem=pair_send.at[spot],
+            recv_sem=pair_recv.at[spot],
+            device_id=other,
+            device_id_type=MESH,
+        )
+
+    def line_move(spot, source, target, sends, recvs, peer):
+        return pltpu.make_async_remote_copy(
+            src_ref=source.at[spot],
+            dst_ref=target.at[spot],
+            send_sem=sends.at[spot],
+            recv_sem=recvs.at[spot],
+            device_id=peer,
+            device_id_type=MESH,
+        )
+
+    def up_move(spot):
+        return line_move(spot, up_out, up_in, up_send, up_recv, up)
+
+    def down_move(spot):
+        return line_move(spot, down_out, down_in, down_send, down_recv, down)
+
+    @pl.loop(0, line)
+    def _(turn):
+        far = line - 1 - turn
+
+        @pl.when(place + far < line)
+        def _():
+            pair_move(place + far).start()
+
+        @pl.when(jnp.logical_and(place - far >= 0, far > 0))
+        def _():
+            pair_move(place - far).start()
+
+    def both(spot):
+        return own_ref[spot * PAIR + side].astype(jnp.float32) + pair_in[spot].astype(jnp.float32)
+
+    @pl.loop(0, line - 1)
+    def _(turn):
+        far = line - 1 - turn
+
+        @pl.when(place + far < line)
+        def _():
+            spot = place + far
+            pair_move(spot).wait_recv()
+
+            @pl.when(has_down)
+            def _():
+                up_move(spot).wait_recv()
+                up_out[spot] = (both(spot) + up_in[spot].astype(jnp.float32)).astype(jnp.bfloat16)
+
+            @pl.when(jnp.logical_not(has_down))
+            def _():
+                up_out[spot] = both(spot).astype(jnp.bfloat16)
+
+            up_move(spot).start()
+
+        @pl.when(place - far >= 0)
+        def _():
+            spot = place - far
+            pair_move(spot).wait_recv()
+
+            @pl.when(has_up)
+            def _():
+                down_move(spot).wait_recv()
+                down_out[spot] = (both(spot) + down_in[spot].astype(jnp.float32)).astype(
+                    jnp.bfloat16
+                )
+
+            @pl.when(jnp.logical_not(has_up))
+            def _():
+                down_out[spot] = both(spot).astype(jnp.bfloat16)
+
+            down_move(spot).start()
+
+    pair_move(place).wait_recv()
+    sum_ref[...] = both(place)
+
+    @pl.when(has_down)
+    def _():
+        up_move(place).wait_recv()
+        sum_ref[...] += up_in[place].astype(jnp.float32)
+
+    @pl.when(has_up)
+    def _():
+        down_move(place).wait_recv()
+        sum_ref[...] += down_in[place].astype(jnp.float32)
+
+    @pl.loop(0, line)
+    def _(spot):
+        pair_move(spot).wait_send()
+
+        @pl.when(spot > place)
+        def _():
+            up_move(spot).wait_send()
+
+        @pl.when(spot < place)
+        def _():
+            down_move(spot).wait_send()
+
+
+def reduce_blocks(own):
+    devices, rows, width = own.shape
+    line = devices // PAIR
+    buffer = pltpu.VMEM((line, rows, width), own.dtype)
+    return pl.pallas_call(
+        functools.partial(reduce_kernel, line),
+        out_shape=jax.ShapeDtypeStruct((rows, width), jnp.float32),
+        in_specs=[pl.BlockSpec(memory_space=pltpu.VMEM)],
+        out_specs=pl.BlockSpec(memory_space=pltpu.VMEM),
+        scratch_shapes=[buffer] * 5 + [pltpu.SemaphoreType.DMA((line,))] * 6,
+        compiler_params=pltpu.CompilerParams(
+            collective_id=1, has_side_effects=True, vmem_limit_bytes=40 * 2**20
+        ),
+        cost_estimate=pl.CostEstimate(flops=0, bytes_accessed=100_000_000, transcendentals=0),
+        name="reduce_blocks",
+    )(own)
+
+
+def total_kernel(
+    devices, ranks, own_ref, sum_ref, rank_in, dp_out, dp_in,
+    rank_send, rank_recv, dp_send, dp_recv,
+):
+    me, rank = lax.axis_index("dp"), lax.axis_index("tensor")
+    barrier = pltpu.get_barrier_semaphore()
+    for shift in range(1, ranks):
+        peer = {"tensor": lax.rem(rank + shift, ranks)}
+        pl.semaphore_signal(barrier, inc=1, device_id=peer, device_id_type=MESH)
+    for shift in range(1, devices):
+        peer = {"dp": lax.rem(me + shift, devices)}
+        pl.semaphore_signal(barrier, inc=1, device_id=peer, device_id_type=MESH)
+    pl.semaphore_wait(barrier, ranks - 1 + devices - 1)
+
+    def rank_move(shift):
+        return pltpu.make_async_remote_copy(
+            src_ref=own_ref,
+            dst_ref=rank_in.at[rank],
+            send_sem=rank_send.at[shift],
+            recv_sem=rank_recv.at[rank],
+            device_id={"tensor": lax.rem(rank + shift, ranks)},
+            device_id_type=MESH,
+        )
+
+    def rank_arrival(source):
+        return pltpu.make_async_remote_copy(
+            src_ref=own_ref,
+            dst_ref=rank_in.at[source],
+            send_sem=rank_send.at[0],
+            recv_sem=rank_recv.at[source],
+            device_id={"tensor": lax.rem(rank + 1, ranks)},
+            device_id_type=MESH,
+        )
+
+    def dp_move(shift):
+        return pltpu.make_async_remote_copy(
+            src_ref=dp_out,
+            dst_ref=dp_in.at[me],
+            send_sem=dp_send.at[shift],
+            recv_sem=dp_recv.at[me],
+            device_id={"dp": lax.rem(me + shift, devices)},
+            device_id_type=MESH,
+        )
+
+    def dp_arrival(source):
+        return pltpu.make_async_remote_copy(
+            src_ref=dp_out,
+            dst_ref=dp_in.at[source],
+            send_sem=dp_send.at[0],
+            recv_sem=dp_recv.at[source],
+            device_id={"dp": lax.rem(me + 1, devices)},
+            device_id_type=MESH,
+        )
+
+    for shift in range(1, ranks):
+        rank_move(shift).start()
+    rank_in[rank] = own_ref[...]
+    for shift in range(1, ranks):
+        rank_arrival(lax.rem(rank + shift, ranks)).wait_recv()
+    part = rank_in[0]
+    for spot in range(1, ranks):
+        part = part + rank_in[spot]
+    dp_out[...] = part
+    for shift in range(1, devices):
+        dp_move(shift).start()
+    dp_in[me] = part
+    for shift in range(1, devices):
+        dp_arrival(lax.rem(me + shift, devices)).wait_recv()
+    whole = dp_in[0]
+    for spot in range(1, devices):
+        whole = whole + dp_in[spot]
+    sum_ref[...] = whole
+    for shift in range(1, ranks):
+        rank_move(shift).wait_send()
+    for shift in range(1, devices):
+        dp_move(shift).wait_send()
+
+
+def total_of(own, collective_id):
+    devices, ranks = lax.axis_size("dp"), lax.axis_size("tensor")
+    return pl.pallas_call(
+        functools.partial(total_kernel, devices, ranks),
+        out_shape=jax.ShapeDtypeStruct(own.shape, own.dtype),
+        in_specs=[pl.BlockSpec(memory_space=pltpu.VMEM)],
+        out_specs=pl.BlockSpec(memory_space=pltpu.VMEM),
+        scratch_shapes=[
+            pltpu.VMEM((ranks,) + own.shape, own.dtype),
+            pltpu.VMEM(own.shape, own.dtype),
+            pltpu.VMEM((devices,) + own.shape, own.dtype),
+            pltpu.SemaphoreType.DMA((ranks,)),
+            pltpu.SemaphoreType.DMA((ranks,)),
+            pltpu.SemaphoreType.DMA((devices,)),
+            pltpu.SemaphoreType.DMA((devices,)),
+        ],
+        compiler_params=pltpu.CompilerParams(
+            collective_id=collective_id, has_side_effects=True
+        ),
+        cost_estimate=pl.CostEstimate(flops=0, bytes_accessed=20_000_000, transcendentals=0),
+        name="total_" + str(collective_id),
+    )(own)
 
 
 def gelu_tanh(values):
@@ -49,28 +407,46 @@
     first_scaling,
     second_scaling,
 ):
-    inward, outward, widening, narrowing, scaling = (
-        lax.all_gather(master_inward.astype(jnp.bfloat16), "dp", axis=1, tiled=True),
-        lax.all_gather(master_outward.astype(jnp.bfloat16), "dp", axis=1, tiled=True),
-        lax.all_gather(master_widening.astype(jnp.bfloat16), "dp", axis=0, tiled=True),
-        lax.all_gather(master_narrowing.astype(jnp.bfloat16), "dp", axis=1, tiled=True),
-        lax.all_gather(master_scaling.astype(jnp.bfloat16), "dp", axis=0, tiled=True),
-    )
+    depth = master_widening.shape[0]
+    hidden_here = master_widening.shape[1]
+    head_cols = master_inward.shape[2]
+    model = inputs.shape[1]
+    cuts = (hidden_here, 2 * hidden_here, 2 * hidden_here + 3 * head_cols)
+    width = cuts[2] + head_cols
+    gain_cols = 128 + (-width) % 128
+    shard = jnp.concatenate(
+        [
+            master_widening,
+            master_narrowing.T,
+            jnp.transpose(master_inward, (1, 0, 2)).reshape(depth, 3 * head_cols),
+            master_outward.T,
+            jnp.broadcast_to(master_scaling[:, None], (depth, gain_cols)),
+        ],
+        axis=1,
+    ).astype(jnp.bfloat16)
+    copies = gather_blocks(shard).reshape(model, width + gain_cols)
+    widening = copies[:, : cuts[0]]
+    narrowing_t = copies[:, cuts[0] : cuts[1]]
+    inward = copies[:, cuts[1] : cuts[2]]
+    outward_t = copies[:, cuts[2] : width]
+    scaling = copies[:, width]
     floats_in = inputs.astype(jnp.float32)
     rows_here = floats_in.shape[0]
     images = rows_here // SEQ
-    heads_here = inward.shape[2] // HEAD_DIM
+    heads_here = head_cols // HEAD_DIM
     factor = HEAD_DIM ** (-0.5)
     centred = floats_in - jnp.mean(floats_in, axis=1, keepdims=True)
     inv_std = lax.rsqrt(jnp.mean(centred * centred, axis=1, keepdims=True) + norm_eps)
     unit_rows = centred * inv_std
     gain_rows = scaling.astype(jnp.float32)
     normed = (unit_rows * gain_rows).astype(jnp.bfloat16)
-    projected = jnp.einsum(
-        "rd,tde->tre", normed, inward, preferred_element_type=jnp.float32
-    ).astype(jnp.bfloat16)
-    blocks = projected.reshape(3, images, SEQ, heads_here, HEAD_DIM)
-    query_rows, key_rows, value_rows = (blocks[0], blocks[1], blocks[2])
+    projected = jnp.dot(normed, inward, preferred_element_type=jnp.float32).astype(jnp.bfloat16)
+    query_rows, key_rows, value_rows = (
+        projected[:, i * head_cols : (i + 1) * head_cols].reshape(
+            images, SEQ, heads_here, HEAD_DIM
+        )
+        for i in range(3)
+    )
     scores = (
         jnp.einsum("bqhd,bkhd->bhqk", query_rows, key_rows, preferred_element_type=jnp.float32)
         * factor
@@ -84,25 +460,22 @@
     attended = attended.astype(jnp.bfloat16).reshape(rows_here, heads_here * HEAD_DIM)
     upper = jnp.dot(normed, widening, preferred_element_type=jnp.float32)
     hidden = gelu_tanh(upper).astype(jnp.bfloat16)
-    partial_sum = jnp.dot(attended, outward, preferred_element_type=jnp.float32) + jnp.dot(
-        hidden, narrowing, preferred_element_type=jnp.float32
-    )
+    partial_sum = jnp.einsum(
+        "re,de->rd", attended, outward_t, preferred_element_type=jnp.float32
+    ) + jnp.einsum("rf,df->rd", hidden, narrowing_t, preferred_element_type=jnp.float32)
     share = rows_here // lax.axis_size("tensor")
     start = lax.axis_index("tensor") * share
-    total = lax.psum(partial_sum.astype(jnp.bfloat16), "tensor").astype(jnp.float32)
-    mixed = lax.dynamic_slice_in_dim(floats_in, start, share, 0) + lax.dynamic_slice_in_dim(
-        total, start, share, 0
-    )
-    output = mixed.astype(jnp.bfloat16)
-    d_attended = jnp.einsum(
-        "rd,ed->re", cotangent, outward, preferred_element_type=jnp.float32
-    ).astype(jnp.bfloat16)
-    grad_outward = jnp.einsum("re,rd->ed", attended, cotangent, preferred_element_type=jnp.float32)
-    d_hidden = jnp.einsum("rd,fd->rf", cotangent, narrowing, preferred_element_type=jnp.float32)
-    grad_narrowing = jnp.einsum("rf,rd->fd", hidden, cotangent, preferred_element_type=jnp.float32)
+    total = lax.psum_scatter(
+        partial_sum.astype(jnp.bfloat16), "tensor", scatter_dimension=0, tiled=True
+    )
+    inputs_mine = lax.dynamic_slice_in_dim(inputs, start, share, 0).astype(jnp.float32)
+    output = (inputs_mine + total.astype(jnp.float32)).astype(jnp.bfloat16)
+    d_attended = jnp.dot(cotangent, outward_t, preferred_element_type=jnp.float32).astype(
+        jnp.bfloat16
+    )
+    d_hidden = jnp.dot(cotangent, narrowing_t, preferred_element_type=jnp.float32)
     gelu_value, gelu_pull = jax.vjp(gelu_tanh, upper)
     d_upper = gelu_pull(d_hidden)[0].astype(jnp.bfloat16)
-    grad_widening = jnp.einsum("rd,rf->df", normed, d_upper, preferred_element_type=jnp.float32)
     back_sum = jnp.einsum("rf,df->rd", d_upper, widening, preferred_element_type=jnp.float32)
     d_att_blocks = d_attended.reshape(images, SEQ, heads_here, HEAD_DIM)
     rescored = (
@@ -127,27 +500,53 @@
         jnp.einsum("bhqk,bqhd->bkhd", d_scores, query_rows, preferred_element_type=jnp.float32)
         * factor
     ).astype(jnp.bfloat16)
-    d_projected = jnp.stack([d_query, d_key, d_value]).reshape(3, rows_here, heads_here * HEAD_DIM)
-    grad_inward = jnp.einsum("rd,tre->tde", normed, d_projected, preferred_element_type=jnp.float32)
+    d_projected = jnp.concatenate(
+        [d.reshape(rows_here, head_cols) for d in (d_query, d_key, d_value)], axis=1
+    )
     back_sum = back_sum + jnp.einsum(
-        "tre,tde->rd", d_projected, inward, preferred_element_type=jnp.float32
-    )
-    d_normed = lax.psum(back_sum.astype(jnp.bfloat16), "tensor").astype(jnp.float32)
-    grad_scaling = jnp.sum(d_normed * unit_rows, axis=0)
+        "re,de->rd", d_projected, inward, preferred_element_type=jnp.float32
+    )
+    d_normed = lax.psum_scatter(
+        back_sum.astype(jnp.bfloat16), "tensor", scatter_dimension=0, tiled=True
+    ).astype(jnp.float32)
+
+    def weight_grad(rows, columns):
+        return jnp.einsum("rd,rf->df", rows, columns, preferred_element_type=jnp.float32)
+
+    grads = jnp.concatenate(
+        [
+            weight_grad(normed, d_upper).astype(jnp.bfloat16),
+            weight_grad(cotangent, hidden).astype(jnp.bfloat16),
+            weight_grad(normed, d_projected).astype(jnp.bfloat16),
+            weight_grad(cotangent, attended).astype(jnp.bfloat16),
+        ],
+        axis=1,
+    )
+    centred_mine = inputs_mine - jnp.mean(inputs_mine, axis=1, keepdims=True)
+    inv_mine = lax.rsqrt(jnp.mean(centred_mine * centred_mine, axis=1, keepdims=True) + norm_eps)
+    unit_mine = centred_mine * inv_mine
+    grad_scaling = jnp.sum(d_normed * unit_mine, axis=0)
     d_unit = d_normed * gain_rows
-    d_floats = inv_std * (
+    d_floats = inv_mine * (
         d_unit
         - jnp.mean(d_unit, axis=1, keepdims=True)
-        - unit_rows * jnp.mean(d_unit * unit_rows, axis=1, keepdims=True)
-    )
-    input_grad = (cotangent.astype(jnp.float32) + d_floats).astype(jnp.bfloat16)
-    grad_inward, grad_outward, grad_widening, grad_narrowing, grad_scaling = (
-        lax.psum_scatter(grad_inward, "dp", scatter_dimension=1, tiled=True),
-        lax.psum_scatter(grad_outward, "dp", scatter_dimension=1, tiled=True),
-        lax.psum_scatter(grad_widening, "dp", scatter_dimension=0, tiled=True),
-        lax.psum_scatter(grad_narrowing, "dp", scatter_dimension=1, tiled=True),
-        lax.psum_scatter(grad_scaling, "dp", scatter_dimension=0, tiled=True),
-    )
+        - unit_mine * jnp.mean(d_unit * unit_mine, axis=1, keepdims=True)
+    )
+    cotangent_mine = lax.dynamic_slice_in_dim(cotangent, start, share, 0).astype(jnp.float32)
+    input_grad = lax.all_gather(
+        (cotangent_mine + d_floats).astype(jnp.bfloat16), "tensor", axis=0, tiled=True
+    )
+    grad_scaling = total_of(grad_scaling.reshape(-1, 128), 2).reshape(-1)
+    grad_scaling = lax.dynamic_slice_in_dim(
+        grad_scaling, lax.axis_index("dp") * depth, depth, 0
+    )
+    summed = reduce_blocks(grads.reshape(lax.axis_size("dp"), depth, width))
+    grad_widening = summed[:, : cuts[0]]
+    grad_narrowing = summed[:, cuts[0] : cuts[1]].T
+    grad_inward = jnp.transpose(
+        summed[:, cuts[1] : cuts[2]].reshape(depth, 3, head_cols), (1, 0, 2)
+    )
+    grad_outward = summed[:, cuts[2] :].T
     part_in = lamb_parts(master_inward, first_inward, second_inward, grad_inward)
     part_out = lamb_parts(master_outward, first_outward, second_outward, grad_outward)
     part_wide = lamb_parts(master_widening, first_widening, second_widening, grad_widening)
@@ -175,7 +574,8 @@
             * replicas,
         ]
     )
-    trust_norms = jnp.sqrt(lax.psum(local_sums, ("dp", "tensor")))
+    packed = jnp.zeros((8, 128), jnp.float32).at[:5, :2].set(local_sums)
+    trust_norms = jnp.sqrt(total_of(packed, 3)[:5, :2])
     fresh_in = master_inward - learn_rate * (trust_norms[0, 0] / trust_norms[0, 1]) * part_in[2]
     fresh_out = master_outward - learn_rate * (trust_norms[1, 0] / trust_norms[1, 1]) * part_out[2]
     fresh_wide = (

time: 716 us -> 510 us (0.71)
  waiting for transfers between devices: 267 us -> 0.02 us
  Pallas kernels: 0 us -> 112 us
  blocking collectives: 155 us -> 90.4 us
  local copies, waits for them, and re-layouts: 66.7 us -> 90.6 us
  other arithmetic: 75.7 us -> 57.6 us
    psum x1 -> x0, waiting for transfers between devices: 183 us -> none  [local(): lax.psum(partial_sum.astype(jnp.bfloat16), 'tensor').astype(jnp.float32)]
    pallas_call x0 -> x4, Pallas kernels: none -> 112 us  [the longest x1 49.2 us: gather_blocks(): pl.pallas_call(functools.partial(gather_kernel, line), out_shape=jax.Shap...]
    reduce_scatter x2 -> x0, waiting for transfers between devices: 73.9 us -> none  [the longest x1 66.1 us: local(): lax.psum_scatter(grad_widening, 'dp', scatter_dimension=0, tiled=True)]
    all_gather x2 -> x0, blocking collectives: 73.6 us -> none  [the longest x1 41.9 us: local(): lax.all_gather(master_inward.astype(jnp.bfloat16), 'dp', axis=1, tiled=True)]
    unnamed x2 -> x1, blocking collectives: 44.8 us -> 90.4 us
    psum x1 -> x0, blocking collectives: 36.8 us -> none  [local(): trust_norms = jnp.sqrt(lax.psum(local_sums, ('dp', 'tensor')))]
    reshape x0 -> x7, local copies, waits for them, and re-layouts: none -> 24.3 us  [the longest x3 15.8 us: local(): projected[:, i * head_cols:(i + 1) * head_cols]]
    convert_element_type x5 -> x0, other arithmetic: 23.4 us -> none  [the longest x1 10.4 us: local(): input_grad = (cotangent.astype(jnp.float32) + d_floats).astype(jnp.bfloat16)]
  transfers between devices with their start and end apart: 7 -> 3, of which waited for: 5 -> 0; matrix products, arithmetic and copies ran while one was open for 28% -> 17% of each run, Pallas kernels for 0% -> 13%
where the time goes in v1:
time: 510 us; the launch traced here: 502 us
  matrix products  124 us (24%)
  Pallas kernels  112 us (22%)
  local copies, waits for them, and re-layouts  90.6 us (18%)
  blocking collectives  90.4 us (18%)
  other arithmetic  57.6 us (11%)
  between operations  22.4 us (4%)
    unnamed x1, blocking collectives  90.4 us
    pallas_call x1, Pallas kernels, gather_blocks(): pl.pallas_call(functools.partial(gather_kernel, line), out_shape=jax.Shap...  49.2 us
    pallas_call x1, Pallas kernels, reduce_blocks(): pl.pallas_call(functools.partial(reduce_kernel, line), out_shape=jax.Shap...  42 us
    unnamed x120, local copies, waits for them, and re-layouts  40.5 us
    dot_general x4, matrix products, weight_grad(): jnp.einsum('rd,rf->df', rows, columns, preferred_element_type=jnp.float32)  26.6 us
    pallas_call x2, Pallas kernels, total_of(): pl.pallas_call(functools.partial(total_kernel, devices, ranks), out_shape...  20.8 us
    reshape x3, local copies, waits for them, and re-layouts, local(): projected[:, i * head_cols:(i + 1) * head_cols]  15.8 us
    dot_general x1, matrix products, local(): jnp.dot(cotangent, narrowing_t, preferred_element_type=jnp.float32)  13 us
  transfers between devices with their start and end apart: 3, of which 0 were waited for; matrix products, arithmetic and copies ran while one was open for 17% of the time, Pallas kernels for 13%

profile of v1, /device:TPU:0, one launch (start us, length us, event | category | flops | bytes accessed | tf_op | source)
XLA Modules:
  0.0 501.9 jit_solution(4862423681755700317)
XLA Ops:
  14.6 49.2 %gather_blocks.1 = bf16[8,96,2432]{2,1,0:T(8,128)(2,1)} custom-call(bf16[96,2432]{1,0:T(8,128)(2,1)} %concatenate.19.own_ref), custom_call_target="tpu_custom_call" | custom-call | bytes 100000000 | tf_op jit(solution)/shard_map/gather_blocks/pallas_call | solution.py:134
  64.9 3.4 convert_reduce_fusion
  68.3 4.1 fusion.4
  74.5 5.6 %convolution_convert_fusion = bf16[3332,576]{0,1:T(8,128)(2,1)S(1)} fusion(bf16[3332,768]{1,0:T(8,128)(2,1)S(1)} %fusion.6, bf16[768,2432]{1,0:T(8,128)(2,1)} %bitcast.126), kind=kOutput, calls=%fused_computation.30 | convolution fusion | flops 2949859584 | bytes 9939456 | tf_op jit(solution)/shard_map/dot_general | solution.py:443
  82.1 4.2 reshape.219
  86.3 5.7 %reshape.220 = bf16[17,196,3,64]{1,0,3,2:T(8,128)(2,1)} reshape(bf16[3332,192]{0,1:T(8,128)(2,1)} %get-tuple-element.165) | data formatting | bytes 2558976 | tf_op jit(solution)/shard_map/reshape | solution.py:445
  92.0 3.9 multiply_reduce_fusion.1
  96.0 2.4 exponential_reduce_fusion
  100.0 5.6 %fusion.18 = bf16[3332,192]{0,1:T(8,128)(2,1)} fusion(bf16[3332,768]{1,0:T(8,128)(2,1)} %param.20, bf16[768,2432]{1,0:T(8,128)(2,1)} %bitcast.127), kind=kOutput, calls=%fused_computation.32 | convolution fusion | flops 983286528 | bytes 6796800 | tf_op jit(solution)/shard_map/dot_general | solution.py:473
  105.6 4.2 reshape.222
  109.8 5.9 %reshape.218 = bf16[17,196,3,64]{1,0,3,2:T(8,128)(2,1)} reshape(bf16[3332,192]{0,1:T(8,128)(2,1)} %get-tuple-element.166) | data formatting | bytes 2558976 | tf_op jit(solution)/shard_map/reshape | solution.py:445
  115.8 7.3 %fusion.34 = bf16[17,196,3,64]{1,3,2,0:T(8,128)(2,1)} fusion(bf16[17,196,3,64]{1,0,3,2:T(8,128)(2,1)S(1)} %reshape.222, f32[17,3,196,196]{2,3,1,0:T(8,128)} %copy-done.2, f32[17,3,196]{2,1,0:T(4,128)S(1)} %log_add_fusion), kind=kOutput, calls=%fused_computation.60 | convolution fusion | flops 257297040 | bytes 10435824 | tf_op jit(solution)/shard_map/bhqk,bqhd->bkhd/dot_general | solution.py:490
  123.1 9.5 %multiply_reduce_fusion = (f32[17,3,196]{2,1,0:T(4,128)}, f32[17,3,196,196]{2,3,1,0:T(8,128)S(1)}) fusion(f32[17,3,196,196]{2,3,1,0:T(8,128)} %copy-done.2, f32[17,3,196]{2,1,0:T(4,128)S(1)} %log_add_fusion, bf16[17,196,3,64]{1,0,3,2:T(8,128)(2,1)} %reshape.218, bf16[17,196,3,64]{1,0,3,2:T(8,128)(2,1)} %copy-done.4), kind=kOutput, calls=%fused_computation.7 | convolution fusion | flops 258606512 | bytes 18312672 | tf_op jit(solution)/shard_map/bqhd,bkhd->bhqk/dot_general | solution.py:487
  132.6 3.8 multiply_convert_fusion
  136.4 4.8 fusion.36
  143.4 3.3 fusion.33
  147.1 6.9 %fusion.55 = f32[3332,768]{1,0:T(8,128)} fusion(bf16[3332,768]{1,0:T(8,128)(2,1)S(1)} %bitcast.135, bf16[768,2432]{1,0:T(8,128)(2,1)S(1)} %bitcast.131), kind=kOutput, calls=%fused_computation.83 | convolution fusion | flops 3930587136 | bytes 16539648 | tf_op jit(solution)/shard_map/dot_general | solution.py:461
  154.1 13.0 %fusion.13 = bf16[3332,768]{1,0:T(8,128)(2,1)} fusion(f32[3332,768]{1,0:T(8,128)} %fusion.55, bf16[3332,768]{1,0:T(8,128)(2,1)S(1)} %bitcast.122, bf16[768,2432]{1,0:T(8,128)(2,1)S(1)} %bitcast.132), kind=kOutput, calls=%fused_computation.19 | convolution fusion | flops 3981766656 | bytes 21657600 | tf_op jit(solution)/shard_map/dot_general | solution.py:476
  167.1 8.6 %fusion.51 = f32[3332,768]{1,0:T(8,128)} fusion(bf16[768,2432]{1,0:T(8,128)(2,1)S(1)} %bitcast.133, f32[3332,768]{1,0:T(8,128)S(1)} %copy-done.29), kind=kOutput, calls=%fused_computation.79 | convolution fusion | flops 3953617920 | bytes 21663744 | tf_op jit(solution)/shard_map/rf,df->rd/dot_general | solution.py:465
  176.7 2.6 reshape.225
  179.4 2.4 copy.164
  181.8 3.0 reshape.224
  184.8 2.4 copy.161
  187.3 2.6 reshape.223
  189.9 2.5 constant_dynamic-update-slice_fusion.2
  192.4 2.4 copy.156
  194.9 2.6 reshape.221
  197.5 11.1 %fusion.53 = f32[3332,768]{1,0:T(8,128)} fusion(bf16[3332,768]{1,0:T(8,128)(2,1)} %fusion.13, bf16[768,2432]{1,0:T(8,128)(2,1)} %bitcast.128), kind=kOutput, calls=%fused_computation.81 | convolution fusion | flops 3930587136 | bytes 16539648 | tf_op jit(solution)/shard_map/rf,df->rd/dot_general | solution.py:479
  209.0 10.6 %add_convert_fusion = bf16[3332,768]{1,0:T(8,128)(2,1)} fusion(f32[3332,768]{1,0:T(8,128)} %fusion.53, bf16[3332,576]{0,1:T(8,128)(2,1)S(1)} %constant_dynamic-update-slice_fusion, bf16[768,2432]{1,0:T(8,128)(2,1)} %bitcast.129), kind=kOutput, calls=%fused_computation.25 | convolution fusion | flops 2953058304 | bytes 20187648 | tf_op jit(solution)/shard_map/re,de->rd/dot_general | solution.py:506
  219.6 5.2 %add_convert_fusion.1 = bf16[3332,768]{1,0:T(8,128)(2,1)} fusion(f32[3332,768]{1,0:T(8,128)S(1)} %bitcast.120, bf16[3332,192]{0,1:T(8,128)(2,1)S(1)} %copy-done.12, bf16[768,2432]{1,0:T(8,128)(2,1)} %bitcast.130), kind=kOutput, calls=%fused_computation.26 | convolution fusion | flops 987764736 | bytes 17026560 | tf_op jit(solution)/shard_map/re,de->rd/dot_general | solution.py:463
  224.9 90.4 %fusion.70 = (bf16[840,768]{1,0:T(8,128)(2,1)S(1)}, bf16[840,768]{1,0:T(8,128)(2,1)S(1)}) fusion(bf16[3332,768]{1,0:T(8,128)(2,1)} %add_convert_fusion.1, bf16[3332,768]{1,0:T(8,128)(2,1)} %add_convert_fusion), kind=kCustom, calls=%all-reduce-scatter.2 | all-reduce-scatter fusion | flops 5160961 | bytes 12816896
  316.7 3.2 collective-permute-start
  320.0 4.1 fusion.39
  330.2 6.1 %concatenate.23 = bf16[861,768]{1,0:T(8,128)(2,1)S(1)} concatenate(bf16[21,768]{1,0:T(8,128)(2,1)S(1)} %collective-permute-done.1, bf16[840,768]{1,0:T(8,128)(2,1)} %copy-done.9), dimensions={0} | concatenate | bytes 2644992
  336.3 3.7 fusion.31
  340.0 7.3 %concatenate.22 = bf16[861,768]{1,0:T(8,128)(2,1)} concatenate(bf16[21,768]{1,0:T(8,128)(2,1)S(1)} %collective-permute-done, bf16[840,768]{1,0:T(8,128)(2,1)S(1)} %get-tuple-element.136), dimensions={0} | concatenate | bytes 2644992
  347.3 5.3 %fusion.38 = (bf16[1,833,768]{2,1,0:T(8,128)(2,1)}, bf16[833,768]{1,0:T(8,128)(2,1)}) fusion(f32[833]{0:T(1024)S(1)} %get-tuple-element.185, f32[833]{0:T(1024)S(1)} %get-tuple-element.186, f32[768]{0:T(1024)S(1)} %convert_reduce_fusion.2, f32[833]{0:T(1024)S(1)} %add_rsqrt_fusion.1, f32[833]{0:T(1024)S(1)} %broadcast_multiply_fusion.3, ...), kind=kLoop, calls=%fused_computation.65 | loop fusion | flops 9596160 | bytes 7693336
  352.6 7.4 %convolution_convert_fusion.6 = bf16[768,576]{0,1:T(8,128)(2,1)S(1)} fusion(bf16[3332,768]{1,0:T(8,128)(2,1)} %copy-done.13, bf16[3332,576]{0,1:T(8,128)(2,1)} %copy-done.24), kind=kOutput, calls=%fused_computation.63 | convolution fusion | flops 2948382720 | bytes 9841152 | tf_op jit(solution)/shard_map/rd,rf->df/dot_general | solution.py:514
  360.1 10.0 %fusion.37 = bf16[768,768]{0,1:T(8,128)(2,1)S(1)} fusion(bf16[3332,768]{1,0:T(8,128)(2,1)S(1)} %bitcast.124, f32[3332,768]{1,0:T(8,128)} %fusion.55), kind=kOutput, calls=%fused_computation.64 | convolution fusion | flops 3954207744 | bytes 16533504 | tf_op jit(solution)/shard_map/rd,rf->df/dot_general | solution.py:514
  370.2 5.0 %convolution_convert_fusion.5 = bf16[768,768]{0,1:T(8,128)(2,1)S(1)} fusion(bf16[3332,768]{1,0:T(8,128)(2,1)S(1)} %bitcast.137, bf16[3332,768]{1,0:T(8,128)(2,1)S(1)} %bitcast.143), kind=kOutput, calls=%fused_computation.58 | convolution fusion | flops 3931176960 | bytes 11415552 | tf_op jit(solution)/shard_map/rd,rf->df/dot_general | solution.py:514
  377.3 4.3 copy.169
  381.6 42.0 %reduce_blocks.1 = f32[96,2304]{1,0:T(8,128)S(1)} custom-call(bf16[8,96,2304]{2,1,0:T(8,128)(2,1)S(1)} %bitcast.114), custom_call_target="tpu_custom_call" | custom-call | bytes 100000000 | tf_op jit(solution)/shard_map/reduce_blocks/pallas_call | solution.py:271
  439.0 2.8 multiply_reduce_fusion.3
  441.8 2.7 maximum_bitcast_fusion.2
  446.0 2.7 maximum_bitcast_fusion
  448.7 10.5 %total_2.1 = f32[6,128]{1,0:T(8,128)} custom-call(f32[6,128]{1,0:T(8,128)} %bitcast.140), custom_call_target="tpu_custom_call" | custom-call | bytes 20000000 | tf_op jit(solution)/shard_map/total_2/pallas_call | solution.py:365
  463.0 10.3 %total_3.1 = f32[8,128]{1,0:T(8,128)} custom-call(f32[8,128]{1,0:T(8,128)} %scatter.4.own_ref), custom_call_target="tpu_custom_call" | custom-call | bytes 20000000 | tf_op jit(solution)/shard_map/total_3/pallas_call | solution.py:365
  488.7 6.1 %reshape.232 = bf16[3332,768]{1,0:T(8,128)(2,1)} reshape(bf16[4,833,768]{2,1,0:T(8,128)(2,1)} %all-gather.3.cloned.1.call-done) | data formatting | bytes 10235904
  (172 shorter events, 56.6 us)
Async XLA Ops:
  7.2 481.5 %all-gather.3.cloned.1.call-start = ((), (), s32[]{:S(2)}) async-start(), calls=%async_computation | async-start | bytes 6451200 | tf_op jit(solution)/shard_map/all_gather | solution.py:536
  8.2 55.6 %copy-start.17 = (f32[192,96]{0,1:T(8,128)}, f32[192,96]{0,1:T(8,128)S(1)}, u32[]{:S(2)}) copy-start(f32[192,96]{0,1:T(8,128)S(1)} %copy.149) | copy-start | bytes 221188
  64.7 7.6 %slice-start.3 = ((s8[5124096]{0:T(1024)(128)(4,1)}), s8[929792]{0:T(1024)(128)(4,1)S(1)}, s32[]{:S(2)}) async-start(s8[5124096]{0:T(1024)(128)(4,1)} %bitcast.117), calls=%async_computation.4 | async-start | bytes 1859584
  64.9 7.5 %slice-start.4 = ((s8[5124096]{0:T(1024)(128)(4,1)}), s8[4194304]{0:T(1024)(128)(4,1)S(1)}, s32[]{:S(2)}) async-start(s8[5124096]{0:T(1024)(128)(4,1)} %bitcast.117), calls=%async_computation.5 | async-start | bytes 8388608
  74.4 5.6 %copy-start.13 = (bf16[3332,768]{1,0:T(8,128)(2,1)}, bf16[3332,768]{1,0:T(8,128)(2,1)S(1)}, u32[]{:S(2)}) copy-start(bf16[3332,768]{1,0:T(8,128)(2,1)S(1)} %fusion.6) | copy-start | bytes 15353860
  86.3 9.7 %copy-start.5 = (bf16[17,196,3,64]{1,0,3,2:T(8,128)(2,1)}, bf16[17,196,3,64]{1,0,3,2:T(8,128)(2,1)S(1)}, u32[]{:S(2)}) copy-start(bf16[17,196,3,64]{1,0,3,2:T(8,128)(2,1)S(1)} %reshape.219) | copy-start | bytes 3838468
  96.0 4.0 copy-start.2
  109.8 6.0 %copy-start.4 = (bf16[17,196,3,64]{1,0,3,2:T(8,128)(2,1)}, bf16[17,196,3,64]{1,0,3,2:T(8,128)(2,1)S(1)}, u32[]{:S(2)}) copy-start(bf16[17,196,3,64]{1,0,3,2:T(8,128)(2,1)S(1)} %reshape.222) | copy-start | bytes 3838468
  115.7 16.8 %slice-start = ((s8[10444800]{0:T(1024)(128)(4,1)}), s8[4194304]{0:T(1024)(128)(4,1)S(1)}, s32[]{:S(2)}) async-start(s8[10444800]{0:T(1024)(128)(4,1)} %bitcast.115), calls=%async_computation.1 | async-start | bytes 8388608
  115.8 16.8 %slice-start.1 = ((s8[10444800]{0:T(1024)(128)(4,1)}), s8[4194304]{0:T(1024)(128)(4,1)S(1)}, s32[]{:S(2)}) async-start(s8[10444800]{0:T(1024)(128)(4,1)} %bitcast.115), calls=%async_computation.2 | async-start | bytes 8388608
  123.1 9.5 %slice-start.2 = ((s8[10444800]{0:T(1024)(128)(4,1)}), s8[2056192]{0:T(1024)(128)(4,1)S(1)}, s32[]{:S(2)}) async-start(s8[10444800]{0:T(1024)(128)(4,1)} %bitcast.115), calls=%async_computation.3 | async-start | bytes 4112384
  136.4 4.8 copy-start.6
  141.2 5.5 %slice-start.12 = ((s8[5124096]{0:T(1024)(128)(4,1)}), s8[929792]{0:T(1024)(128)(4,1)S(1)}, s32[]{:S(2)}) async-start(s8[5124096]{0:T(1024)(128)(4,1)} %bitcast.134), calls=%async_computation.13 | async-start | bytes 1859584
  143.4 3.7 slice-start.13
  143.4 10.6 %slice-start.8 = ((s8[5124096]{0:T(1024)(128)(4,1)}), s8[929792]{0:T(1024)(128)(4,1)S(1)}, s32[]{:S(2)}) async-start(s8[5124096]{0:T(1024)(128)(4,1)} %bitcast.121), calls=%async_computation.9 | async-start | bytes 1859584
  147.1 6.9 %slice-start.9 = ((s8[5124096]{0:T(1024)(128)(4,1)}), s8[4194304]{0:T(1024)(128)(4,1)S(1)}, s32[]{:S(2)}) async-start(s8[5124096]{0:T(1024)(128)(4,1)} %bitcast.121), calls=%async_computation.10 | async-start | bytes 8388608
  154.1 13.0 %copy-start.29 = (f32[3332,768]{1,0:T(8,128)S(1)}, f32[3332,768]{1,0:T(8,128)}, u32[]{:S(2)}) copy-start(f32[3332,768]{1,0:T(8,128)} %fusion.55) | copy-start | bytes 30707716
  167.1 8.6 %copy-start.7 = (bf16[17,196,3,64]{1,3,2,0:T(8,128)(2,1)S(1)}, bf16[17,196,3,64]{1,3,2,0:T(8,128)(2,1)}, u32[]{:S(2)}) copy-start(bf16[17,196,3,64]{1,3,2,0:T(8,128)(2,1)} %fusion.34) | copy-start | bytes 3838468
  197.5 11.1 %copy-start.11 = (bf16[3332,192]{0,1:T(8,128)(2,1)S(1)}, bf16[3332,192]{0,1:T(8,128)(2,1)}, u32[]{:S(2)}) copy-start(bf16[3332,192]{0,1:T(8,128)(2,1)} %reshape.224) | copy-start | bytes 3838468
  197.5 11.1 %copy-start.23 = (bf16[3332,576]{0,1:T(8,128)(2,1)S(1)}, bf16[3332,576]{0,1:T(8,128)(2,1)}, u32[]{:S(2)}) copy-start(bf16[3332,576]{0,1:T(8,128)(2,1)} %constant_dynamic-update-slice_fusion.2) | copy-start | bytes 11515396
  197.5 11.2 %copy-start.10 = (bf16[3332,192]{0,1:T(8,128)(2,1)S(1)}, bf16[3332,192]{0,1:T(8,128)(2,1)}, u32[]{:S(2)}) copy-start(bf16[3332,192]{0,1:T(8,128)(2,1)} %reshape.225) | copy-start | bytes 3838468
  208.8 10.9 %slice-start.5 = ((s8[10248192]{0:T(1024)(128)(4,1)}), s8[4194304]{0:T(1024)(128)(4,1)S(1)}, s32[]{:S(2)}) async-start(s8[10248192]{0:T(1024)(128)(4,1)} %bitcast.119), calls=%async_computation.6 | async-start | bytes 8388608
  208.9 10.7 %copy-start.24 = (bf16[3332,576]{0,1:T(8,128)(2,1)}, bf16[3332,576]{0,1:T(8,128)(2,1)S(1)}, u32[]{:S(2)}) copy-start(bf16[3332,576]{0,1:T(8,128)(2,1)S(1)} %constant_dynamic-update-slice_fusion) | copy-start | bytes 11515396
  209.0 10.7 %slice-start.6 = ((s8[10248192]{0:T(1024)(128)(4,1)}), s8[4194304]{0:T(1024)(128)(4,1)S(1)}, s32[]{:S(2)}) async-start(s8[10248192]{0:T(1024)(128)(4,1)} %bitcast.119), calls=%async_computation.7 | async-start | bytes 8388608
  209.0 10.7 %slice-start.7 = ((s8[10248192]{0:T(1024)(128)(4,1)}), s8[1859584]{0:T(1024)(128)(4,1)S(1)}, s32[]{:S(2)}) async-start(s8[10248192]{0:T(1024)(128)(4,1)} %bitcast.119), calls=%async_computation.8 | async-start | bytes 3719168
  209.0 10.7 %copy-start.12 = (bf16[3332,192]{0,1:T(8,128)(2,1)S(1)}, bf16[3332,192]{0,1:T(8,128)(2,1)}, u32[]{:S(2)}) copy-start(bf16[3332,192]{0,1:T(8,128)(2,1)} %reshape.221) | copy-start | bytes 3838468
  315.2 13.7 %copy-start.9 = (bf16[840,768]{1,0:T(8,128)(2,1)}, bf16[840,768]{1,0:T(8,128)(2,1)S(1)}, u32[]{:S(2)}) copy-start(bf16[840,768]{1,0:T(8,128)(2,1)S(1)} %get-tuple-element.137) | copy-start | bytes 3870724
  315.2 12.8 %copy-start.19 = (f32[3,96,192]{2,1,0:T(8,128)S(1)}, f32[3,96,192]{2,1,0:T(8,128)}, u32[]{:S(2)}) copy-start(f32[3,96,192]{2,1,0:T(8,128)} %param.21) | copy-start | bytes 663556
  315.3 14.9 %collective-permute-start.1 = (bf16[21,768]{1,0:T(8,128)(2,1)S(1)}, bf16[21,768]{1,0:T(8,128)(2,1)S(1)}, u32[]{:S(2)}, u32[]{:S(2)}) collective-permute-start(bf16[21,768]{1,0:T(8,128)(2,1)S(1)} %slice.121), channel_id=1, source_target_pairs={{0,1},{1,2},{2,3},{4,5},{5,6},{6,7},{8,9},{9,10},{10,11},{12,13},{... | collective-permute-start | bytes 96776
  316.7 12.2 %copy-start.28 = (u32[32]{0:T(128)S(1)}, u32[32]{0:T(128)}, u32[]{:S(2)}) copy-start(u32[32]{0:T(128)} %constant.123) | copy-start | bytes 388
  316.7 23.3 %collective-permute-start = (bf16[21,768]{1,0:T(8,128)(2,1)S(1)}, bf16[21,768]{1,0:T(8,128)(2,1)S(1)}, u32[]{:S(2)}, u32[]{:S(2)}) collective-permute-start(bf16[21,768]{1,0:T(8,128)(2,1)S(1)} %slice.120), channel_id=1, source_target_pairs={{0,1},{1,2},{2,3},{4,5},{5,6},{6,7},{8,9},{9,10},{10,11},{12,13},{... | collective-permute-start | bytes 96776
  347.3 12.8 %slice-start.10 = ((s8[5124096]{0:T(1024)(128)(4,1)}), s8[929792]{0:T(1024)(128)(4,1)S(1)}, s32[]{:S(2)}) async-start(s8[5124096]{0:T(1024)(128)(4,1)} %bitcast.123), calls=%async_computation.11 | async-start | bytes 1859584
  352.6 7.5 %slice-start.11 = ((s8[5124096]{0:T(1024)(128)(4,1)}), s8[4194304]{0:T(1024)(128)(4,1)S(1)}, s32[]{:S(2)}) async-start(s8[5124096]{0:T(1024)(128)(4,1)} %bitcast.123), calls=%async_computation.12 | async-start | bytes 8388608
  352.6 17.5 %slice-start.14 = ((s8[5124096]{0:T(1024)(128)(4,1)}), s8[4194304]{0:T(1024)(128)(4,1)S(1)}, s32[]{:S(2)}) async-start(s8[5124096]{0:T(1024)(128)(4,1)} %bitcast.136), calls=%async_computation.15 | async-start | bytes 8388608
  352.6 17.5 %slice-start.16 = ((s8[5124096]{0:T(1024)(128)(4,1)}), s8[4194304]{0:T(1024)(128)(4,1)S(1)}, s32[]{:S(2)}) async-start(s8[5124096]{0:T(1024)(128)(4,1)} %bitcast.142), calls=%async_computation.17 | async-start | bytes 8388608
  360.1 10.1 %slice-start.15 = ((s8[5124096]{0:T(1024)(128)(4,1)}), s8[929792]{0:T(1024)(128)(4,1)S(1)}, s32[]{:S(2)}) async-start(s8[5124096]{0:T(1024)(128)(4,1)} %bitcast.136), calls=%async_computation.16 | async-start | bytes 1859584
  360.1 10.1 %slice-start.17 = ((s8[5124096]{0:T(1024)(128)(4,1)}), s8[929792]{0:T(1024)(128)(4,1)S(1)}, s32[]{:S(2)}) async-start(s8[5124096]{0:T(1024)(128)(4,1)} %bitcast.142), calls=%async_computation.18 | async-start | bytes 1859584
  424.5 9.4 %copy-start.18 = (f32[192,96]{0,1:T(8,128)S(1)}, f32[192,96]{0,1:T(8,128)}, u32[]{:S(2)}) copy-start(f32[192,96]{0,1:T(8,128)} %copy-done.17) | copy-start | bytes 221188
  424.5 12.6 %copy-start.15 = (f32[96,768]{1,0:T(8,128)S(1)}, f32[96,768]{1,0:T(8,128)}, u32[]{:S(2)}) copy-start(f32[96,768]{1,0:T(8,128)} %param.27) | copy-start | bytes 884740
  424.5 14.5 %copy-start.14 = (f32[768,96]{0,1:T(8,128)S(1)}, f32[768,96]{0,1:T(8,128)}, u32[]{:S(2)}) copy-start(f32[768,96]{0,1:T(8,128)} %param.30) | copy-start | bytes 884740
  424.5 34.6 %copy-start.25 = (f32[96]{0:T(128)S(1)}, f32[96]{0:T(128)}, u32[]{:S(2)}) copy-start(f32[96]{0:T(128)} %param.33) | copy-start | bytes 1156
  424.5 34.6 %copy-start.26 = (f32[96]{0:T(128)S(1)}, f32[96]{0:T(128)}, u32[]{:S(2)}) copy-start(f32[96]{0:T(128)} %param.34) | copy-start | bytes 1156
  424.5 34.6 %copy-start.27 = (f32[96]{0:T(128)S(1)}, f32[96]{0:T(128)}, u32[]{:S(2)}) copy-start(f32[96]{0:T(128)} %param.35) | copy-start | bytes 1156
  424.6 9.4 %copy-start.1 = (f32[96,2304]{1,0:T(8,128)S(1)}, f32[96,2304]{1,0:T(8,128)}, u32[]{:S(2)}) copy-start(f32[96,2304]{1,0:T(8,128)} %copy-done) | copy-start | bytes 2654212
  424.7 58.8 %copy-start.16 = (f32[3,96,192]{1,2,0:T(8,128)S(1)}, f32[3,96,192]{1,2,0:T(8,128)}, u32[]{:S(2)}) copy-start(f32[3,96,192]{1,2,0:T(8,128)} %copy.176) | copy-start | bytes 663556
  439.0 55.8 %copy-start.20 = (f32[96,768]{1,0:T(8,128)}, f32[96,768]{1,0:T(8,128)S(1)}, u32[]{:S(2)}) copy-start(f32[96,768]{1,0:T(8,128)S(1)} %get-tuple-element.154) | copy-start | bytes 884740
  439.0 55.8 %copy-start.21 = (f32[96,768]{1,0:T(8,128)}, f32[96,768]{1,0:T(8,128)S(1)}, u32[]{:S(2)}) copy-start(f32[96,768]{1,0:T(8,128)S(1)} %get-tuple-element.155) | copy-start | bytes 884740
  441.8 53.0 %copy-start.22 = (f32[768,96]{0,1:T(8,128)}, f32[768,96]{0,1:T(8,128)S(1)}, u32[]{:S(2)}) copy-start(f32[768,96]{0,1:T(8,128)S(1)} %get-tuple-element.152) | copy-start | bytes 884740
  (3 other events, 6.5 us)
Sparse Core Ops, SparseCore 0:
  352.7 37.0 all-gather.2

commit v2 on v1

--- a/solution.py
+++ b/solution.py
@@ -384,8 +384,225 @@
     )(own)
 
 
-def gelu_tanh(values):
-    return jax.nn.gelu(values, approximate=True)
+def image_kernel(
+    images, cuts, x_ref, c_ref, x_old_ref, c_old_ref, w1_ref, w2_ref, gain_ref,
+    out_ref, grad_in_ref, g1_ref, g2_ref, g_gain_ref,
+    acc1, acc2, qkv, back_cols, front_cols, partial, pair_in, chip_sum, line_in, total,
+    s1, r1, s2, r2, s3, r3,
+):
+    step = pl.program_id(0)
+    rank = lax.axis_index("tensor")
+    core = rank % 2
+    sibling = {"tensor": rank + 1 - 2 * core}
+    across = {"tensor": lax.rem(rank + 2, 4)}
+    width, head_cols = cuts
+    heads = head_cols // HEAD_DIM
+    rows, model = x_ref.shape[1], x_ref.shape[2]
+    half = model // 2
+    f32, b16 = jnp.float32, jnp.bfloat16
+
+    @pl.when(step == 0)
+    def _():
+        barrier = pltpu.get_barrier_semaphore()
+        pl.semaphore_signal(barrier, inc=1, device_id=sibling, device_id_type=MESH)
+        pl.semaphore_signal(barrier, inc=1, device_id=across, device_id_type=MESH)
+        pl.semaphore_wait(barrier, 2)
+        acc1[...] = jnp.zeros_like(acc1)
+        acc2[...] = jnp.zeros_like(acc2)
+        g_gain_ref[...] = jnp.zeros_like(g_gain_ref)
+
+    def move(source, target, sends, recvs, slot, peer):
+        return pltpu.make_async_remote_copy(
+            src_ref=source,
+            dst_ref=target,
+            send_sem=sends.at[slot],
+            recv_sem=recvs.at[slot],
+            device_id=peer,
+            device_id_type=MESH,
+        )
+
+    def first(slot):
+        return move(partial.at[slot, 1 - core], pair_in.at[slot], s1, r1, slot, sibling)
+
+    def second(slot):
+        return move(chip_sum.at[slot], line_in.at[slot], s2, r2, slot, across)
+
+    def third(slot):
+        return move(total.at[slot, core], total.at[slot, core], s3, r3, slot, sibling)
+
+    def normalised(values):
+        floats = values.astype(f32)
+        centred = floats - jnp.mean(floats, axis=1, keepdims=True)
+        inv_std = lax.rsqrt(jnp.mean(centred * centred, axis=1, keepdims=True) + norm_eps)
+        return floats, centred * inv_std, inv_std
+
+    gain = gain_ref[...].astype(f32)
+
+    @pl.when(step >= 3)
+    def _():
+        slot = (step - 3) % 2
+        third(slot).wait()
+        floats, unit, inv_std = normalised(x_old_ref[0])
+        sums = jnp.concatenate([total[slot, 0, 0], total[slot, 1, 0]], axis=1).astype(f32)
+        out_ref[0] = (floats + sums).astype(b16)
+        d_normed = jnp.concatenate([total[slot, 0, 1], total[slot, 1, 1]], axis=1).astype(f32)
+        weighted = d_normed * unit
+        g_gain_ref[...] += jnp.sum(weighted, axis=0, keepdims=True)
+        d_unit = d_normed * gain
+        d_floats = inv_std * (
+            d_unit
+            - jnp.mean(d_unit, axis=1, keepdims=True)
+            - unit * jnp.mean(weighted * gain, axis=1, keepdims=True)
+        )
+        grad_in_ref[0] = (c_old_ref[0].astype(f32) + d_floats).astype(b16)
+
+    @pl.when(jnp.logical_and(step >= 2, step < images + 2))
+    def _():
+        slot = (step - 2) % 2
+        second(slot).wait()
+        total[slot, core] = (chip_sum[slot].astype(f32) + line_in[slot].astype(f32)).astype(b16)
+        third(slot).start()
+
+    @pl.when(jnp.logical_and(step >= 1, step < images + 1))
+    def _():
+        slot = (step - 1) % 2
+        first(slot).wait()
+        chip_sum[slot] = (partial[slot, core].astype(f32) + pair_in[slot].astype(f32)).astype(b16)
+        second(slot).start()
+
+    @pl.when(step < images)
+    def _():
+        slot = step % 2
+        _floats, unit, _inv = normalised(x_ref[0])
+        normed = (unit * gain).astype(b16)
+        cot = c_ref[0]
+
+        def mm(a, b):
+            return jnp.dot(a, b, preferred_element_type=f32)
+
+        def mm_nt(a, b):
+            return lax.dot_general(a, b, (((1,), (1,)), ((), ())), preferred_element_type=f32)
+
+        def mm_tn(a, b):
+            return lax.dot_general(a, b, (((0,), (0,)), ((), ())), preferred_element_type=f32)
+
+        qkv[:, : 3 * head_cols] = mm(normed, w1_ref[:, width:]).astype(b16)
+        qkv[:, 3 * head_cols :] = mm(cot, w2_ref[:, width:]).astype(b16)
+        keys_wide = pl.cdiv(rows, 128) * 128
+        filler = jnp.zeros((keys_wide - rows, HEAD_DIM), b16)
+        real = lax.broadcasted_iota(jnp.int32, (rows, keys_wide), 1) < SEQ
+        for head in range(heads):
+            def part(kind):
+                at = kind * head_cols + head * HEAD_DIM
+                return qkv[:, at : at + HEAD_DIM]
+
+            query = part(0) * jnp.asarray(HEAD_DIM ** (-0.5), b16)
+            key = jnp.concatenate([part(1), filler], axis=0)
+            value = jnp.concatenate([part(2), filler], axis=0)
+            d_att = part(3)
+            scores = jnp.where(real, mm_nt(query, key), -1e30)
+            powers = jnp.exp(scores - jnp.max(scores, axis=1, keepdims=True))
+            probs = powers * (1.0 / jnp.sum(powers, axis=1, keepdims=True))
+            probs_low = probs.astype(b16)
+            spot = head * HEAD_DIM
+            front_cols[:, width + spot : width + spot + HEAD_DIM] = mm(probs_low, value).astype(b16)
+            d_probs = mm_nt(d_att, value)
+            d_value = mm_tn(probs_low, d_att)[:rows].astype(b16)
+            inner = jnp.sum(probs * d_probs, axis=1, keepdims=True)
+            d_scores = (probs * (d_probs - inner)).astype(b16)
+            d_query = (mm(d_scores, key) * (HEAD_DIM ** (-0.5))).astype(b16)
+            d_key = mm_tn(d_scores, query)[:rows].astype(b16)
+            for kind, value_of in ((0, d_query), (1, d_key), (2, d_value)):
+                at = width + kind * head_cols + spot
+                back_cols[:, at : at + HEAD_DIM] = value_of
+
+        upper = mm(normed, w1_ref[:, :width])
+        d_hidden = mm(cot, w2_ref[:, :width])
+        scale = (2.0 / 3.141592653589793) ** 0.5
+        square = upper * upper
+        bend = jnp.tanh(scale * upper * (1.0 + 0.044715 * square))
+        step_up = 0.5 * (1.0 + bend)
+        front_cols[:, :width] = (upper * step_up).astype(b16)
+        slope = step_up + (0.5 * scale) * upper * (1.0 - bend * bend) * (
+            1.0 + (3.0 * 0.044715) * square
+        )
+        back_cols[:, :width] = (d_hidden * slope).astype(b16)
+
+        out_part = mm_nt(front_cols[...], w2_ref[...]).astype(b16)
+        partial[slot, 0, 0] = out_part[:, :half]
+        partial[slot, 1, 0] = out_part[:, half:]
+        back_part = mm_nt(back_cols[...], w1_ref[...]).astype(b16)
+        partial[slot, 0, 1] = back_part[:, :half]
+        partial[slot, 1, 1] = back_part[:, half:]
+        first(slot).start()
+        acc1[...] += mm_tn(normed, back_cols[...])
+        acc2[...] += mm_tn(cot, front_cols[...])
+
+    @pl.when(step == images - 1)
+    def _():
+        g1_ref[...] = acc1[...].astype(b16)
+        g2_ref[...] = acc2[...].astype(b16)
+
+
+def image_block(inputs, cotangent, w1, w2, gain, width, head_cols):
+    images, rows, model = inputs.shape
+    half = model // 2
+    now = lambda i: (jnp.minimum(i, images - 1), 0, 0)
+    old = lambda i: (jnp.maximum(i - 3, 0), 0, 0)
+    fixed = lambda i: (0, 0)
+    block = (1, rows, model)
+
+    def whole(shape):
+        return pl.BlockSpec(shape, fixed, pipeline_mode=pl.Buffered(1))
+
+    bf = jnp.bfloat16
+    return pl.pallas_call(
+        functools.partial(image_kernel, images, (width, head_cols)),
+        grid=(images + 3,),
+        out_shape=(
+            jax.ShapeDtypeStruct(inputs.shape, bf),
+            jax.ShapeDtypeStruct(inputs.shape, bf),
+            jax.ShapeDtypeStruct(w1.shape, bf),
+            jax.ShapeDtypeStruct(w2.shape, bf),
+            jax.ShapeDtypeStruct((1, model), jnp.float32),
+        ),
+        in_specs=[
+            pl.BlockSpec(block, now),
+            pl.BlockSpec(block, now),
+            pl.BlockSpec(block, old),
+            pl.BlockSpec(block, old),
+            whole(w1.shape),
+            whole(w2.shape),
+            whole((1, model)),
+        ],
+        out_specs=[
+            pl.BlockSpec(block, old),
+            pl.BlockSpec(block, old),
+            whole(w1.shape),
+            whole(w2.shape),
+            whole((1, model)),
+        ],
+        scratch_shapes=[
+            pltpu.VMEM(w1.shape, jnp.float32),
+            pltpu.VMEM(w2.shape, jnp.float32),
+            pltpu.VMEM((rows, 4 * head_cols), bf),
+            pltpu.VMEM((rows, w1.shape[1]), bf),
+            pltpu.VMEM((rows, w2.shape[1]), bf),
+            pltpu.VMEM((2, 2, 2, rows, half), bf),
+            pltpu.VMEM((2, 2, rows, half), bf),
+            pltpu.VMEM((2, 2, rows, half), bf),
+            pltpu.VMEM((2, 2, rows, half), bf),
+            pltpu.VMEM((2, 2, 2, rows, half), bf),
+        ]
+        + [pltpu.SemaphoreType.DMA((2,))] * 6,
+        compiler_params=pltpu.CompilerParams(
+            collective_id=4,
+            has_side_effects=True,
+            vmem_limit_bytes=60 * 2**20,
+            dimension_semantics=("arbitrary",),
+        ),
+        name="image_block",
+    )(inputs, cotangent, inputs, cotangent, w1, w2, gain)
 
 
 def local(
@@ -411,141 +628,57 @@
     hidden_here = master_widening.shape[1]
     head_cols = master_inward.shape[2]
     model = inputs.shape[1]
-    cuts = (hidden_here, 2 * hidden_here, 2 * hidden_here + 3 * head_cols)
+    cuts = (hidden_here, hidden_here + 3 * head_cols, 2 * hidden_here + 3 * head_cols)
     width = cuts[2] + head_cols
     gain_cols = 128 + (-width) % 128
     shard = jnp.concatenate(
         [
             master_widening,
+            jnp.transpose(master_inward, (1, 0, 2)).reshape(depth, 3 * head_cols),
             master_narrowing.T,
-            jnp.transpose(master_inward, (1, 0, 2)).reshape(depth, 3 * head_cols),
             master_outward.T,
             jnp.broadcast_to(master_scaling[:, None], (depth, gain_cols)),
         ],
         axis=1,
     ).astype(jnp.bfloat16)
     copies = gather_blocks(shard).reshape(model, width + gain_cols)
-    widening = copies[:, : cuts[0]]
-    narrowing_t = copies[:, cuts[0] : cuts[1]]
-    inward = copies[:, cuts[1] : cuts[2]]
-    outward_t = copies[:, cuts[2] : width]
-    scaling = copies[:, width]
-    floats_in = inputs.astype(jnp.float32)
-    rows_here = floats_in.shape[0]
+    wide_cut = hidden_here + 3 * head_cols
+    rows_here = inputs.shape[0]
     images = rows_here // SEQ
-    heads_here = head_cols // HEAD_DIM
-    factor = HEAD_DIM ** (-0.5)
-    centred = floats_in - jnp.mean(floats_in, axis=1, keepdims=True)
-    inv_std = lax.rsqrt(jnp.mean(centred * centred, axis=1, keepdims=True) + norm_eps)
-    unit_rows = centred * inv_std
-    gain_rows = scaling.astype(jnp.float32)
-    normed = (unit_rows * gain_rows).astype(jnp.bfloat16)
-    projected = jnp.dot(normed, inward, preferred_element_type=jnp.float32).astype(jnp.bfloat16)
-    query_rows, key_rows, value_rows = (
-        projected[:, i * head_cols : (i + 1) * head_cols].reshape(
-            images, SEQ, heads_here, HEAD_DIM
-        )
-        for i in range(3)
-    )
-    scores = (
-        jnp.einsum("bqhd,bkhd->bhqk", query_rows, key_rows, preferred_element_type=jnp.float32)
-        * factor
-    )
-    peak = jnp.max(scores, axis=-1, keepdims=True)
-    log_total = peak + jnp.log(jnp.sum(jnp.exp(scores - peak), axis=-1, keepdims=True))
-    probs_low = jnp.exp(scores - log_total).astype(jnp.bfloat16)
-    attended = jnp.einsum(
-        "bhqk,bkhd->bqhd", probs_low, value_rows, preferred_element_type=jnp.float32
-    )
-    attended = attended.astype(jnp.bfloat16).reshape(rows_here, heads_here * HEAD_DIM)
-    upper = jnp.dot(normed, widening, preferred_element_type=jnp.float32)
-    hidden = gelu_tanh(upper).astype(jnp.bfloat16)
-    partial_sum = jnp.einsum(
-        "re,de->rd", attended, outward_t, preferred_element_type=jnp.float32
-    ) + jnp.einsum("rf,df->rd", hidden, narrowing_t, preferred_element_type=jnp.float32)
+    padded = -(-SEQ // 16) * 16
+
+    def by_image(values):
+        return jnp.pad(
+            values.reshape(images, SEQ, model), ((0, 0), (0, padded - SEQ), (0, 0))
+        )
+
+    summed_out, input_grad, grads_one, grads_two, grad_scaling = image_block(
+        by_image(inputs),
+        by_image(cotangent),
+        copies[:, :wide_cut],
+        copies[:, wide_cut:width],
+        copies[:, width].reshape(1, model),
+        hidden_here,
+        head_cols,
+    )
     share = rows_here // lax.axis_size("tensor")
     start = lax.axis_index("tensor") * share
-    total = lax.psum_scatter(
-        partial_sum.astype(jnp.bfloat16), "tensor", scatter_dimension=0, tiled=True
-    )
-    inputs_mine = lax.dynamic_slice_in_dim(inputs, start, share, 0).astype(jnp.float32)
-    output = (inputs_mine + total.astype(jnp.float32)).astype(jnp.bfloat16)
-    d_attended = jnp.dot(cotangent, outward_t, preferred_element_type=jnp.float32).astype(
-        jnp.bfloat16
-    )
-    d_hidden = jnp.dot(cotangent, narrowing_t, preferred_element_type=jnp.float32)
-    gelu_value, gelu_pull = jax.vjp(gelu_tanh, upper)
-    d_upper = gelu_pull(d_hidden)[0].astype(jnp.bfloat16)
-    back_sum = jnp.einsum("rf,df->rd", d_upper, widening, preferred_element_type=jnp.float32)
-    d_att_blocks = d_attended.reshape(images, SEQ, heads_here, HEAD_DIM)
-    rescored = (
-        jnp.einsum("bqhd,bkhd->bhqk", query_rows, key_rows, preferred_element_type=jnp.float32)
-        * factor
-    )
-    probs_full = jnp.exp(rescored - log_total)
-    probs_again = probs_full.astype(jnp.bfloat16)
-    d_probs = jnp.einsum(
-        "bqhd,bkhd->bhqk", d_att_blocks, value_rows, preferred_element_type=jnp.float32
-    )
-    d_value = jnp.einsum(
-        "bhqk,bqhd->bkhd", probs_again, d_att_blocks, preferred_element_type=jnp.float32
-    ).astype(jnp.bfloat16)
-    inner = jnp.sum(probs_full * d_probs, axis=-1, keepdims=True)
-    d_scores = (probs_full * (d_probs - inner)).astype(jnp.bfloat16)
-    d_query = (
-        jnp.einsum("bhqk,bkhd->bqhd", d_scores, key_rows, preferred_element_type=jnp.float32)
-        * factor
-    ).astype(jnp.bfloat16)
-    d_key = (
-        jnp.einsum("bhqk,bqhd->bkhd", d_scores, query_rows, preferred_element_type=jnp.float32)
-        * factor
-    ).astype(jnp.bfloat16)
-    d_projected = jnp.concatenate(
-        [d.reshape(rows_here, head_cols) for d in (d_query, d_key, d_value)], axis=1
-    )
-    back_sum = back_sum + jnp.einsum(
-        "re,de->rd", d_projected, inward, preferred_element_type=jnp.float32
-    )
-    d_normed = lax.psum_scatter(
-        back_sum.astype(jnp.bfloat16), "tensor", scatter_dimension=0, tiled=True
-    ).astype(jnp.float32)
-
-    def weight_grad(rows, columns):
-        return jnp.einsum("rd,rf->df", rows, columns, preferred_element_type=jnp.float32)
-
-    grads = jnp.concatenate(
-        [
-            weight_grad(normed, d_upper).astype(jnp.bfloat16),
-            weight_grad(cotangent, hidden).astype(jnp.bfloat16),
-            weight_grad(normed, d_projected).astype(jnp.bfloat16),
-            weight_grad(cotangent, attended).astype(jnp.bfloat16),
-        ],
-        axis=1,
-    )
-    centred_mine = inputs_mine - jnp.mean(inputs_mine, axis=1, keepdims=True)
-    inv_mine = lax.rsqrt(jnp.mean(centred_mine * centred_mine, axis=1, keepdims=True) + norm_eps)
-    unit_mine = centred_mine * inv_mine
-    grad_scaling = jnp.sum(d_normed * unit_mine, axis=0)
-    d_unit = d_normed * gain_rows
-    d_floats = inv_mine * (
-        d_unit
-        - jnp.mean(d_unit, axis=1, keepdims=True)
-        - unit_mine * jnp.mean(d_unit * unit_mine, axis=1, keepdims=True)
-    )
-    cotangent_mine = lax.dynamic_slice_in_dim(cotangent, start, share, 0).astype(jnp.float32)
-    input_grad = lax.all_gather(
-        (cotangent_mine + d_floats).astype(jnp.bfloat16), "tensor", axis=0, tiled=True
-    )
+    output = lax.dynamic_slice_in_dim(
+        summed_out[:, :SEQ].reshape(rows_here, model), start, share, 0
+    )
+    input_grad = input_grad[:, :SEQ].reshape(rows_here, model)
+    grads = jnp.concatenate([grads_one, grads_two], axis=1)
+    grad_scaling = grad_scaling * (1.0 / lax.axis_size("tensor"))
     grad_scaling = total_of(grad_scaling.reshape(-1, 128), 2).reshape(-1)
     grad_scaling = lax.dynamic_slice_in_dim(
         grad_scaling, lax.axis_index("dp") * depth, depth, 0
     )
     summed = reduce_blocks(grads.reshape(lax.axis_size("dp"), depth, width))
     grad_widening = summed[:, : cuts[0]]
-    grad_narrowing = summed[:, cuts[0] : cuts[1]].T
     grad_inward = jnp.transpose(
-        summed[:, cuts[1] : cuts[2]].reshape(depth, 3, head_cols), (1, 0, 2)
-    )
+        summed[:, cuts[0] : cuts[1]].reshape(depth, 3, head_cols), (1, 0, 2)
+    )
+    grad_narrowing = summed[:, cuts[1] : cuts[2]].T
     grad_outward = summed[:, cuts[2] :].T
     part_in = lamb_parts(master_inward, first_inward, second_inward, grad_inward)
     part_out = lamb_parts(master_outward, first_outward, second_outward, grad_outward)

time: 510 us -> 369 us (0.72); the launches traced: 502 us -> 368 us
  Pallas kernels: 112 us -> 257 us
  matrix products: 124 us -> 0 us
  blocking collectives: 90.4 us -> 0 us
  other arithmetic: 57.6 us -> 26.5 us
  between operations: 22.4 us -> 7.64 us
  local copies, waits for them, and re-layouts: 90.6 us -> 76.8 us
    pallas_call x0 -> x1, Pallas kernels: none -> 143 us  [image_block(): pl.pallas_call(functools.partial(image_kernel, images, (width, head_cols)...]
    dot_general x18 -> x0, matrix products: 124 us -> none  [the longest x4 26.6 us: weight_grad(): jnp.einsum('rd,rf->df', rows, columns, preferred_element_type=jnp.float32)]
    unnamed x1 -> x0, blocking collectives: 90.4 us -> none
    unnamed x120 -> x43, local copies, waits for them, and re-layouts: 40.5 us -> 10.6 us
    reduce_sum x6 -> x0, other arithmetic: 17.4 us -> none  [the longest x1 4.06 us: local(): jnp.mean(centred * centred, axis=1, keepdims=True) + norm_eps]
    slice x4 -> x7, local copies, waits for them, and re-layouts: 3.13 us -> 18 us  [the longest x1 5.16 us: local(): summed_out[:, :SEQ].reshape(rows_here, model)]
    pad x0 -> x2, local copies, waits for them, and re-layouts: none -> 10.3 us  [by_image(): jnp.pad(values.reshape(images, SEQ, model), ((0, 0), (0, padded - SEQ), (...]
    convert_element_type x4 -> x0, local copies, waits for them, and re-layouts: 8.36 us -> none  [the longest x1 2.45 us: local(): d_query = (jnp.einsum('bhqk,bkhd->bqhd', d_scores, key_rows, preferred_el...]
  transfers between devices with their start and end apart: 3 -> 0, of which waited for: 0 -> 0; matrix products, arithmetic and copies ran while one was open for 17% -> 0% of each run, Pallas kernels for 13% -> 0%
where the time goes in v2:
time: 369 us; the launch traced here: 368 us
  Pallas kernels  257 us (70%)
  local copies, waits for them, and re-layouts  76.8 us (21%)
  other arithmetic  26.5 us (7%)
  between operations  7.64 us (2%)
    pallas_call x1, Pallas kernels, image_block(): pl.pallas_call(functools.partial(image_kernel, images, (width, head_cols)...  143 us
    pallas_call x1, Pallas kernels, gather_blocks(): pl.pallas_call(functools.partial(gather_kernel, line), out_shape=jax.Shap...  49.2 us
    pallas_call x1, Pallas kernels, reduce_blocks(): pl.pallas_call(functools.partial(reduce_kernel, line), out_shape=jax.Shap...  43.4 us
    pallas_call x2, Pallas kernels, total_of(): pl.pallas_call(functools.partial(total_kernel, devices, ranks), out_shape...  20.8 us
    reshape x2, local copies, waits for them, and re-layouts, by_image(): values.reshape(images, SEQ, model)  15.7 us
    unnamed x43, local copies, waits for them, and re-layouts  10.6 us
    pad x2, local copies, waits for them, and re-layouts, by_image(): jnp.pad(values.reshape(images, SEQ, model), ((0, 0), (0, padded - SEQ), (...  10.3 us
    reshape x1, local copies, waits for them, and re-layouts, local(): summed_out[:, :SEQ].reshape(rows_here, model)  7.8 us

profile of v2, /device:TPU:0, one launch (start us, length us, event | category | flops | bytes accessed | tf_op | source)
XLA Modules:
  0.0 367.6 jit_solution(13168425916643376916)
XLA Ops:
  0.7 1.0 copy.100
  1.7 1.8 multiply_reduce_fusion.5
  3.7 1.3 multiply_reduce_fusion.10
  5.2 1.0 convert.20
  6.1 1.0 convert_bitcast_fusion
  7.1 1.0 concatenate.16.own_ref
  8.1 49.2 %gather_blocks.1 = bf16[8,96,2432]{2,1,0:T(8,128)(2,1)} custom-call(bf16[96,2432]{1,0:T(8,128)(2,1)} %concatenate.16.own_ref), custom_call_target="tpu_custom_call" | custom-call | bytes 100000000 | tf_op jit(solution)/shard_map/gather_blocks/pallas_call | solution.py:134
  57.3 3.1 slice.100.w1_ref
  60.4 3.4 slice.101.w2_ref
  63.7 1.1 slice_reduce_fusion
  65.4 7.8 %reshape.155 = bf16[17,196,768]{2,1,0:T(8,128)(2,1)} reshape(bf16[3332,768]{1,0:T(8,128)(2,1)} %param.19) | data formatting | bytes 10235904 | tf_op jit(solution)/shard_map/reshape | solution.py:652
  73.2 5.2 %pad.13.x_ref.x_old_ref = bf16[17,208,768]{2,1,0:T(8,128)(2,1)} pad(bf16[17,196,768]{2,1,0:T(8,128)(2,1)} %reshape.155, bf16[]{:T(256)} %constant.77.clone.1), padding=0_0x0_12x0_0 | pad | bytes 10549250 | tf_op jit(solution)/shard_map/jit(_pad)/pad | solution.py:651
  78.4 7.8 %reshape.156 = bf16[17,196,768]{2,1,0:T(8,128)(2,1)} reshape(bf16[3332,768]{1,0:T(8,128)(2,1)} %param.20) | data formatting | bytes 10235904 | tf_op jit(solution)/shard_map/reshape | solution.py:652
  86.3 5.2 %pad.14.c_ref.c_old_ref = bf16[17,208,768]{2,1,0:T(8,128)(2,1)} pad(bf16[17,196,768]{2,1,0:T(8,128)(2,1)} %reshape.156, bf16[]{:T(256)} %constant.77.clone.1), padding=0_0x0_12x0_0 | pad | bytes 10549250 | tf_op jit(solution)/shard_map/jit(_pad)/pad | solution.py:651
  91.4 143.2 %image_block.1 = (bf16[17,208,768]{2,1,0:T(8,128)(2,1)}, bf16[17,208,768]{2,1,0:T(8,128)(2,1)}, bf16[768,1344]{1,0:T(8,128)(2,1)}, bf16[768,960]{1,0:T(8,128)(2,1)}, f32[1,768]{1,0:T(1,128)}) custom-call(bf16[17,208,768]{2,1,0:T(8,128)(2,1)} %pad.13.x_ref.x_old_ref, bf16[17,208,768]{2,1,0:T(8,128)(2,1)} %pad.14.c_ref.c_old_ref, ...), custom_call_target="tpu_custom_call" | custom-call | tf_op jit(solution)/shard_map/image_block/pallas_call | solution.py:559
  234.7 3.1 pad_maximum_fusion
  237.9 43.4 %reduce_blocks.1 = f32[96,2304]{1,0:T(8,128)S(1)} custom-call(bf16[8,96,2304]{2,1,0:T(8,128)(2,1)S(1)} %bitcast.47), custom_call_target="tpu_custom_call" | custom-call | bytes 100000000 | tf_op jit(solution)/shard_map/reduce_blocks/pallas_call | solution.py:271
  281.3 0.9 multiply_reduce_fusion.3
  282.3 1.6 multiply_reduce_fusion.1
  283.9 2.7 maximum_bitcast_fusion.2
  286.7 0.8 multiply_reduce_fusion.6
  287.8 1.1 copy.102
  288.9 1.1 copy.104
  290.1 0.8 multiply_reduce_fusion.4
  290.9 1.5 multiply_reduce_fusion.7
  292.4 2.7 maximum_bitcast_fusion
  295.1 0.6 multiply_reduce_fusion.8
  295.7 9.9 %total_2.1 = f32[6,128]{1,0:T(8,128)} custom-call(f32[6,128]{1,0:T(8,128)} %bitcast.53), custom_call_target="tpu_custom_call" | custom-call | bytes 20000000 | tf_op jit(solution)/shard_map/total_2/pallas_call | solution.py:365
  305.6 1.9 multiply_reduce_fusion.9
  307.4 1.4 maximum_multiply_fusion
  309.4 10.9 %total_3.1 = f32[8,128]{1,0:T(8,128)} custom-call(f32[8,128]{1,0:T(8,128)} %scatter.4.own_ref), custom_call_target="tpu_custom_call" | custom-call | bytes 20000000 | tf_op jit(solution)/shard_map/total_3/pallas_call | solution.py:365
  320.4 0.7 slice_sqrt_fusion
  324.9 1.9 fusion.6
  328.1 0.9 fusion.7
  330.5 0.7 copy.117
  331.2 0.7 copy.118
  333.5 0.9 copy.113
  334.3 0.8 copy.114
  335.1 0.6 copy.119
  335.8 0.7 copy.115
  336.5 0.7 copy.116
  337.3 0.9 copy.111
  338.1 0.9 copy.112
  339.0 5.2 %slice.83 = bf16[17,196,768]{2,1,0:T(8,128)(2,1)} slice(bf16[17,208,768]{2,1,0:T(8,128)(2,1)} %get-tuple-element.40), slice={[0:17], [0:196], [0:768]} | slice | bytes 10235904 | tf_op jit(solution)/shard_map/slice | solution.py:667
  344.2 7.8 %reshape.159 = bf16[3332,768]{1,0:T(8,128)(2,1)} reshape(bf16[17,196,768]{2,1,0:T(8,128)(2,1)} %slice.83) | data formatting | bytes 10235904 | tf_op jit(solution)/shard_map/reshape | solution.py:667
  352.0 2.7 constant_dynamic-slice_fusion
  354.6 5.1 %slice.84 = bf16[17,196,768]{2,1,0:T(8,128)(2,1)} slice(bf16[17,208,768]{2,1,0:T(8,128)(2,1)} %get-tuple-element.41), slice={[0:17], [0:196], [0:768]} | slice | bytes 10235904 | tf_op jit(solution)/shard_map/slice | solution.py:669
  359.8 7.8 %reshape.160 = bf16[3332,768]{1,0:T(8,128)(2,1)} reshape(bf16[17,196,768]{2,1,0:T(8,128)(2,1)} %slice.84) | data formatting | bytes 10235904 | tf_op jit(solution)/shard_map/reshape | solution.py:669
  (44 shorter events, 3.5 us)
Async XLA Ops:
  234.7 46.6 %copy-start.1 = (f32[96,768]{1,0:T(8,128)S(1)}, f32[96,768]{1,0:T(8,128)}, u32[]{:S(2)}) copy-start(f32[96,768]{1,0:T(8,128)} %param.27) | copy-start | bytes 884740
  234.7 46.6 %copy-start.6 = (f32[96,768]{1,0:T(8,128)S(1)}, f32[96,768]{1,0:T(8,128)}, u32[]{:S(2)}) copy-start(f32[96,768]{1,0:T(8,128)} %param.28) | copy-start | bytes 884740
  234.7 46.6 %copy-start.7 = (f32[96,768]{1,0:T(8,128)S(1)}, f32[96,768]{1,0:T(8,128)}, u32[]{:S(2)}) copy-start(f32[96,768]{1,0:T(8,128)} %param.29) | copy-start | bytes 884740
  234.7 47.5 %copy-start = (f32[768,96]{0,1:T(8,128)S(1)}, f32[768,96]{0,1:T(8,128)}, u32[]{:S(2)}) copy-start(f32[768,96]{0,1:T(8,128)} %param.30) | copy-start | bytes 884740
  234.7 47.5 %copy-start.8 = (f32[768,96]{0,1:T(8,128)S(1)}, f32[768,96]{0,1:T(8,128)}, u32[]{:S(2)}) copy-start(f32[768,96]{0,1:T(8,128)} %param.31) | copy-start | bytes 884740
  234.7 47.5 %copy-start.9 = (f32[768,96]{0,1:T(8,128)S(1)}, f32[768,96]{0,1:T(8,128)}, u32[]{:S(2)}) copy-start(f32[768,96]{0,1:T(8,128)} %param.32) | copy-start | bytes 884740
  237.8 48.7 %copy-start.10 = (f32[192,96]{1,0:T(8,128)S(1)}, f32[192,96]{1,0:T(8,128)}, u32[]{:S(2)}) copy-start(f32[192,96]{1,0:T(8,128)} %param.25) | copy-start | bytes 221188
  237.8 48.8 %copy-start.11 = (f32[192,96]{1,0:T(8,128)S(1)}, f32[192,96]{1,0:T(8,128)}, u32[]{:S(2)}) copy-start(f32[192,96]{1,0:T(8,128)} %param.26) | copy-start | bytes 221188
  237.8 49.8 %copy-start.2 = (f32[3,96,192]{2,1,0:T(8,128)S(1)}, f32[3,96,192]{2,1,0:T(8,128)}, u32[]{:S(2)}) copy-start(f32[3,96,192]{2,1,0:T(8,128)} %param.21) | copy-start | bytes 663556
  281.3 13.8 %copy-start.12 = (f32[1,768]{1,0:T(1,128)S(1)}, f32[1,768]{1,0:T(1,128)}, u32[]{:S(2)}) copy-start(f32[1,768]{1,0:T(1,128)} %get-tuple-element.44) | copy-start | bytes 9220
  281.3 24.2 %copy-start.13 = (f32[96]{0:T(128)S(1)}, f32[96]{0:T(128)}, u32[]{:S(2)}) copy-start(f32[96]{0:T(128)} %param.33) | copy-start | bytes 1156
  282.2 46.8 %copy-start.3 = (f32[96,768]{1,0:T(8,128)}, f32[96,768]{1,0:T(8,128)S(1)}, u32[]{:S(2)}) copy-start(f32[96,768]{1,0:T(8,128)S(1)} %get-tuple-element.157) | copy-start | bytes 884740
  282.3 46.8 %copy-start.4 = (f32[96,768]{1,0:T(8,128)}, f32[96,768]{1,0:T(8,128)S(1)}, u32[]{:S(2)}) copy-start(f32[96,768]{1,0:T(8,128)S(1)} %get-tuple-element.158) | copy-start | bytes 884740
  283.9 49.6 %copy-start.5 = (f32[768,96]{0,1:T(8,128)}, f32[768,96]{0,1:T(8,128)S(1)}, u32[]{:S(2)}) copy-start(f32[768,96]{0,1:T(8,128)S(1)} %get-tuple-element.155) | copy-start | bytes 884740

commit v3 on v2

--- a/solution.py
+++ b/solution.py
@@ -384,11 +384,15 @@
     )(own)
 
 
+WINDOW = 224
+
+
 def image_kernel(
-    images, cuts, x_ref, c_ref, x_old_ref, c_old_ref, w1_ref, w2_ref, gain_ref,
-    out_ref, grad_in_ref, g1_ref, g2_ref, g_gain_ref,
-    acc1, acc2, qkv, back_cols, front_cols, partial, pair_in, chip_sum, line_in, total,
-    s1, r1, s2, r2, s3, r3,
+    images, cuts, x_hbm, c_hbm, tail_ref, w_ref,
+    out_ref, grad_in_ref, g_ref,
+    acc1, acc2, gain_row, g_gain, windows, kept, qkv, back_cols, front_cols,
+    partial, pair_in, chip_sum, line_in, total,
+    in_sem, s1, r1, s2, r2, s3, r3,
 ):
     step = pl.program_id(0)
     rank = lax.axis_index("tensor")
@@ -397,9 +401,28 @@
     across = {"tensor": lax.rem(rank + 2, 4)}
     width, head_cols = cuts
     heads = head_cols // HEAD_DIM
-    rows, model = x_ref.shape[1], x_ref.shape[2]
+    rows, model = kept.shape[2], kept.shape[3]
     half = model // 2
     f32, b16 = jnp.float32, jnp.bfloat16
+    back_width, front_width = back_cols.shape[1], front_cols.shape[1]
+    last_window = images * SEQ // 16 * 16 - WINDOW
+
+    def window_start(image):
+        return pl.multiple_of(jnp.minimum(image * SEQ // 16 * 16, last_window), 16)
+
+    def fetches(image, slot):
+        return [
+            pltpu.make_async_copy(
+                source.at[pl.ds(window_start(image), WINDOW)],
+                windows.at[slot, kind, pl.ds(0, WINDOW)],
+                in_sem.at[slot, kind],
+            )
+            for kind, source in ((0, x_hbm), (1, c_hbm))
+        ]
+
+    def one_hot(shape, row_is):
+        at = [lax.broadcasted_iota(jnp.int32, shape, axis) for axis in (0, 1)]
+        return jnp.where(row_is(*at), 1.0, 0.0).astype(b16)
 
     @pl.when(step == 0)
     def _():
@@ -407,9 +430,25 @@
         pl.semaphore_signal(barrier, inc=1, device_id=sibling, device_id_type=MESH)
         pl.semaphore_signal(barrier, inc=1, device_id=across, device_id_type=MESH)
         pl.semaphore_wait(barrier, 2)
+        for copy in fetches(0, 0):
+            copy.start()
+        for slot in range(2):
+            for kind in range(2):
+                windows[slot, kind, WINDOW:] = tail_ref[kind]
         acc1[...] = jnp.zeros_like(acc1)
         acc2[...] = jnp.zeros_like(acc2)
-        g_gain_ref[...] = jnp.zeros_like(g_gain_ref)
+        back_cols[...] = jnp.zeros_like(back_cols)
+        front_cols[...] = jnp.zeros_like(front_cols)
+        g_gain[...] = jnp.zeros_like(g_gain)
+        for ref in (out_ref, grad_in_ref):
+            ref[:16] = jnp.zeros((16, model), b16)
+        turned = w_ref[:, back_width + front_width - 128 :].astype(f32).T
+        gain_row[...] = turned[127:128]
+
+    @pl.when(step < images - 1)
+    def _():
+        for copy in fetches(step + 1, (step + 1) % 2):
+            copy.start()
 
     def move(source, target, sends, recvs, slot, peer):
         return pltpu.make_async_remote_copy(
@@ -436,25 +475,44 @@
         inv_std = lax.rsqrt(jnp.mean(centred * centred, axis=1, keepdims=True) + norm_eps)
         return floats, centred * inv_std, inv_std
 
-    gain = gain_ref[...].astype(f32)
+    gain = gain_row[...]
+
+    def place(ref, image, values):
+        @pl.when(image < images - 1)
+        def _():
+            start = pl.multiple_of(image * SEQ // 16 * 16, 16)
+            offset = image * SEQ - start
+            spread = one_hot(
+                (WINDOW, rows), lambda r, j: jnp.logical_and(r == j + offset, j < SEQ)
+            )
+            placed = jnp.dot(spread, values, preferred_element_type=f32)
+            before = lax.broadcasted_iota(jnp.int32, (16, model), 0) < offset
+            head = jnp.where(before, ref[pl.ds(start, 16), :].astype(f32), placed[:16])
+            ref[pl.ds(start, 16), :] = head.astype(b16)
+            ref[pl.ds(start + 16, WINDOW - 16), :] = placed[16:].astype(b16)
+
+        @pl.when(image == images - 1)
+        def _():
+            ref[(images - 1) * SEQ :] = values[:SEQ]
 
     @pl.when(step >= 3)
     def _():
         slot = (step - 3) % 2
         third(slot).wait()
-        floats, unit, inv_std = normalised(x_old_ref[0])
+        floats, unit, inv_std = normalised(kept[(step - 3) % 4, 0])
         sums = jnp.concatenate([total[slot, 0, 0], total[slot, 1, 0]], axis=1).astype(f32)
-        out_ref[0] = (floats + sums).astype(b16)
+        place(out_ref, step - 3, (floats + sums).astype(b16))
         d_normed = jnp.concatenate([total[slot, 0, 1], total[slot, 1, 1]], axis=1).astype(f32)
         weighted = d_normed * unit
-        g_gain_ref[...] += jnp.sum(weighted, axis=0, keepdims=True)
+        g_gain[...] += jnp.sum(weighted, axis=0, keepdims=True)
         d_unit = d_normed * gain
         d_floats = inv_std * (
             d_unit
             - jnp.mean(d_unit, axis=1, keepdims=True)
             - unit * jnp.mean(weighted * gain, axis=1, keepdims=True)
         )
-        grad_in_ref[0] = (c_old_ref[0].astype(f32) + d_floats).astype(b16)
+        floats_back = kept[(step - 3) % 4, 1].astype(f32) + d_floats
+        place(grad_in_ref, step - 3, floats_back.astype(b16))
 
     @pl.when(jnp.logical_and(step >= 2, step < images + 2))
     def _():
@@ -473,9 +531,19 @@
     @pl.when(step < images)
     def _():
         slot = step % 2
-        _floats, unit, _inv = normalised(x_ref[0])
+        for copy in fetches(step, slot):
+            copy.wait()
+        offset = step * SEQ - window_start(step)
+        pick = one_hot(
+            (rows, windows.shape[2]), lambda r, j: jnp.logical_and(j == r + offset, r < SEQ)
+        )
+        for kind in range(2):
+            kept[step % 4, kind] = jnp.dot(
+                pick, windows[slot, kind], preferred_element_type=f32
+            ).astype(b16)
+        _floats, unit, _inv = normalised(kept[step % 4, 0])
         normed = (unit * gain).astype(b16)
-        cot = c_ref[0]
+        cot = kept[step % 4, 1]
 
         def mm(a, b):
             return jnp.dot(a, b, preferred_element_type=f32)
@@ -486,8 +554,8 @@
         def mm_tn(a, b):
             return lax.dot_general(a, b, (((0,), (0,)), ((), ())), preferred_element_type=f32)
 
-        qkv[:, : 3 * head_cols] = mm(normed, w1_ref[:, width:]).astype(b16)
-        qkv[:, 3 * head_cols :] = mm(cot, w2_ref[:, width:]).astype(b16)
+        qkv[:, : 3 * head_cols] = mm(normed, w_ref[:, width:back_width])[:, : 3 * head_cols].astype(b16)
+        qkv[:, 3 * head_cols :] = mm(cot, w_ref[:, back_width + width :])[:, :head_cols].astype(b16)
         keys_wide = pl.cdiv(rows, 128) * 128
         filler = jnp.zeros((keys_wide - rows, HEAD_DIM), b16)
         real = lax.broadcasted_iota(jnp.int32, (rows, keys_wide), 1) < SEQ
@@ -516,8 +584,8 @@
                 at = width + kind * head_cols + spot
                 back_cols[:, at : at + HEAD_DIM] = value_of
 
-        upper = mm(normed, w1_ref[:, :width])
-        d_hidden = mm(cot, w2_ref[:, :width])
+        upper = mm(normed, w_ref[:, :width])
+        d_hidden = mm(cot, w_ref[:, back_width : back_width + width])
         scale = (2.0 / 3.141592653589793) ** 0.5
         square = upper * upper
         bend = jnp.tanh(scale * upper * (1.0 + 0.044715 * square))
@@ -528,71 +596,70 @@
         )
         back_cols[:, :width] = (d_hidden * slope).astype(b16)
 
-        out_part = mm_nt(front_cols[...], w2_ref[...]).astype(b16)
+        out_part = mm_nt(front_cols[...], w_ref[:, back_width:]).astype(b16)
         partial[slot, 0, 0] = out_part[:, :half]
         partial[slot, 1, 0] = out_part[:, half:]
-        back_part = mm_nt(back_cols[...], w1_ref[...]).astype(b16)
+        back_part = mm_nt(back_cols[...], w_ref[:, :back_width]).astype(b16)
         partial[slot, 0, 1] = back_part[:, :half]
         partial[slot, 1, 1] = back_part[:, half:]
         first(slot).start()
         acc1[...] += mm_tn(normed, back_cols[...])
         acc2[...] += mm_tn(cot, front_cols[...])
 
-    @pl.when(step == images - 1)
-    def _():
-        g1_ref[...] = acc1[...].astype(b16)
-        g2_ref[...] = acc2[...].astype(b16)
-
-
-def image_block(inputs, cotangent, w1, w2, gain, width, head_cols):
-    images, rows, model = inputs.shape
+    @pl.when(step == images + 2)
+    def _():
+        g_ref[:, :back_width] = acc1[...].astype(b16)
+        inner = back_width + front_width - 128
+        g_ref[:, back_width:inner] = acc2[:, : front_width - 128].astype(b16)
+        spare = jnp.broadcast_to(g_gain[...], (128, model)).T
+        last = lax.broadcasted_iota(jnp.int32, (model, 128), 1) == 127
+        g_ref[:, inner:] = jnp.where(last, spare, acc2[:, front_width - 128 :]).astype(b16)
+
+
+def image_block(inputs, cotangent, tails, weights, width, head_cols, back_width):
+    tokens, model = inputs.shape
+    images = tokens // SEQ
+    rows = -(-SEQ // 16) * 16
     half = model // 2
-    now = lambda i: (jnp.minimum(i, images - 1), 0, 0)
-    old = lambda i: (jnp.maximum(i - 3, 0), 0, 0)
+    front_width = weights.shape[1] - back_width
     fixed = lambda i: (0, 0)
-    block = (1, rows, model)
 
     def whole(shape):
         return pl.BlockSpec(shape, fixed, pipeline_mode=pl.Buffered(1))
 
     bf = jnp.bfloat16
+    anywhere = pl.BlockSpec(memory_space=pl.ANY)
     return pl.pallas_call(
         functools.partial(image_kernel, images, (width, head_cols)),
         grid=(images + 3,),
         out_shape=(
             jax.ShapeDtypeStruct(inputs.shape, bf),
             jax.ShapeDtypeStruct(inputs.shape, bf),
-            jax.ShapeDtypeStruct(w1.shape, bf),
-            jax.ShapeDtypeStruct(w2.shape, bf),
-            jax.ShapeDtypeStruct((1, model), jnp.float32),
+            jax.ShapeDtypeStruct(weights.shape, bf),
         ),
         in_specs=[
-            pl.BlockSpec(block, now),
-            pl.BlockSpec(block, now),
-            pl.BlockSpec(block, old),
-            pl.BlockSpec(block, old),
-            whole(w1.shape),
-            whole(w2.shape),
-            whole((1, model)),
+            anywhere,
+            anywhere,
+            pl.BlockSpec(tails.shape, lambda i: (0, 0, 0), pipeline_mode=pl.Buffered(1)),
+            whole(weights.shape),
         ],
-        out_specs=[
-            pl.BlockSpec(block, old),
-            pl.BlockSpec(block, old),
-            whole(w1.shape),
-            whole(w2.shape),
-            whole((1, model)),
-        ],
+        out_specs=[whole(inputs.shape), whole(inputs.shape), whole(weights.shape)],
         scratch_shapes=[
-            pltpu.VMEM(w1.shape, jnp.float32),
-            pltpu.VMEM(w2.shape, jnp.float32),
+            pltpu.VMEM((model, back_width), jnp.float32),
+            pltpu.VMEM((model, front_width), jnp.float32),
+            pltpu.VMEM((1, model), jnp.float32),
+            pltpu.VMEM((1, model), jnp.float32),
+            pltpu.VMEM((2, 2, WINDOW + tails.shape[1], model), bf),
+            pltpu.VMEM((4, 2, rows, model), bf),
             pltpu.VMEM((rows, 4 * head_cols), bf),
-            pltpu.VMEM((rows, w1.shape[1]), bf),
-            pltpu.VMEM((rows, w2.shape[1]), bf),
+            pltpu.VMEM((rows, back_width), bf),
+            pltpu.VMEM((rows, front_width), bf),
             pltpu.VMEM((2, 2, 2, rows, half), bf),
             pltpu.VMEM((2, 2, rows, half), bf),
             pltpu.VMEM((2, 2, rows, half), bf),
             pltpu.VMEM((2, 2, rows, half), bf),
             pltpu.VMEM((2, 2, 2, rows, half), bf),
+            pltpu.SemaphoreType.DMA((2, 2)),
         ]
         + [pltpu.SemaphoreType.DMA((2,))] * 6,
         compiler_params=pltpu.CompilerParams(
@@ -602,7 +669,7 @@
             dimension_semantics=("arbitrary",),
         ),
         name="image_block",
-    )(inputs, cotangent, inputs, cotangent, w1, w2, gain)
+    )(inputs, cotangent, tails, weights)
 
 
 def local(
@@ -628,58 +695,45 @@
     hidden_here = master_widening.shape[1]
     head_cols = master_inward.shape[2]
     model = inputs.shape[1]
-    cuts = (hidden_here, hidden_here + 3 * head_cols, 2 * hidden_here + 3 * head_cols)
-    width = cuts[2] + head_cols
-    gain_cols = 128 + (-width) % 128
+    back_width = hidden_here + 3 * head_cols
+    gap = (-back_width) % 128
+    back_width += gap
+    used = back_width + hidden_here + head_cols
+    width = -(-(used + 1) // 128) * 128
     shard = jnp.concatenate(
         [
             master_widening,
             jnp.transpose(master_inward, (1, 0, 2)).reshape(depth, 3 * head_cols),
+            jnp.zeros((depth, gap), jnp.float32),
             master_narrowing.T,
             master_outward.T,
-            jnp.broadcast_to(master_scaling[:, None], (depth, gain_cols)),
+            jnp.broadcast_to(master_scaling[:, None], (depth, width - used)),
         ],
         axis=1,
     ).astype(jnp.bfloat16)
-    copies = gather_blocks(shard).reshape(model, width + gain_cols)
-    wide_cut = hidden_here + 3 * head_cols
+    copies = gather_blocks(shard).reshape(model, width)
     rows_here = inputs.shape[0]
-    images = rows_here // SEQ
-    padded = -(-SEQ // 16) * 16
-
-    def by_image(values):
-        return jnp.pad(
-            values.reshape(images, SEQ, model), ((0, 0), (0, padded - SEQ), (0, 0))
-        )
-
-    summed_out, input_grad, grads_one, grads_two, grad_scaling = image_block(
-        by_image(inputs),
-        by_image(cotangent),
-        copies[:, :wide_cut],
-        copies[:, wide_cut:width],
-        copies[:, width].reshape(1, model),
-        hidden_here,
-        head_cols,
+    whole_rows = rows_here // 16 * 16
+    tails = jnp.stack(
+        [
+            jnp.pad(rows[whole_rows:], ((0, whole_rows + 16 - rows_here), (0, 0)))
+            for rows in (inputs, cotangent)
+        ]
+    )
+    summed_out, input_grad, grads = image_block(
+        inputs, cotangent, tails, copies, hidden_here, head_cols, back_width
     )
     share = rows_here // lax.axis_size("tensor")
     start = lax.axis_index("tensor") * share
-    output = lax.dynamic_slice_in_dim(
-        summed_out[:, :SEQ].reshape(rows_here, model), start, share, 0
-    )
-    input_grad = input_grad[:, :SEQ].reshape(rows_here, model)
-    grads = jnp.concatenate([grads_one, grads_two], axis=1)
-    grad_scaling = grad_scaling * (1.0 / lax.axis_size("tensor"))
-    grad_scaling = total_of(grad_scaling.reshape(-1, 128), 2).reshape(-1)
-    grad_scaling = lax.dynamic_slice_in_dim(
-        grad_scaling, lax.axis_index("dp") * depth, depth, 0
-    )
+    output = lax.dynamic_slice_in_dim(summed_out, start, share, 0)
     summed = reduce_blocks(grads.reshape(lax.axis_size("dp"), depth, width))
-    grad_widening = summed[:, : cuts[0]]
+    grad_widening = summed[:, :hidden_here]
     grad_inward = jnp.transpose(
-        summed[:, cuts[0] : cuts[1]].reshape(depth, 3, head_cols), (1, 0, 2)
-    )
-    grad_narrowing = summed[:, cuts[1] : cuts[2]].T
-    grad_outward = summed[:, cuts[2] :].T
+        summed[:, hidden_here : back_width - gap].reshape(depth, 3, head_cols), (1, 0, 2)
+    )
+    grad_narrowing = summed[:, back_width : back_width + hidden_here].T
+    grad_outward = summed[:, back_width + hidden_here : used].T
+    grad_scaling = summed[:, width - 1]
     part_in = lamb_parts(master_inward, first_inward, second_inward, grad_inward)
     part_out = lamb_parts(master_outward, first_outward, second_outward, grad_outward)
     part_wide = lamb_parts(master_widening, first_widening, second_widening, grad_widening)

time: 369 us -> 310 us (0.84)
  local copies, waits for them, and re-layouts: 76.8 us -> 24.8 us
  Pallas kernels: 257 us -> 253 us
    reshape x4 -> x0, local copies, waits for them, and re-layouts: 31.3 us -> none  [the longest x2 15.7 us: by_image(): values.reshape(images, SEQ, model)]
    slice x7, local copies, waits for them, and re-layouts: 18 us -> 0.35 us  [the longest x1 0.17 us: local(): grad_scaling = summed[:, width - 1]]
    pallas_call x2 -> x1, Pallas kernels: 20.8 us -> 9.96 us  [total_of(): pl.pallas_call(functools.partial(total_kernel, devices, ranks), out_shape...]
    pad x2 -> x0, local copies, waits for them, and re-layouts: 10.3 us -> none  [by_image(): jnp.pad(values.reshape(images, SEQ, model), ((0, 0), (0, padded - SEQ), (...]
    unnamed x43 -> x42, local copies, waits for them, and re-layouts: 10.6 us -> 18.6 us
    pallas_call x1, Pallas kernels: 143 us -> 149 us  [image_block(): pl.pallas_call(functools.partial(image_kernel, images, (width, head_cols)...]
where the time goes in v3:
time: 310 us
  Pallas kernels  253 us (82%)
  local copies, waits for them, and re-layouts  24.8 us (8%)
  other arithmetic  23.8 us (8%)
  between operations  7.66 us (2%)
    pallas_call x1, Pallas kernels, image_block(): pl.pallas_call(functools.partial(image_kernel, images, (width, head_cols)...  149 us
    pallas_call x1, Pallas kernels, gather_blocks(): pl.pallas_call(functools.partial(gather_kernel, line), out_shape=jax.Shap...  49.2 us
    pallas_call x1, Pallas kernels, reduce_blocks(): pl.pallas_call(functools.partial(reduce_kernel, line), out_shape=jax.Shap...  45.5 us
    unnamed x42, local copies, waits for them, and re-layouts  18.6 us
    pallas_call x1, Pallas kernels, total_of(): pl.pallas_call(functools.partial(total_kernel, devices, ranks), out_shape...  9.96 us

profile of v3, /device:TPU:0, one launch (start us, length us, event | category | flops | bytes accessed | tf_op | source)
XLA Modules:
  0.0 309.6 jit_solution(16058663584725916524)
XLA Ops:
  0.7 1.0 copy.100
  1.7 1.7 multiply_reduce_fusion.5
  3.4 0.2 copy.99
  3.6 0.2 copy.101
  3.7 1.3 multiply_reduce_fusion.9
  5.2 1.0 convert.22
  6.1 1.0 convert_bitcast_fusion
  7.1 0.9 concatenate.13.own_ref
  8.0 49.2 %gather_blocks.1 = bf16[8,96,2432]{2,1,0:T(8,128)(2,1)} custom-call(bf16[96,2432]{1,0:T(8,128)(2,1)} %concatenate.13.own_ref), custom_call_target="tpu_custom_call" | custom-call | bytes 100000000 | tf_op jit(solution)/shard_map/gather_blocks/pallas_call | solution.py:134
  57.2 0.6 pad_maximum_fusion.tail_ref
  57.9 148.7 %image_block.1 = (bf16[3332,768]{1,0:T(8,128)(2,1)}, bf16[3332,768]{1,0:T(8,128)(2,1)}, bf16[768,2432]{1,0:T(8,128)(2,1)}) custom-call(bf16[3332,768]{1,0:T(8,128)(2,1)} %x_hbm.1, bf16[3332,768]{1,0:T(8,128)(2,1)} %c_hbm.1, bf16[2,16,768]{2,1,0:T(8,128)(2,1)} %pad_maximum_fusion.tail_ref, bf16[768,2432]{1,0:T(8,128)(2,1)} %bitcast.50), custom_call_target="tpu_custom_call" | custom-call | tf_op jit(solution)/shard_map/image_block/pallas_call | solution.py:632
  206.7 2.0 copy-done
  208.7 45.5 %reduce_blocks.1 = f32[96,2432]{1,0:T(8,128)S(1)} custom-call(bf16[8,96,2432]{2,1,0:T(8,128)(2,1)S(1)} %bitcast.49), custom_call_target="tpu_custom_call" | custom-call | bytes 100000000 | tf_op jit(solution)/shard_map/reduce_blocks/pallas_call | solution.py:271
  254.3 1.6 multiply_reduce_fusion.1
  255.9 1.4 maximum_bitcast_fusion.3
  257.3 1.6 multiply_reduce_fusion.3
  259.0 1.4 maximum_bitcast_fusion.2
  260.3 0.1 copy.103
  260.8 1.1 copy.104
  261.9 0.8 multiply_reduce_fusion.4
  262.8 1.4 maximum_bitcast_fusion
  264.1 1.0 copy.106
  265.1 1.0 copy.107
  266.1 0.7 multiply_reduce_fusion.6
  266.8 0.6 multiply_reduce_fusion.7
  267.4 1.4 maximum_bitcast_fusion.1
  268.8 0.2 slice_reduce_fusion
  269.0 1.1 multiply_reduce_fusion.8
  270.1 1.4 maximum_multiply_fusion
  271.5 0.6 scatter.4.own_ref
  272.1 10.0 %total_3.1 = f32[8,128]{1,0:T(8,128)} custom-call(f32[8,128]{1,0:T(8,128)} %scatter.4.own_ref), custom_call_target="tpu_custom_call" | custom-call | bytes 20000000 | tf_op jit(solution)/shard_map/total_3/pallas_call | solution.py:365
  282.1 0.7 slice_sqrt_fusion
  282.7 0.6 fusion.15
  284.7 0.5 fusion.5
  286.6 2.0 fusion.6
  289.9 2.0 fusion.7
  293.3 0.7 copy.117
  294.0 0.7 copy.118
  296.1 0.2 fusion.9
  296.3 0.9 copy.113
  297.1 0.8 copy.114
  297.9 0.6 copy.119
  298.6 0.7 copy.115
  299.3 0.7 copy.116
  300.1 0.9 copy.111
  300.9 0.9 copy.112
  301.8 2.7 constant_dynamic-slice_fusion
  304.5 5.1 %copy.121 = bf16[3332,768]{1,0:T(8,128)(2,1)} copy(bf16[3332,768]{1,0:T(8,128)(2,1)} %get-tuple-element.201) | data formatting | bytes 10235904
  (38 shorter events, 0.6 us)
Async XLA Ops:
  0.7 56.6 %slice-start = ((bf16[3332,768]{1,0:T(8,128)(2,1)}), bf16[4,768]{1,0:T(4,128)(2,1)S(1)}, s32[]{:S(2)}) async-start(bf16[3332,768]{1,0:T(8,128)(2,1)} %x_hbm.1), calls=%async_computation | async-start | bytes 12288 | tf_op jit(solution)/shard_map/slice | solution.py:719
  0.7 56.5 %slice-start.1 = ((bf16[3332,768]{1,0:T(8,128)(2,1)}), bf16[4,768]{1,0:T(4,128)(2,1)S(1)}, s32[]{:S(2)}) async-start(bf16[3332,768]{1,0:T(8,128)(2,1)} %c_hbm.1), calls=%async_computation.1 | async-start | bytes 12288 | tf_op jit(solution)/shard_map/slice | solution.py:719
  57.9 196.4 %copy-start.1 = (f32[768,96]{0,1:T(8,128)S(1)}, f32[768,96]{0,1:T(8,128)}, u32[]{:S(2)}) copy-start(f32[768,96]{0,1:T(8,128)} %param.30) | copy-start | bytes 884740
  57.9 196.4 %copy-start.6 = (f32[768,96]{0,1:T(8,128)S(1)}, f32[768,96]{0,1:T(8,128)}, u32[]{:S(2)}) copy-start(f32[768,96]{0,1:T(8,128)} %param.31) | copy-start | bytes 884740
  57.9 196.4 %copy-start.7 = (f32[768,96]{0,1:T(8,128)S(1)}, f32[768,96]{0,1:T(8,128)}, u32[]{:S(2)}) copy-start(f32[768,96]{0,1:T(8,128)} %param.32) | copy-start | bytes 884740
  57.9 199.4 %copy-start.2 = (f32[96,768]{1,0:T(8,128)S(1)}, f32[96,768]{1,0:T(8,128)}, u32[]{:S(2)}) copy-start(f32[96,768]{1,0:T(8,128)} %param.27) | copy-start | bytes 884740
  57.9 199.4 %copy-start.8 = (f32[96,768]{1,0:T(8,128)S(1)}, f32[96,768]{1,0:T(8,128)}, u32[]{:S(2)}) copy-start(f32[96,768]{1,0:T(8,128)} %param.28) | copy-start | bytes 884740
  57.9 199.4 %copy-start.9 = (f32[96,768]{1,0:T(8,128)S(1)}, f32[96,768]{1,0:T(8,128)}, u32[]{:S(2)}) copy-start(f32[96,768]{1,0:T(8,128)} %param.29) | copy-start | bytes 884740
  57.9 202.6 %copy-start.3 = (f32[3,96,192]{2,1,0:T(8,128)S(1)}, f32[3,96,192]{2,1,0:T(8,128)}, u32[]{:S(2)}) copy-start(f32[3,96,192]{2,1,0:T(8,128)} %param.21) | copy-start | bytes 663556
  57.9 202.7 %copy-start.5 = (f32[3,96,192]{2,1,0:T(8,128)S(1)}, f32[3,96,192]{2,1,0:T(8,128)}, u32[]{:S(2)}) copy-start(f32[3,96,192]{2,1,0:T(8,128)} %param.22) | copy-start | bytes 663556
  206.6 2.1 copy-start
  254.3 12.5 %copy-start.4 = (f32[192,96]{1,0:T(8,128)S(1)}, f32[192,96]{1,0:T(8,128)}, u32[]{:S(2)}) copy-start(f32[192,96]{1,0:T(8,128)} %param.24) | copy-start | bytes 221188
  254.3 14.7 %copy-start.10 = (f32[96]{0:T(128)S(1)}, f32[96]{0:T(128)}, u32[]{:S(2)}) copy-start(f32[96]{0:T(128)} %param.33) | copy-start | bytes 1156
  254.3 14.7 %copy-start.11 = (f32[96]{0:T(128)S(1)}, f32[96]{0:T(128)}, u32[]{:S(2)}) copy-start(f32[96]{0:T(128)} %param.34) | copy-start | bytes 1156
  254.3 14.7 %copy-start.12 = (f32[96]{0:T(128)S(1)}, f32[96]{0:T(128)}, u32[]{:S(2)}) copy-start(f32[96]{0:T(128)} %param.35) | copy-start | bytes 1156

commit v4 on v3

--- a/solution.py
+++ b/solution.py
@@ -670,6 +670,85 @@
         ),
         name="image_block",
     )(inputs, cotangent, tails, weights)
+
+
+def parts_kernel(cuts, replicas, summed_ref, *refs):
+    states, outs, sums_ref = refs[:15], refs[15:30], refs[30]
+    hidden_here, head_cols, back_width, used = cuts
+    width = summed_ref.shape[1]
+    row = lax.broadcasted_iota(jnp.int32, sums_ref.shape, 0)
+    lane = lax.broadcasted_iota(jnp.int32, sums_ref.shape, 1)
+    sums = jnp.zeros(sums_ref.shape, jnp.float32)
+
+    def square_sum(values):
+        return jnp.sum(jnp.sum(values * values, axis=1, keepdims=True), axis=0, keepdims=True)
+
+    def one(index, grad, at=None):
+        master, first, second = (
+            ref[...] if at is None else ref[at] for ref in states[3 * index : 3 * index + 3]
+        )
+        results = lamb_parts(master, first, second, grad)
+        for ref, value in zip(outs[3 * index : 3 * index + 3], results):
+            if at is None:
+                ref[...] = value
+            else:
+                ref[at] = value
+        return square_sum(master), square_sum(results[2])
+
+    def add(total, index, pair, scale=1.0):
+        for column in range(2):
+            here = jnp.logical_and(row == index, lane == column)
+            total = total + jnp.where(here, pair[column] * scale, 0.0)
+        return total
+
+    for kind in range(3):
+        at = hidden_here + kind * head_cols
+        sums = add(sums, 0, one(0, summed_ref[:, at : at + head_cols], kind))
+    outward_at = back_width + hidden_here
+    sums = add(sums, 1, one(1, summed_ref[:, outward_at:used].T))
+    sums = add(sums, 2, one(2, summed_ref[:, :hidden_here]))
+    sums = add(sums, 3, one(3, summed_ref[:, back_width:outward_at].T))
+    gain = summed_ref[:, width - 128 :].T
+    sums = add(sums, 4, one(4, gain[127:128]), replicas)
+    sums_ref[...] = sums
+
+
+def fresh_kernel(sums_ref, *refs):
+    masters, updates, fresh, low = refs[:5], refs[5:10], refs[10:15], refs[15:20]
+    for index in range(5):
+        norms = jnp.sqrt(sums_ref[index : index + 1, :])
+        rate = learn_rate * (norms[:, 0:1] / norms[:, 1:2])
+        if len(masters[index].shape) == 3:
+            rate = rate.reshape(1, 1, 1)
+        value = masters[index][...] - rate * updates[index][...]
+        fresh[index][...] = value
+        low[index][...] = value.astype(jnp.bfloat16)
+
+
+def lamb_step(summed, states, cuts):
+    vmem = pl.BlockSpec(memory_space=pltpu.VMEM)
+    flat = [array for group in states for array in group]
+    like = [jax.ShapeDtypeStruct(array.shape, jnp.float32) for array in flat]
+    *parts, sums = pl.pallas_call(
+        functools.partial(parts_kernel, cuts, 1.0 / lax.axis_size("tensor")),
+        out_shape=like + [jax.ShapeDtypeStruct((8, 128), jnp.float32)],
+        in_specs=[vmem] * 16,
+        out_specs=[vmem] * 16,
+        compiler_params=pltpu.CompilerParams(vmem_limit_bytes=40 * 2**20),
+        name="lamb_parts",
+    )(summed, *flat)
+    sums = total_of(sums, 3)
+    masters = [group[0] for group in states]
+    fresh = pl.pallas_call(
+        fresh_kernel,
+        out_shape=[jax.ShapeDtypeStruct(m.shape, jnp.float32) for m in masters]
+        + [jax.ShapeDtypeStruct(m.shape, jnp.bfloat16) for m in masters],
+        in_specs=[vmem] * 11,
+        out_specs=[vmem] * 10,
+        compiler_params=pltpu.CompilerParams(vmem_limit_bytes=40 * 2**20),
+        name="lamb_fresh",
+    )(sums, *masters, *parts[2::3])
+    return parts, fresh, jnp.sqrt(sums[:5, :2])
 
 
 def local(
@@ -727,78 +806,21 @@
     start = lax.axis_index("tensor") * share
     output = lax.dynamic_slice_in_dim(summed_out, start, share, 0)
     summed = reduce_blocks(grads.reshape(lax.axis_size("dp"), depth, width))
-    grad_widening = summed[:, :hidden_here]
-    grad_inward = jnp.transpose(
-        summed[:, hidden_here : back_width - gap].reshape(depth, 3, head_cols), (1, 0, 2)
+    states = (
+        (master_inward, first_inward, second_inward),
+        (master_outward, first_outward, second_outward),
+        (master_widening, first_widening, second_widening),
+        (master_narrowing, first_narrowing, second_narrowing),
+        tuple(v.reshape(1, depth) for v in (master_scaling, first_scaling, second_scaling)),
     )
-    grad_narrowing = summed[:, back_width : back_width + hidden_here].T
-    grad_outward = summed[:, back_width + hidden_here : used].T
-    grad_scaling = summed[:, width - 1]
-    part_in = lamb_parts(master_inward, first_inward, second_inward, grad_inward)
-    part_out = lamb_parts(master_outward, first_outward, second_outward, grad_outward)
-    part_wide = lamb_parts(master_widening, first_widening, second_widening, grad_widening)
-    part_narrow = lamb_parts(master_narrowing, first_narrowing, second_narrowing, grad_narrowing)
-    part_scale = lamb_parts(master_scaling, first_scaling, second_scaling, grad_scaling)
-    replicas = 1.0 / lax.axis_size("tensor")
-    local_sums = jnp.stack(
-        [
-            jnp.stack([jnp.sum(master_inward * master_inward), jnp.sum(part_in[2] * part_in[2])]),
-            jnp.stack(
-                [jnp.sum(master_outward * master_outward), jnp.sum(part_out[2] * part_out[2])]
-            ),
-            jnp.stack(
-                [jnp.sum(master_widening * master_widening), jnp.sum(part_wide[2] * part_wide[2])]
-            ),
-            jnp.stack(
-                [
-                    jnp.sum(master_narrowing * master_narrowing),
-                    jnp.sum(part_narrow[2] * part_narrow[2]),
-                ]
-            ),
-            jnp.stack(
-                [jnp.sum(master_scaling * master_scaling), jnp.sum(part_scale[2] * part_scale[2])]
-            )
-            * replicas,
-        ]
+    parts, fresh, trust_norms = lamb_step(
+        summed, states, (hidden_here, head_cols, back_width, used)
     )
-    packed = jnp.zeros((8, 128), jnp.float32).at[:5, :2].set(local_sums)
-    trust_norms = jnp.sqrt(total_of(packed, 3)[:5, :2])
-    fresh_in = master_inward - learn_rate * (trust_norms[0, 0] / trust_norms[0, 1]) * part_in[2]
-    fresh_out = master_outward - learn_rate * (trust_norms[1, 0] / trust_norms[1, 1]) * part_out[2]
-    fresh_wide = (
-        master_widening - learn_rate * (trust_norms[2, 0] / trust_norms[2, 1]) * part_wide[2]
-    )
-    fresh_narrow = (
-        master_narrowing - learn_rate * (trust_norms[3, 0] / trust_norms[3, 1]) * part_narrow[2]
-    )
-    fresh_scale = (
-        master_scaling - learn_rate * (trust_norms[4, 0] / trust_norms[4, 1]) * part_scale[2]
-    )
-    return (
-        output,
-        input_grad,
-        part_in[0],
-        part_in[1],
-        fresh_in,
-        fresh_in.astype(jnp.bfloat16),
-        part_out[0],
-        part_out[1],
-        fresh_out,
-        fresh_out.astype(jnp.bfloat16),
-        part_wide[0],
-        part_wide[1],
-        fresh_wide,
-        fresh_wide.astype(jnp.bfloat16),
-        part_narrow[0],
-        part_narrow[1],
-        fresh_narrow,
-        fresh_narrow.astype(jnp.bfloat16),
-        part_scale[0],
-        part_scale[1],
-        fresh_scale,
-        fresh_scale.astype(jnp.bfloat16),
-        trust_norms,
-    )
+    results = []
+    for index in range(5):
+        group = (parts[3 * index], parts[3 * index + 1], fresh[index], fresh[5 + index])
+        results += [v.reshape(depth) for v in group] if index == 4 else group
+    return (output, input_grad, *results, trust_norms)
 
 
 def solution(mesh):

time: 310 us -> 296 us (0.955)
  other arithmetic: 23.8 us -> 4.23 us
  local copies, waits for them, and re-layouts: 24.8 us -> 33.4 us
  between operations: 7.66 us -> 0.91 us
  Pallas kernels: 253 us -> 257 us
    reduce_sum x8 -> x0, other arithmetic: 9.6 us -> none  [the longest x1 1.73 us: local(): jnp.sum(master_inward * master_inward)]
    unnamed x42 -> x62, local copies, waits for them, and re-layouts: 18.6 us -> 28 us
    another operation x5 -> x2, other arithmetic: 6.45 us -> 1.64 us  [the longest x4 5.46 us: local(): jnp.stack([jnp.stack([jnp.sum(master_inward * master_inward), jnp.sum(par...]
    convert_element_type x5 -> x0, other arithmetic: 4.73 us -> none  [the longest x1 1.98 us: local(): fresh_narrow.astype(jnp.bfloat16)]
    pallas_call x0 -> x2, Pallas kernels: none -> 3.22 us  [the longest x1 2.03 us: lamb_step(): pl.pallas_call(functools.partial(parts_kernel, cuts, 1.0 / lax.axis_size(...]
where the time goes in v4:
time: 296 us; the launch traced here: 295 us
  Pallas kernels  257 us (87%)
  local copies, waits for them, and re-layouts  33.4 us (11%)
  other arithmetic  4.23 us (1%)
    pallas_call x1, Pallas kernels, image_block(): pl.pallas_call(functools.partial(image_kernel, images, (width, head_cols)...  149 us
    pallas_call x1, Pallas kernels, gather_blocks(): pl.pallas_call(functools.partial(gather_kernel, line), out_shape=jax.Shap...  49.2 us
    pallas_call x1, Pallas kernels, reduce_blocks(): pl.pallas_call(functools.partial(reduce_kernel, line), out_shape=jax.Shap...  45.5 us
    unnamed x62, local copies, waits for them, and re-layouts  28 us
    pallas_call x1, Pallas kernels, total_of(): pl.pallas_call(functools.partial(total_kernel, devices, ranks), out_shape...  9.94 us

profile of v4, /device:TPU:0, one launch (start us, length us, event | category | flops | bytes accessed | tf_op | source)
XLA Modules:
  0.0 295.1 jit_solution(17694108381227079031)
XLA Ops:
  0.7 0.7 slice.10
  1.4 0.7 slice.9
  2.1 0.6 pad_maximum_fusion.tail_ref
  2.7 1.0 convert_bitcast_fusion.1
  3.7 0.2 copy.51
  3.9 0.2 copy.53
  4.0 1.0 convert.22
  5.0 1.0 convert_bitcast_fusion
  6.0 1.0 copy.52
  7.0 0.7 convert.26
  7.6 0.1 broadcast_in_dim.10
  7.7 0.9 concatenate.4.own_ref
  8.6 49.2 %gather_blocks.1 = bf16[8,96,2432]{2,1,0:T(8,128)(2,1)} custom-call(bf16[96,2432]{1,0:T(8,128)(2,1)} %concatenate.4.own_ref), custom_call_target="tpu_custom_call" | custom-call | bytes 100000000 | tf_op jit(solution)/shard_map/gather_blocks/pallas_call | solution.py:134
  57.8 0.0 copy-start.24
  57.8 0.0 copy-start.25
  57.8 0.0 copy-start.2
  57.9 148.7 %image_block.1 = (bf16[3332,768]{1,0:T(8,128)(2,1)}, bf16[3332,768]{1,0:T(8,128)(2,1)}, bf16[768,2432]{1,0:T(8,128)(2,1)}) custom-call(bf16[3332,768]{1,0:T(8,128)(2,1)} %x_hbm.1, bf16[3332,768]{1,0:T(8,128)(2,1)} %c_hbm.1, bf16[2,16,768]{2,1,0:T(8,128)(2,1)} %pad_maximum_fusion.tail_ref, bf16[768,2432]{1,0:T(8,128)(2,1)} %bitcast.26), custom_call_target="tpu_custom_call" | custom-call | tf_op jit(solution)/shard_map/image_block/pallas_call | solution.py:632
  206.6 2.1 copy-done
  208.6 45.5 %reduce_blocks.1.summed_ref = f32[96,2432]{1,0:T(8,128)S(1)} custom-call(bf16[8,96,2432]{2,1,0:T(8,128)(2,1)S(1)} %bitcast.21), custom_call_target="tpu_custom_call" | custom-call | bytes 100000000 | tf_op jit(solution)/shard_map/reduce_blocks/pallas_call | solution.py:271
  254.2 0.2 copy.54.refs_9_.refs_3_
  254.4 0.2 copy.55.refs_10_
  254.5 1.1 copy.56.refs_11_
  255.7 1.0 copy-done.8
  256.7 1.0 copy-done.9
  257.7 1.0 copy-done.10
  258.6 0.9 copy-done.15
  259.5 0.9 copy-done.16
  260.4 2.0 lamb_parts.1
  262.4 0.7 copy-done.4
  263.2 0.7 copy-done.5
  263.9 0.7 copy-done.11
  264.7 0.7 copy-done.13
  265.4 0.6 copy-done.17
  266.0 0.6 copy-done.20
  266.6 9.9 %total_3.1.sums_ref = f32[8,128]{1,0:T(8,128)} custom-call(f32[8,128]{1,0:T(8,128)} %copy-done.20), custom_call_target="tpu_custom_call" | custom-call | bytes 20000000 | tf_op jit(solution)/shard_map/total_3/pallas_call | solution.py:365
  276.6 1.0 copy-done.6
  277.5 1.0 copy-done.12
  278.5 1.0 copy-done.14
  279.5 0.9 copy-done.18
  280.4 0.7 copy-done.19
  281.0 1.2 lamb_fresh.1
  282.2 0.9 copy.60
  283.1 0.8 copy.61
  283.9 0.7 copy.62
  284.6 1.9 copy.58
  286.4 0.9 copy.59
  287.3 2.7 constant_dynamic-slice_fusion
  290.0 5.1 %copy.64 = bf16[3332,768]{1,0:T(8,128)(2,1)} copy(bf16[3332,768]{1,0:T(8,128)(2,1)} %get-tuple-element.153) | data formatting | bytes 10235904
  (35 shorter events, 0.1 us)
Async XLA Ops:
  57.8 196.4 %copy-start.24 = (f32[768,96]{0,1:T(8,128)S(1)}, f32[768,96]{0,1:T(8,128)}, u32[]{:S(2)}) copy-start(f32[768,96]{0,1:T(8,128)} %param.28) | copy-start | bytes 884740
  57.8 196.5 %copy-start.25 = (f32[768,96]{0,1:T(8,128)S(1)}, f32[768,96]{0,1:T(8,128)}, u32[]{:S(2)}) copy-start(f32[768,96]{0,1:T(8,128)} %param.29) | copy-start | bytes 884740
  57.8 197.8 %copy-start.1 = (f32[96,768]{1,0:T(8,128)S(1)}, f32[96,768]{1,0:T(8,128)}, u32[]{:S(2)}) copy-start(f32[96,768]{1,0:T(8,128)} %refs_2_.3) | copy-start | bytes 884740
  57.8 197.8 %copy-start.2 = (f32[3,96,192]{2,1,0:T(8,128)S(1)}, f32[3,96,192]{2,1,0:T(8,128)}, u32[]{:S(2)}) copy-start(f32[3,96,192]{2,1,0:T(8,128)} %refs_0_.3) | copy-start | bytes 663556
  57.8 197.8 %copy-start.3 = (f32[192,96]{1,0:T(8,128)S(1)}, f32[192,96]{1,0:T(8,128)}, u32[]{:S(2)}) copy-start(f32[192,96]{1,0:T(8,128)} %refs_1_.3) | copy-start | bytes 221188
  57.9 197.8 %copy-start.7 = (f32[3,96,192]{2,1,0:T(8,128)S(1)}, f32[3,96,192]{2,1,0:T(8,128)}, u32[]{:S(2)}) copy-start(f32[3,96,192]{2,1,0:T(8,128)} %refs_1_.2) | copy-start | bytes 663556
  206.5 49.2 %copy-start.21 = (f32[96]{0:T(128)S(1)}, f32[96]{0:T(128)}, u32[]{:S(2)}) copy-start(f32[96]{0:T(128)} %param.31) | copy-start | bytes 1156
  206.5 49.2 %copy-start.22 = (f32[96]{0:T(128)S(1)}, f32[96]{0:T(128)}, u32[]{:S(2)}) copy-start(f32[96]{0:T(128)} %param.32) | copy-start | bytes 1156
  206.6 49.2 %copy-start.23 = (f32[96]{0:T(128)S(1)}, f32[96]{0:T(128)}, u32[]{:S(2)}) copy-start(f32[96]{0:T(128)} %param.33) | copy-start | bytes 1156
  206.6 2.1 copy-start
  255.7 1.0 copy-start.8
  256.7 1.0 copy-start.9
  257.7 1.0 copy-start.10
  258.6 0.9 copy-start.15
  259.5 0.9 copy-start.16
  262.4 0.7 copy-start.4
  263.2 0.7 copy-start.5
  263.9 0.7 copy-start.11
  264.6 0.7 copy-start.13
  265.4 0.6 copy-start.17
  266.0 0.6 copy-start.20
  276.5 1.0 copy-start.6
  277.5 1.0 copy-start.12
  278.5 1.0 copy-start.14
  279.5 0.9 copy-start.18
  280.4 0.7 copy-start.19

commit v5 on v4

--- a/solution.py
+++ b/solution.py
@@ -377,7 +377,7 @@
             pltpu.SemaphoreType.DMA((devices,)),
         ],
         compiler_params=pltpu.CompilerParams(
-            collective_id=collective_id, has_side_effects=True
+            collective_id=collective_id, has_side_effects=True, vmem_limit_bytes=60 * 2**20
         ),
         cost_estimate=pl.CostEstimate(flops=0, bytes_accessed=20_000_000, transcendentals=0),
         name="total_" + str(collective_id),
@@ -435,6 +435,8 @@
         for slot in range(2):
             for kind in range(2):
                 windows[slot, kind, WINDOW:] = tail_ref[kind]
+        total[...] = jnp.zeros_like(total)
+        kept[...] = jnp.zeros_like(kept)
         acc1[...] = jnp.zeros_like(acc1)
         acc2[...] = jnp.zeros_like(acc2)
         back_cols[...] = jnp.zeros_like(back_cols)
@@ -477,49 +479,54 @@
 
     gain = gain_row[...]
 
-    def place(ref, image, values):
-        @pl.when(image < images - 1)
-        def _():
-            start = pl.multiple_of(image * SEQ // 16 * 16, 16)
-            offset = image * SEQ - start
-            spread = one_hot(
-                (WINDOW, rows), lambda r, j: jnp.logical_and(r == j + offset, j < SEQ)
-            )
-            placed = jnp.dot(spread, values, preferred_element_type=f32)
-            before = lax.broadcasted_iota(jnp.int32, (16, model), 0) < offset
-            head = jnp.where(before, ref[pl.ds(start, 16), :].astype(f32), placed[:16])
-            ref[pl.ds(start, 16), :] = head.astype(b16)
-            ref[pl.ds(start + 16, WINDOW - 16), :] = placed[16:].astype(b16)
-
-        @pl.when(image == images - 1)
+    image = jnp.maximum(step - 3, 0)
+
+    def place(ref, values):
+        start = pl.multiple_of(image * SEQ // 16 * 16, 16)
+        offset = image * SEQ - start
+        spread = one_hot((WINDOW, rows), lambda r, j: jnp.logical_and(r == j + offset, j < SEQ))
+        placed = jnp.dot(spread, values, preferred_element_type=f32)
+        before = lax.broadcasted_iota(jnp.int32, (16, model), 0) < offset
+        head = jnp.where(before, ref[pl.ds(start, 16), :].astype(f32), placed[:16])
+        ref[pl.ds(start, 16), :] = head.astype(b16)
+        ref[pl.ds(start + 16, WINDOW - 16), :] = placed[16:].astype(b16)
+
+    def place_late(ref, values):
+        @pl.when(step < images + 2)
+        def _():
+            place(ref, values)
+
+        @pl.when(step == images + 2)
         def _():
             ref[(images - 1) * SEQ :] = values[:SEQ]
 
     @pl.when(step >= 3)
     def _():
-        slot = (step - 3) % 2
-        third(slot).wait()
-        floats, unit, inv_std = normalised(kept[(step - 3) % 4, 0])
+        third((step - 3) % 3).wait()
+
+    def finish(put):
+        slot, spot = (step + 3) % 3, (step + 1) % 4
+        floats, unit, inv_std = normalised(kept[spot, 0])
         sums = jnp.concatenate([total[slot, 0, 0], total[slot, 1, 0]], axis=1).astype(f32)
-        place(out_ref, step - 3, (floats + sums).astype(b16))
+        put(out_ref, (floats + sums).astype(b16))
         d_normed = jnp.concatenate([total[slot, 0, 1], total[slot, 1, 1]], axis=1).astype(f32)
         weighted = d_normed * unit
-        g_gain[...] += jnp.sum(weighted, axis=0, keepdims=True)
+        counted = jnp.sum(weighted, axis=0, keepdims=True)
+        g_gain[...] += jnp.where(step >= 3, counted, 0.0)
         d_unit = d_normed * gain
         d_floats = inv_std * (
             d_unit
             - jnp.mean(d_unit, axis=1, keepdims=True)
             - unit * jnp.mean(weighted * gain, axis=1, keepdims=True)
         )
-        floats_back = kept[(step - 3) % 4, 1].astype(f32) + d_floats
-        place(grad_in_ref, step - 3, floats_back.astype(b16))
+        put(grad_in_ref, (kept[spot, 1].astype(f32) + d_floats).astype(b16))
 
     @pl.when(jnp.logical_and(step >= 2, step < images + 2))
     def _():
-        slot = (step - 2) % 2
+        slot, spot = (step - 2) % 2, (step - 2) % 3
         second(slot).wait()
-        total[slot, core] = (chip_sum[slot].astype(f32) + line_in[slot].astype(f32)).astype(b16)
-        third(slot).start()
+        total[spot, core] = (chip_sum[slot].astype(f32) + line_in[slot].astype(f32)).astype(b16)
+        third(spot).start()
 
     @pl.when(jnp.logical_and(step >= 1, step < images + 1))
     def _():
@@ -596,6 +603,7 @@
         )
         back_cols[:, :width] = (d_hidden * slope).astype(b16)
 
+        finish(place)
         out_part = mm_nt(front_cols[...], w_ref[:, back_width:]).astype(b16)
         partial[slot, 0, 0] = out_part[:, :half]
         partial[slot, 1, 0] = out_part[:, half:]
@@ -605,6 +613,10 @@
         first(slot).start()
         acc1[...] += mm_tn(normed, back_cols[...])
         acc2[...] += mm_tn(cot, front_cols[...])
+
+    @pl.when(step >= images)
+    def _():
+        finish(place_late)
 
     @pl.when(step == images + 2)
     def _():
@@ -658,10 +670,11 @@
             pltpu.VMEM((2, 2, rows, half), bf),
             pltpu.VMEM((2, 2, rows, half), bf),
             pltpu.VMEM((2, 2, rows, half), bf),
-            pltpu.VMEM((2, 2, 2, rows, half), bf),
+            pltpu.VMEM((3, 2, 2, rows, half), bf),
             pltpu.SemaphoreType.DMA((2, 2)),
         ]
-        + [pltpu.SemaphoreType.DMA((2,))] * 6,
+        + [pltpu.SemaphoreType.DMA((2,))] * 4
+        + [pltpu.SemaphoreType.DMA((3,))] * 2,
         compiler_params=pltpu.CompilerParams(
             collective_id=4,
             has_side_effects=True,
@@ -707,7 +720,7 @@
     outward_at = back_width + hidden_here
     sums = add(sums, 1, one(1, summed_ref[:, outward_at:used].T))
     sums = add(sums, 2, one(2, summed_ref[:, :hidden_here]))
-    sums = add(sums, 3, one(3, summed_ref[:, back_width:outward_at].T))
+    sums = add(sums, 3, one(3, summed_ref[:, back_width:outward_at]))
     gain = summed_ref[:, width - 128 :].T
     sums = add(sums, 4, one(4, gain[127:128]), replicas)
     sums_ref[...] = sums
@@ -726,27 +739,31 @@
 
 
 def lamb_step(summed, states, cuts):
-    vmem = pl.BlockSpec(memory_space=pltpu.VMEM)
+    def blocks(arrays):
+        return [pl.BlockSpec(a.shape, lambda i, n=a.ndim: (0,) * n) for a in arrays]
+
+    one_step = {"grid": (1,), "compiler_params": pltpu.CompilerParams(vmem_limit_bytes=60 * 2**20)}
     flat = [array for group in states for array in group]
     like = [jax.ShapeDtypeStruct(array.shape, jnp.float32) for array in flat]
+    like.append(jax.ShapeDtypeStruct((8, 128), jnp.float32))
     *parts, sums = pl.pallas_call(
         functools.partial(parts_kernel, cuts, 1.0 / lax.axis_size("tensor")),
-        out_shape=like + [jax.ShapeDtypeStruct((8, 128), jnp.float32)],
-        in_specs=[vmem] * 16,
-        out_specs=[vmem] * 16,
-        compiler_params=pltpu.CompilerParams(vmem_limit_bytes=40 * 2**20),
+        out_shape=like,
+        in_specs=blocks([summed, *flat]),
+        out_specs=blocks(like),
         name="lamb_parts",
+        **one_step,
     )(summed, *flat)
     sums = total_of(sums, 3)
     masters = [group[0] for group in states]
+    made = [jax.ShapeDtypeStruct(m.shape, t) for t in (jnp.float32, jnp.bfloat16) for m in masters]
     fresh = pl.pallas_call(
         fresh_kernel,
-        out_shape=[jax.ShapeDtypeStruct(m.shape, jnp.float32) for m in masters]
-        + [jax.ShapeDtypeStruct(m.shape, jnp.bfloat16) for m in masters],
-        in_specs=[vmem] * 11,
-        out_specs=[vmem] * 10,
-        compiler_params=pltpu.CompilerParams(vmem_limit_bytes=40 * 2**20),
+        out_shape=made,
+        in_specs=blocks([sums, *masters, *masters]),
+        out_specs=blocks(made),
         name="lamb_fresh",
+        **one_step,
     )(sums, *masters, *parts[2::3])
     return parts, fresh, jnp.sqrt(sums[:5, :2])
 
@@ -810,7 +827,7 @@
         (master_inward, first_inward, second_inward),
         (master_outward, first_outward, second_outward),
         (master_widening, first_widening, second_widening),
-        (master_narrowing, first_narrowing, second_narrowing),
+        (master_narrowing.T, first_narrowing.T, second_narrowing.T),
         tuple(v.reshape(1, depth) for v in (master_scaling, first_scaling, second_scaling)),
     )
     parts, fresh, trust_norms = lamb_step(
@@ -819,7 +836,11 @@
     results = []
     for index in range(5):
         group = (parts[3 * index], parts[3 * index + 1], fresh[index], fresh[5 + index])
-        results += [v.reshape(depth) for v in group] if index == 4 else group
+        if index == 3:
+            group = [v.T for v in group]
+        if index == 4:
+            group = [v.reshape(depth) for v in group]
+        results += group
     return (output, input_grad, *results, trust_norms)
 
 

time: 296 us -> 286 us (0.966)
  local copies, waits for them, and re-layouts: 33.4 us -> 15.8 us
  Pallas kernels: 257 us -> 265 us
    unnamed x62 -> x7, local copies, waits for them, and re-layouts: 28 us -> 9.71 us
    pallas_call x1, Pallas kernels: 149 us -> 153 us  [image_block(): pl.pallas_call(functools.partial(image_kernel, images, (width, head_cols)...]
where the time goes in v5:
time: 286 us; the launch traced here: 285 us
  Pallas kernels  265 us (93%)
  local copies, waits for them, and re-layouts  15.8 us (6%)
  other arithmetic  4.23 us (1%)
    pallas_call x1, Pallas kernels, image_block(): pl.pallas_call(functools.partial(image_kernel, images, (width, head_cols)...  153 us
    pallas_call x1, Pallas kernels, gather_blocks(): pl.pallas_call(functools.partial(gather_kernel, line), out_shape=jax.Shap...  49.2 us
    pallas_call x1, Pallas kernels, reduce_blocks(): pl.pallas_call(functools.partial(reduce_kernel, line), out_shape=jax.Shap...  45.3 us
    pallas_call x1, Pallas kernels, total_of(): pl.pallas_call(functools.partial(total_kernel, devices, ranks), out_shape...  9.96 us
    unnamed x7, local copies, waits for them, and re-layouts  9.71 us

profile of v5, /device:TPU:0, one launch (start us, length us, event | category | flops | bytes accessed | tf_op | source)
XLA Modules:
  0.0 285.4 jit_solution(2629848354901878207)
XLA Ops:
  0.7 0.7 slice.10
  1.4 0.7 slice.9
  2.1 0.6 pad_maximum_fusion.tail_ref
  2.7 1.0 convert_bitcast_fusion
  3.7 0.2 copy.43
  3.9 0.2 copy.45
  4.0 1.0 bitcast_convert_fusion
  5.0 1.0 convert.21
  6.0 1.0 copy.44
  7.0 0.7 convert.25
  7.6 0.1 broadcast_in_dim.10
  7.7 0.9 concatenate.4.own_ref
  8.6 49.2 %gather_blocks.1 = bf16[8,96,2432]{2,1,0:T(8,128)(2,1)} custom-call(bf16[96,2432]{1,0:T(8,128)(2,1)} %concatenate.4.own_ref), custom_call_target="tpu_custom_call" | custom-call | bytes 100000000 | tf_op jit(solution)/shard_map/gather_blocks/pallas_call | solution.py:134
  57.8 153.2 %image_block.1 = (bf16[3332,768]{1,0:T(8,128)(2,1)}, bf16[3332,768]{1,0:T(8,128)(2,1)}, bf16[768,2432]{1,0:T(8,128)(2,1)}) custom-call(bf16[3332,768]{1,0:T(8,128)(2,1)} %x_hbm.1, bf16[3332,768]{1,0:T(8,128)(2,1)} %c_hbm.1, bf16[2,16,768]{2,1,0:T(8,128)(2,1)} %pad_maximum_fusion.tail_ref, bf16[768,2432]{1,0:T(8,128)(2,1)} %bitcast.28), custom_call_target="tpu_custom_call" | custom-call | tf_op jit(solution)/shard_map/image_block/pallas_call | solution.py:644
  211.0 0.0 copy-start
  211.0 2.0 copy-done
  213.1 45.3 %reduce_blocks.1.summed_ref = f32[96,2432]{1,0:T(8,128)S(1)} custom-call(bf16[8,96,2432]{2,1,0:T(8,128)(2,1)S(1)} %bitcast.27), custom_call_target="tpu_custom_call" | custom-call | bytes 100000000 | tf_op jit(solution)/shard_map/reduce_blocks/pallas_call | solution.py:271
  258.4 0.0 copy-start.1
  258.4 0.9 copy-done.1
  259.3 4.2 %lamb_parts.1 = (f32[3,96,192]{2,1,0:T(8,128)}, f32[3,96,192]{2,1,0:T(8,128)}, f32[3,96,192]{2,1,0:T(8,128)}, f32[192,96]{1,0:T(8,128)}, f32[192,96]{1,0:T(8,128...) custom-call(f32[96,2432]{1,0:T(8,128)} %copy-done.1, ...), custom_call_target="tpu_custom_call" | custom-call | tf_op jit(solution)/shard_map/lamb_parts/pallas_call | solution.py:749
  263.5 10.0 %total_3.1.sums_ref = f32[8,128]{1,0:T(8,128)} custom-call(f32[8,128]{1,0:T(8,128)} %get-tuple-element.57.own_ref), custom_call_target="tpu_custom_call" | custom-call | bytes 20000000 | tf_op jit(solution)/shard_map/total_3/pallas_call | solution.py:365
  273.5 2.8 lamb_fresh.1
  276.3 0.7 slice_sqrt_fusion
  277.0 0.7 copy.46
  277.6 2.7 constant_dynamic-slice_fusion
  280.3 5.1 %copy.48 = bf16[3332,768]{1,0:T(8,128)(2,1)} copy(bf16[3332,768]{1,0:T(8,128)(2,1)} %get-tuple-element.153) | data formatting | bytes 10235904
  (2 shorter events, 0.0 us)
Async XLA Ops:
  211.0 2.1 copy-start
  258.4 0.9 copy-start.1

commit v6 on v5

--- a/solution.py
+++ b/solution.py
@@ -396,7 +396,7 @@
 ):
     step = pl.program_id(0)
     rank = lax.axis_index("tensor")
-    core = rank % 2
+    core, half_of_images = rank % 2, rank // 2
     sibling = {"tensor": rank + 1 - 2 * core}
     across = {"tensor": lax.rem(rank + 2, 4)}
     width, head_cols = cuts
@@ -407,6 +407,9 @@
     back_width, front_width = back_cols.shape[1], front_cols.shape[1]
     last_window = images * SEQ // 16 * 16 - WINDOW
 
+    def image_at(turn):
+        return turn // 2 + (turn % 2) * (images // 2 + 1)
+
     def window_start(image):
         return pl.multiple_of(jnp.minimum(image * SEQ // 16 * 16, last_window), 16)
 
@@ -426,6 +429,7 @@
 
     @pl.when(step == 0)
     def _():
+        line_in[...] = jnp.zeros_like(line_in)
         barrier = pltpu.get_barrier_semaphore()
         pl.semaphore_signal(barrier, inc=1, device_id=sibling, device_id_type=MESH)
         pl.semaphore_signal(barrier, inc=1, device_id=across, device_id_type=MESH)
@@ -449,7 +453,7 @@
 
     @pl.when(step < images - 1)
     def _():
-        for copy in fetches(step + 1, (step + 1) % 2):
+        for copy in fetches(image_at(step + 1), (step + 1) % 2):
             copy.start()
 
     def move(source, target, sends, recvs, slot, peer):
@@ -465,8 +469,21 @@
     def first(slot):
         return move(partial.at[slot, 1 - core], pair_in.at[slot], s1, r1, slot, sibling)
 
-    def second(slot):
-        return move(chip_sum.at[slot], line_in.at[slot], s2, r2, slot, across)
+    def second(slot, kind):
+        return pltpu.make_async_remote_copy(
+            src_ref=chip_sum.at[slot, kind],
+            dst_ref=line_in.at[slot, kind],
+            send_sem=s2.at[slot, kind],
+            recv_sem=r2.at[slot, kind],
+            device_id=across,
+            device_id_type=MESH,
+        )
+
+    def gives_output(turn):
+        return jnp.logical_or(turn % 2 != half_of_images, turn == images - 1)
+
+    def takes_output(turn):
+        return jnp.logical_or(turn % 2 == half_of_images, turn == images - 1)
 
     def third(slot):
         return move(total.at[slot, core], total.at[slot, core], s3, r3, slot, sibling)
@@ -479,7 +496,7 @@
 
     gain = gain_row[...]
 
-    image = jnp.maximum(step - 3, 0)
+    image = image_at(jnp.maximum(step - 3, 0))
 
     def place(ref, values):
         start = pl.multiple_of(image * SEQ // 16 * 16, 16)
@@ -492,13 +509,15 @@
         ref[pl.ds(start + 16, WINDOW - 16), :] = placed[16:].astype(b16)
 
     def place_late(ref, values):
-        @pl.when(step < images + 2)
+        @pl.when(step < images + 1)
         def _():
             place(ref, values)
 
-        @pl.when(step == images + 2)
-        def _():
-            ref[(images - 1) * SEQ :] = values[:SEQ]
+        for turn in (images - 2, images - 1):
+
+            @pl.when(step == turn + 3)
+            def _(at=image_at(turn) * SEQ):
+                ref[at : at + SEQ] = values[:SEQ]
 
     @pl.when(step >= 3)
     def _():
@@ -524,7 +543,16 @@
     @pl.when(jnp.logical_and(step >= 2, step < images + 2))
     def _():
         slot, spot = (step - 2) % 2, (step - 2) % 3
-        second(slot).wait()
+        second(slot, 1).wait()
+
+        @pl.when(gives_output(step - 2))
+        def _():
+            second(slot, 0).wait_send()
+
+        @pl.when(takes_output(step - 2))
+        def _():
+            second(slot, 0).wait_recv()
+
         total[spot, core] = (chip_sum[slot].astype(f32) + line_in[slot].astype(f32)).astype(b16)
         third(spot).start()
 
@@ -533,14 +561,18 @@
         slot = (step - 1) % 2
         first(slot).wait()
         chip_sum[slot] = (partial[slot, core].astype(f32) + pair_in[slot].astype(f32)).astype(b16)
-        second(slot).start()
+        second(slot, 1).start()
+
+        @pl.when(gives_output(step - 1))
+        def _():
+            second(slot, 0).start()
 
     @pl.when(step < images)
     def _():
         slot = step % 2
-        for copy in fetches(step, slot):
+        for copy in fetches(image_at(step), slot):
             copy.wait()
-        offset = step * SEQ - window_start(step)
+        offset = image_at(step) * SEQ - window_start(image_at(step))
         pick = one_hot(
             (rows, windows.shape[2]), lambda r, j: jnp.logical_and(j == r + offset, r < SEQ)
         )
@@ -673,7 +705,8 @@
             pltpu.VMEM((3, 2, 2, rows, half), bf),
             pltpu.SemaphoreType.DMA((2, 2)),
         ]
-        + [pltpu.SemaphoreType.DMA((2,))] * 4
+        + [pltpu.SemaphoreType.DMA((2,))] * 2
+        + [pltpu.SemaphoreType.DMA((2, 2))] * 2
         + [pltpu.SemaphoreType.DMA((3,))] * 2,
         compiler_params=pltpu.CompilerParams(
             collective_id=4,

time: 286 us -> 281 us (0.983)
  Pallas kernels: 265 us -> 260 us
    pallas_call x1, Pallas kernels: 153 us -> 146 us  [image_block(): pl.pallas_call(functools.partial(image_kernel, images, (width, head_cols)...]
where the time goes in v6:
time: 281 us
  Pallas kernels  260 us (93%)
  local copies, waits for them, and re-layouts  15.8 us (6%)
  other arithmetic  4.23 us (2%)
    pallas_call x1, Pallas kernels, image_block(): pl.pallas_call(functools.partial(image_kernel, images, (width, head_cols)...  146 us
    pallas_call x1, Pallas kernels, gather_blocks(): pl.pallas_call(functools.partial(gather_kernel, line), out_shape=jax.Shap...  49.2 us
    pallas_call x1, Pallas kernels, reduce_blocks(): pl.pallas_call(functools.partial(reduce_kernel, line), out_shape=jax.Shap...  45.3 us
    pallas_call x1, Pallas kernels, total_of(): pl.pallas_call(functools.partial(total_kernel, devices, ranks), out_shape...  11.8 us
    unnamed x7, local copies, waits for them, and re-layouts  9.71 us

profile of v6, /device:TPU:0, one launch (start us, length us, event | category | flops | bytes accessed | tf_op | source)
XLA Modules:
  0.0 280.5 jit_solution(18253405836520331143)
XLA Ops:
  0.7 0.7 slice.10
  1.4 0.7 slice.9
  2.1 0.6 pad_maximum_fusion.tail_ref
  2.7 1.0 convert_bitcast_fusion
  3.7 0.2 copy.43
  3.9 0.2 copy.45
  4.0 1.0 bitcast_convert_fusion
  5.0 1.0 convert.21
  6.0 1.0 copy.44
  7.0 0.7 convert.25
  7.6 0.1 broadcast_in_dim.10
  7.7 0.9 concatenate.4.own_ref
  8.6 49.2 %gather_blocks.1 = bf16[8,96,2432]{2,1,0:T(8,128)(2,1)} custom-call(bf16[96,2432]{1,0:T(8,128)(2,1)} %concatenate.4.own_ref), custom_call_target="tpu_custom_call" | custom-call | bytes 100000000 | tf_op jit(solution)/shard_map/gather_blocks/pallas_call | solution.py:134
  57.8 146.5 %image_block.1 = (bf16[3332,768]{1,0:T(8,128)(2,1)}, bf16[3332,768]{1,0:T(8,128)(2,1)}, bf16[768,2432]{1,0:T(8,128)(2,1)}) custom-call(bf16[3332,768]{1,0:T(8,128)(2,1)} %x_hbm.1, bf16[3332,768]{1,0:T(8,128)(2,1)} %c_hbm.1, bf16[2,16,768]{2,1,0:T(8,128)(2,1)} %pad_maximum_fusion.tail_ref, bf16[768,2432]{1,0:T(8,128)(2,1)} %bitcast.28), custom_call_target="tpu_custom_call" | custom-call | tf_op jit(solution)/shard_map/image_block/pallas_call | solution.py:676
  204.3 0.0 copy-start
  204.3 2.0 copy-done
  206.3 45.3 %reduce_blocks.1.summed_ref = f32[96,2432]{1,0:T(8,128)S(1)} custom-call(bf16[8,96,2432]{2,1,0:T(8,128)(2,1)S(1)} %bitcast.27), custom_call_target="tpu_custom_call" | custom-call | bytes 100000000 | tf_op jit(solution)/shard_map/reduce_blocks/pallas_call | solution.py:271
  251.7 0.0 copy-start.1
  251.7 0.9 copy-done.1
  252.6 4.2 %lamb_parts.1 = (f32[3,96,192]{2,1,0:T(8,128)}, f32[3,96,192]{2,1,0:T(8,128)}, f32[3,96,192]{2,1,0:T(8,128)}, f32[192,96]{1,0:T(8,128)}, f32[192,96]{1,0:T(8,128...) custom-call(f32[96,2432]{1,0:T(8,128)} %copy-done.1, ...), custom_call_target="tpu_custom_call" | custom-call | tf_op jit(solution)/shard_map/lamb_parts/pallas_call | solution.py:782
  256.8 11.8 %total_3.1.sums_ref = f32[8,128]{1,0:T(8,128)} custom-call(f32[8,128]{1,0:T(8,128)} %get-tuple-element.57.own_ref), custom_call_target="tpu_custom_call" | custom-call | bytes 20000000 | tf_op jit(solution)/shard_map/total_3/pallas_call | solution.py:365
  268.6 2.8 lamb_fresh.1
  271.4 0.7 slice_sqrt_fusion
  272.1 0.7 copy.46
  272.7 2.7 constant_dynamic-slice_fusion
  275.4 5.1 %copy.48 = bf16[3332,768]{1,0:T(8,128)(2,1)} copy(bf16[3332,768]{1,0:T(8,128)(2,1)} %get-tuple-element.153) | data formatting | bytes 10235904
  (2 shorter events, 0.0 us)
Async XLA Ops:
  204.3 2.1 copy-start
  251.7 0.9 copy-start.1

commit v7 on v6

--- a/solution.py
+++ b/solution.py
@@ -48,7 +48,23 @@
     pl.semaphore_wait(barrier, 1 + jnp.minimum(place, 1) + jnp.minimum(line - 1 - place, 1))
 
 
-def gather_kernel(line, own_ref, all_ref, own_sem, up_sem, down_sem, pair_sem, recv_sem):
+def gather_kernel(
+    line, cuts, wide_ref, inward_ref, narrow_ref, outward_ref, scaling_ref, all_ref,
+    own_ref, own_sem, up_sem, down_sem, pair_sem, recv_sem,
+):
+    hidden_here, head_cols, back_width, used = cuts
+    depth, width = own_ref.shape
+    b16 = jnp.bfloat16
+    own_ref[:, :hidden_here] = wide_ref[...].astype(b16)
+    for kind in range(3):
+        at = hidden_here + kind * head_cols
+        own_ref[:, at : at + head_cols] = inward_ref[kind].astype(b16)
+    at = hidden_here + 3 * head_cols
+    own_ref[:, at:back_width] = jnp.zeros((depth, back_width - at), b16)
+    own_ref[:, back_width : back_width + hidden_here] = narrow_ref[...].astype(b16)
+    own_ref[:, back_width + hidden_here : used] = outward_ref[...].T.astype(b16)
+    gain = jnp.broadcast_to(scaling_ref[...], (128, depth)).T
+    own_ref[:, used:] = gain[:, : width - used].astype(b16)
     me = lax.axis_index("dp")
     place, side = me // PAIR, me % PAIR
     up, down, other = {"dp": me + PAIR}, {"dp": me - PAIR}, {"dp": me + 1 - 2 * side}
@@ -127,26 +143,29 @@
             move(spot, held(block), block, down_sem, down).wait_send()
 
 
-def gather_blocks(own):
-    rows, width = own.shape
+def gather_blocks(masters, cuts, width):
+    depth = masters[0].shape[0]
     devices = lax.axis_size("dp")
     line = devices // PAIR
     return pl.pallas_call(
-        functools.partial(gather_kernel, line),
-        out_shape=jax.ShapeDtypeStruct((devices, rows, width), own.dtype),
-        in_specs=[pl.BlockSpec(memory_space=pltpu.VMEM)],
+        functools.partial(gather_kernel, line, cuts),
+        out_shape=jax.ShapeDtypeStruct((devices, depth, width), jnp.bfloat16),
+        in_specs=[pl.BlockSpec(memory_space=pltpu.VMEM)] * 5,
         out_specs=pl.BlockSpec(memory_space=pl.ANY),
         scratch_shapes=[
+            pltpu.VMEM((depth, width), jnp.bfloat16),
             pltpu.SemaphoreType.DMA,
             pltpu.SemaphoreType.DMA((line,)),
             pltpu.SemaphoreType.DMA((line,)),
             pltpu.SemaphoreType.DMA((line,)),
             pltpu.SemaphoreType.DMA((devices,)),
         ],
-        compiler_params=pltpu.CompilerParams(collective_id=0, has_side_effects=True),
+        compiler_params=pltpu.CompilerParams(
+            collective_id=0, has_side_effects=True, vmem_limit_bytes=60 * 2**20
+        ),
         cost_estimate=pl.CostEstimate(flops=0, bytes_accessed=100_000_000, transcendentals=0),
         name="gather_blocks",
-    )(own)
+    )(*masters)
 
 
 def reduce_kernel(
@@ -391,6 +410,7 @@
     images, cuts, x_hbm, c_hbm, tail_ref, w_ref,
     out_ref, grad_in_ref, g_ref,
     acc1, acc2, gain_row, g_gain, windows, kept, qkv, back_cols, front_cols,
+    normed_pair, cot_pair,
     partial, pair_in, chip_sum, line_in, total,
     in_sem, s1, r1, s2, r2, s3, r3,
 ):
@@ -583,6 +603,9 @@
         _floats, unit, _inv = normalised(kept[step % 4, 0])
         normed = (unit * gain).astype(b16)
         cot = kept[step % 4, 1]
+        here = pl.ds(pl.multiple_of(slot * rows, 16), rows)
+        normed_pair[here, :] = normed
+        cot_pair[here, :] = cot
 
         def mm(a, b):
             return jnp.dot(a, b, preferred_element_type=f32)
@@ -612,7 +635,7 @@
             probs = powers * (1.0 / jnp.sum(powers, axis=1, keepdims=True))
             probs_low = probs.astype(b16)
             spot = head * HEAD_DIM
-            front_cols[:, width + spot : width + spot + HEAD_DIM] = mm(probs_low, value).astype(b16)
+            front_cols[here, width + spot : width + spot + HEAD_DIM] = mm(probs_low, value).astype(b16)
             d_probs = mm_nt(d_att, value)
             d_value = mm_tn(probs_low, d_att)[:rows].astype(b16)
             inner = jnp.sum(probs * d_probs, axis=1, keepdims=True)
@@ -621,7 +644,7 @@
             d_key = mm_tn(d_scores, query)[:rows].astype(b16)
             for kind, value_of in ((0, d_query), (1, d_key), (2, d_value)):
                 at = width + kind * head_cols + spot
-                back_cols[:, at : at + HEAD_DIM] = value_of
+                back_cols[here, at : at + HEAD_DIM] = value_of
 
         upper = mm(normed, w_ref[:, :width])
         d_hidden = mm(cot, w_ref[:, back_width : back_width + width])
@@ -629,22 +652,32 @@
         square = upper * upper
         bend = jnp.tanh(scale * upper * (1.0 + 0.044715 * square))
         step_up = 0.5 * (1.0 + bend)
-        front_cols[:, :width] = (upper * step_up).astype(b16)
+        front_cols[here, :width] = (upper * step_up).astype(b16)
         slope = step_up + (0.5 * scale) * upper * (1.0 - bend * bend) * (
             1.0 + (3.0 * 0.044715) * square
         )
-        back_cols[:, :width] = (d_hidden * slope).astype(b16)
+        back_cols[here, :width] = (d_hidden * slope).astype(b16)
 
         finish(place)
-        out_part = mm_nt(front_cols[...], w_ref[:, back_width:]).astype(b16)
+        out_part = mm_nt(front_cols[here, :], w_ref[:, back_width:]).astype(b16)
         partial[slot, 0, 0] = out_part[:, :half]
         partial[slot, 1, 0] = out_part[:, half:]
-        back_part = mm_nt(back_cols[...], w_ref[:, :back_width]).astype(b16)
+        back_part = mm_nt(back_cols[here, :], w_ref[:, :back_width]).astype(b16)
         partial[slot, 0, 1] = back_part[:, :half]
         partial[slot, 1, 1] = back_part[:, half:]
         first(slot).start()
-        acc1[...] += mm_tn(normed, back_cols[...])
-        acc2[...] += mm_tn(cot, front_cols[...])
+
+        @pl.when(slot == 1)
+        def _():
+            acc1[...] += mm_tn(normed_pair[...], back_cols[...])
+            acc2[...] += mm_tn(cot_pair[...], front_cols[...])
+
+        if images % 2:
+
+            @pl.when(step == images - 1)
+            def _():
+                acc1[...] += mm_tn(normed_pair[:rows], back_cols[:rows])
+                acc2[...] += mm_tn(cot_pair[:rows], front_cols[:rows])
 
     @pl.when(step >= images)
     def _():
@@ -696,8 +729,10 @@
             pltpu.VMEM((2, 2, WINDOW + tails.shape[1], model), bf),
             pltpu.VMEM((4, 2, rows, model), bf),
             pltpu.VMEM((rows, 4 * head_cols), bf),
-            pltpu.VMEM((rows, back_width), bf),
-            pltpu.VMEM((rows, front_width), bf),
+            pltpu.VMEM((2 * rows, back_width), bf),
+            pltpu.VMEM((2 * rows, front_width), bf),
+            pltpu.VMEM((2 * rows, model), bf),
+            pltpu.VMEM((2 * rows, model), bf),
             pltpu.VMEM((2, 2, 2, rows, half), bf),
             pltpu.VMEM((2, 2, rows, half), bf),
             pltpu.VMEM((2, 2, rows, half), bf),
@@ -829,18 +864,18 @@
     back_width += gap
     used = back_width + hidden_here + head_cols
     width = -(-(used + 1) // 128) * 128
-    shard = jnp.concatenate(
-        [
+    cuts = (hidden_here, head_cols, back_width, used)
+    copies = gather_blocks(
+        (
             master_widening,
-            jnp.transpose(master_inward, (1, 0, 2)).reshape(depth, 3 * head_cols),
-            jnp.zeros((depth, gap), jnp.float32),
+            master_inward,
             master_narrowing.T,
-            master_outward.T,
-            jnp.broadcast_to(master_scaling[:, None], (depth, width - used)),
-        ],
-        axis=1,
-    ).astype(jnp.bfloat16)
-    copies = gather_blocks(shard).reshape(model, width)
+            master_outward,
+            master_scaling.reshape(1, depth),
+        ),
+        cuts,
+        width,
+    ).reshape(model, width)
     rows_here = inputs.shape[0]
     whole_rows = rows_here // 16 * 16
     tails = jnp.stack(
@@ -863,9 +898,7 @@
         (master_narrowing.T, first_narrowing.T, second_narrowing.T),
         tuple(v.reshape(1, depth) for v in (master_scaling, first_scaling, second_scaling)),
     )
-    parts, fresh, trust_norms = lamb_step(
-        summed, states, (hidden_here, head_cols, back_width, used)
-    )
+    parts, fresh, trust_norms = lamb_step(summed, states, cuts)
     results = []
     for index in range(5):
         group = (parts[3 * index], parts[3 * index + 1], fresh[index], fresh[5 + index])

time: 281 us -> 280 us (level)
  Pallas kernels: 260 us -> 264 us
  other arithmetic: 4.23 us -> 0.63 us
    pallas_call x1, Pallas kernels: 146 us -> 152 us  [image_block(): pl.pallas_call(functools.partial(image_kernel, images, (width, head_cols)...]
    unnamed x7 -> x6, local copies, waits for them, and re-layouts: 9.71 us -> 8.73 us
where the time goes in v7:
time: 280 us; the launch traced here: 279 us
  Pallas kernels  264 us (94%)
  local copies, waits for them, and re-layouts  13.5 us (5%)
    pallas_call x1, Pallas kernels, image_block(): pl.pallas_call(functools.partial(image_kernel, images, (width, head_cols)...  152 us
    pallas_call x1, Pallas kernels, gather_blocks(): pl.pallas_call(functools.partial(gather_kernel, line, cuts), out_shape=ja...  49.5 us
    pallas_call x1, Pallas kernels, reduce_blocks(): pl.pallas_call(functools.partial(reduce_kernel, line), out_shape=jax.Shap...  45.3 us
    pallas_call x1, Pallas kernels, total_of(): pl.pallas_call(functools.partial(total_kernel, devices, ranks), out_shape...  11 us
    unnamed x6, local copies, waits for them, and re-layouts  8.73 us

profile of v7, /device:TPU:0, one launch (start us, length us, event | category | flops | bytes accessed | tf_op | source)
XLA Modules:
  0.0 279.2 jit_solution(12125440076417802249)
XLA Ops:
  0.7 49.5 %gather_blocks.1 = bf16[8,96,2432]{2,1,0:T(8,128)(2,1)} custom-call(f32[96,768]{1,0:T(8,128)} %refs_2_.3, f32[3,96,192]{2,1,0:T(8,128)} %refs_0_.3, f32[96,768]{1,0:T(8,128)} %bitcast.22, f32[192,96]{1,0:T(8,128)} %refs_1_.3, f32[1,96]{1,0:T(1,128)} %bitcast.27), custom_call_target="tpu_custom_call" | custom-call | bytes 100000000 | tf_op jit(solution)/shard_map/gather_blocks/pallas_call | solution.py:150
  50.2 0.7 slice.10
  50.9 0.7 slice.9
  51.6 0.6 pad_maximum_fusion.tail_ref
  52.3 151.5 %image_block.1 = (bf16[3332,768]{1,0:T(8,128)(2,1)}, bf16[3332,768]{1,0:T(8,128)(2,1)}, bf16[768,2432]{1,0:T(8,128)(2,1)}) custom-call(bf16[3332,768]{1,0:T(8,128)(2,1)} %x_hbm.1, bf16[3332,768]{1,0:T(8,128)(2,1)} %c_hbm.1, bf16[2,16,768]{2,1,0:T(8,128)(2,1)} %pad_maximum_fusion.tail_ref, bf16[768,2432]{1,0:T(8,128)(2,1)} %bitcast.21), custom_call_target="tpu_custom_call" | custom-call | tf_op jit(solution)/shard_map/image_block/pallas_call | solution.py:709
  203.8 0.0 copy-start
  203.8 2.0 copy-done
  205.9 45.3 %reduce_blocks.1.summed_ref = f32[96,2432]{1,0:T(8,128)S(1)} custom-call(bf16[8,96,2432]{2,1,0:T(8,128)(2,1)S(1)} %bitcast.20), custom_call_target="tpu_custom_call" | custom-call | bytes 100000000 | tf_op jit(solution)/shard_map/reduce_blocks/pallas_call | solution.py:290
  251.2 0.0 copy-start.1
  251.2 0.9 copy-done.1
  252.1 4.2 %lamb_parts.1 = (f32[3,96,192]{2,1,0:T(8,128)}, f32[3,96,192]{2,1,0:T(8,128)}, f32[3,96,192]{2,1,0:T(8,128)}, f32[192,96]{1,0:T(8,128)}, f32[192,96]{1,0:T(8,128...) custom-call(f32[96,2432]{1,0:T(8,128)} %copy-done.1, ...), custom_call_target="tpu_custom_call" | custom-call | tf_op jit(solution)/shard_map/lamb_parts/pallas_call | solution.py:817
  256.4 11.0 %total_3.1.sums_ref = f32[8,128]{1,0:T(8,128)} custom-call(f32[8,128]{1,0:T(8,128)} %get-tuple-element.57.own_ref), custom_call_target="tpu_custom_call" | custom-call | bytes 20000000 | tf_op jit(solution)/shard_map/total_3/pallas_call | solution.py:384
  267.4 2.8 lamb_fresh.1
  270.1 0.7 slice_sqrt_fusion
  270.8 0.7 copy.40
  271.5 2.7 constant_dynamic-slice_fusion
  274.1 5.1 %copy.42 = bf16[3332,768]{1,0:T(8,128)(2,1)} copy(bf16[3332,768]{1,0:T(8,128)(2,1)} %get-tuple-element.130) | data formatting | bytes 10235904
  (1 shorter events, 0.0 us)
Async XLA Ops:
  203.8 2.1 copy-start
  251.2 0.9 copy-start.1

commit v8 on v6

--- a/solution.py
+++ b/solution.py
@@ -48,7 +48,23 @@
     pl.semaphore_wait(barrier, 1 + jnp.minimum(place, 1) + jnp.minimum(line - 1 - place, 1))
 
 
-def gather_kernel(line, own_ref, all_ref, own_sem, up_sem, down_sem, pair_sem, recv_sem):
+def gather_kernel(
+    line, cuts, wide_ref, inward_ref, narrow_ref, outward_ref, scaling_ref, all_ref,
+    own_ref, own_sem, up_sem, down_sem, pair_sem, recv_sem,
+):
+    hidden_here, head_cols, back_width, used = cuts
+    depth, width = own_ref.shape
+    b16 = jnp.bfloat16
+    own_ref[:, :hidden_here] = wide_ref[...].astype(b16)
+    for kind in range(3):
+        at = hidden_here + kind * head_cols
+        own_ref[:, at : at + head_cols] = inward_ref[kind].astype(b16)
+    at = hidden_here + 3 * head_cols
+    own_ref[:, at:back_width] = jnp.zeros((depth, back_width - at), b16)
+    own_ref[:, back_width : back_width + hidden_here] = narrow_ref[...].astype(b16)
+    own_ref[:, back_width + hidden_here : used] = outward_ref[...].T.astype(b16)
+    gain = jnp.broadcast_to(scaling_ref[...], (128, depth)).T
+    own_ref[:, used:] = gain[:, : width - used].astype(b16)
     me = lax.axis_index("dp")
     place, side = me // PAIR, me % PAIR
     up, down, other = {"dp": me + PAIR}, {"dp": me - PAIR}, {"dp": me + 1 - 2 * side}
@@ -127,26 +143,29 @@
             move(spot, held(block), block, down_sem, down).wait_send()
 
 
-def gather_blocks(own):
-    rows, width = own.shape
+def gather_blocks(masters, cuts, width):
+    depth = masters[0].shape[0]
     devices = lax.axis_size("dp")
     line = devices // PAIR
     return pl.pallas_call(
-        functools.partial(gather_kernel, line),
-        out_shape=jax.ShapeDtypeStruct((devices, rows, width), own.dtype),
-        in_specs=[pl.BlockSpec(memory_space=pltpu.VMEM)],
+        functools.partial(gather_kernel, line, cuts),
+        out_shape=jax.ShapeDtypeStruct((devices, depth, width), jnp.bfloat16),
+        in_specs=[pl.BlockSpec(memory_space=pltpu.VMEM)] * 5,
         out_specs=pl.BlockSpec(memory_space=pl.ANY),
         scratch_shapes=[
+            pltpu.VMEM((depth, width), jnp.bfloat16),
             pltpu.SemaphoreType.DMA,
             pltpu.SemaphoreType.DMA((line,)),
             pltpu.SemaphoreType.DMA((line,)),
             pltpu.SemaphoreType.DMA((line,)),
             pltpu.SemaphoreType.DMA((devices,)),
         ],
-        compiler_params=pltpu.CompilerParams(collective_id=0, has_side_effects=True),
+        compiler_params=pltpu.CompilerParams(
+            collective_id=0, has_side_effects=True, vmem_limit_bytes=60 * 2**20
+        ),
         cost_estimate=pl.CostEstimate(flops=0, bytes_accessed=100_000_000, transcendentals=0),
         name="gather_blocks",
-    )(own)
+    )(*masters)
 
 
 def reduce_kernel(
@@ -540,33 +559,6 @@
         )
         put(grad_in_ref, (kept[spot, 1].astype(f32) + d_floats).astype(b16))
 
-    @pl.when(jnp.logical_and(step >= 2, step < images + 2))
-    def _():
-        slot, spot = (step - 2) % 2, (step - 2) % 3
-        second(slot, 1).wait()
-
-        @pl.when(gives_output(step - 2))
-        def _():
-            second(slot, 0).wait_send()
-
-        @pl.when(takes_output(step - 2))
-        def _():
-            second(slot, 0).wait_recv()
-
-        total[spot, core] = (chip_sum[slot].astype(f32) + line_in[slot].astype(f32)).astype(b16)
-        third(spot).start()
-
-    @pl.when(jnp.logical_and(step >= 1, step < images + 1))
-    def _():
-        slot = (step - 1) % 2
-        first(slot).wait()
-        chip_sum[slot] = (partial[slot, core].astype(f32) + pair_in[slot].astype(f32)).astype(b16)
-        second(slot, 1).start()
-
-        @pl.when(gives_output(step - 1))
-        def _():
-            second(slot, 0).start()
-
     @pl.when(step < images)
     def _():
         slot = step % 2
@@ -642,13 +634,43 @@
         back_part = mm_nt(back_cols[...], w_ref[:, :back_width]).astype(b16)
         partial[slot, 0, 1] = back_part[:, :half]
         partial[slot, 1, 1] = back_part[:, half:]
-        first(slot).start()
         acc1[...] += mm_tn(normed, back_cols[...])
         acc2[...] += mm_tn(cot, front_cols[...])
 
     @pl.when(step >= images)
     def _():
         finish(place_late)
+
+    @pl.when(jnp.logical_and(step >= 2, step < images + 2))
+    def _():
+        slot, spot = (step - 2) % 2, (step - 2) % 3
+        second(slot, 1).wait()
+
+        @pl.when(gives_output(step - 2))
+        def _():
+            second(slot, 0).wait_send()
+
+        @pl.when(takes_output(step - 2))
+        def _():
+            second(slot, 0).wait_recv()
+
+        total[spot, core] = (chip_sum[slot].astype(f32) + line_in[slot].astype(f32)).astype(b16)
+        third(spot).start()
+
+    @pl.when(jnp.logical_and(step >= 1, step < images + 1))
+    def _():
+        slot = (step - 1) % 2
+        first(slot).wait()
+        chip_sum[slot] = (partial[slot, core].astype(f32) + pair_in[slot].astype(f32)).astype(b16)
+        second(slot, 1).start()
+
+        @pl.when(gives_output(step - 1))
+        def _():
+            second(slot, 0).start()
+
+    @pl.when(step < images)
+    def _():
+        first(step % 2).start()
 
     @pl.when(step == images + 2)
     def _():
@@ -829,18 +851,18 @@
     back_width += gap
     used = back_width + hidden_here + head_cols
     width = -(-(used + 1) // 128) * 128
-    shard = jnp.concatenate(
-        [
+    cuts = (hidden_here, head_cols, back_width, used)
+    copies = gather_blocks(
+        (
             master_widening,
-            jnp.transpose(master_inward, (1, 0, 2)).reshape(depth, 3 * head_cols),
-            jnp.zeros((depth, gap), jnp.float32),
+            master_inward,
             master_narrowing.T,
-            master_outward.T,
-            jnp.broadcast_to(master_scaling[:, None], (depth, width - used)),
-        ],
-        axis=1,
-    ).astype(jnp.bfloat16)
-    copies = gather_blocks(shard).reshape(model, width)
+            master_outward,
+            master_scaling.reshape(1, depth),
+        ),
+        cuts,
+        width,
+    ).reshape(model, width)
     rows_here = inputs.shape[0]
     whole_rows = rows_here // 16 * 16
     tails = jnp.stack(
@@ -863,9 +885,7 @@
         (master_narrowing.T, first_narrowing.T, second_narrowing.T),
         tuple(v.reshape(1, depth) for v in (master_scaling, first_scaling, second_scaling)),
     )
-    parts, fresh, trust_norms = lamb_step(
-        summed, states, (hidden_here, head_cols, back_width, used)
-    )
+    parts, fresh, trust_norms = lamb_step(summed, states, cuts)
     results = []
     for index in range(5):
         group = (parts[3 * index], parts[3 * index + 1], fresh[index], fresh[5 + index])

time: 281 us -> 287 us (1.021)
  Pallas kernels: 260 us -> 272 us
  other arithmetic: 4.23 us -> 0.63 us
    pallas_call x1, Pallas kernels: 146 us -> 160 us  [image_block(): pl.pallas_call(functools.partial(image_kernel, images, (width, head_cols)...]
    unnamed x7 -> x6, local copies, waits for them, and re-layouts: 9.71 us -> 8.73 us
where the time goes in v8:
time: 287 us
  Pallas kernels  272 us (95%)
  local copies, waits for them, and re-layouts  13.5 us (5%)
    pallas_call x1, Pallas kernels, image_block(): pl.pallas_call(functools.partial(image_kernel, images, (width, head_cols)...  160 us
    pallas_call x1, Pallas kernels, gather_blocks(): pl.pallas_call(functools.partial(gather_kernel, line, cuts), out_shape=ja...  49.5 us
    pallas_call x1, Pallas kernels, reduce_blocks(): pl.pallas_call(functools.partial(reduce_kernel, line), out_shape=jax.Shap...  45.3 us
    pallas_call x1, Pallas kernels, total_of(): pl.pallas_call(functools.partial(total_kernel, devices, ranks), out_shape...  9.81 us
    unnamed x6, local copies, waits for them, and re-layouts  8.73 us

profile of v8, /device:TPU:0, one launch (start us, length us, event | category | flops | bytes accessed | tf_op | source)
XLA Modules:
  0.0 286.7 jit_solution(15806266054361411735)
XLA Ops:
  0.7 49.5 %gather_blocks.1 = bf16[8,96,2432]{2,1,0:T(8,128)(2,1)} custom-call(f32[96,768]{1,0:T(8,128)} %refs_2_.3, f32[3,96,192]{2,1,0:T(8,128)} %refs_0_.3, f32[96,768]{1,0:T(8,128)} %bitcast.22, f32[192,96]{1,0:T(8,128)} %refs_1_.3, f32[1,96]{1,0:T(1,128)} %bitcast.27), custom_call_target="tpu_custom_call" | custom-call | bytes 100000000 | tf_op jit(solution)/shard_map/gather_blocks/pallas_call | solution.py:150
  50.2 0.7 slice.10
  50.9 0.7 slice.9
  51.6 0.6 pad_maximum_fusion.tail_ref
  52.3 160.2 %image_block.1 = (bf16[3332,768]{1,0:T(8,128)(2,1)}, bf16[3332,768]{1,0:T(8,128)(2,1)}, bf16[768,2432]{1,0:T(8,128)(2,1)}) custom-call(bf16[3332,768]{1,0:T(8,128)(2,1)} %x_hbm.1, bf16[3332,768]{1,0:T(8,128)(2,1)} %c_hbm.1, bf16[2,16,768]{2,1,0:T(8,128)(2,1)} %pad_maximum_fusion.tail_ref, bf16[768,2432]{1,0:T(8,128)(2,1)} %bitcast.21), custom_call_target="tpu_custom_call" | custom-call | tf_op jit(solution)/shard_map/image_block/pallas_call | solution.py:698
  212.5 0.0 copy-start
  212.5 2.0 copy-done
  214.5 45.3 %reduce_blocks.1.summed_ref = f32[96,2432]{1,0:T(8,128)S(1)} custom-call(bf16[8,96,2432]{2,1,0:T(8,128)(2,1)S(1)} %bitcast.20), custom_call_target="tpu_custom_call" | custom-call | bytes 100000000 | tf_op jit(solution)/shard_map/reduce_blocks/pallas_call | solution.py:290
  259.9 0.0 copy-start.1
  259.9 0.9 copy-done.1
  260.8 4.2 %lamb_parts.1 = (f32[3,96,192]{2,1,0:T(8,128)}, f32[3,96,192]{2,1,0:T(8,128)}, f32[3,96,192]{2,1,0:T(8,128)}, f32[192,96]{1,0:T(8,128)}, f32[192,96]{1,0:T(8,128...) custom-call(f32[96,2432]{1,0:T(8,128)} %copy-done.1, ...), custom_call_target="tpu_custom_call" | custom-call | tf_op jit(solution)/shard_map/lamb_parts/pallas_call | solution.py:804
  265.0 9.8 %total_3.1.sums_ref = f32[8,128]{1,0:T(8,128)} custom-call(f32[8,128]{1,0:T(8,128)} %get-tuple-element.57.own_ref), custom_call_target="tpu_custom_call" | custom-call | bytes 20000000 | tf_op jit(solution)/shard_map/total_3/pallas_call | solution.py:384
  274.8 2.8 lamb_fresh.1
  277.6 0.7 slice_sqrt_fusion
  278.3 0.7 copy.40
  278.9 2.7 constant_dynamic-slice_fusion
  281.6 5.1 %copy.42 = bf16[3332,768]{1,0:T(8,128)(2,1)} copy(bf16[3332,768]{1,0:T(8,128)(2,1)} %get-tuple-element.130) | data formatting | bytes 10235904
  (1 shorter events, 0.0 us)
Async XLA Ops:
  212.5 2.1 copy-start
  259.9 0.9 copy-start.1
